TPU v7x, 1024 devices: a whole 4x8x16 slice. The times are simulated.
1024 devices in a mesh: dp: 8 (over y), seq: 8 (over x, core), tp: 16 (over z).
Axes of the slice: x: 4, y: 8, z: 16, core: 2. Of those that a mesh axis runs over, the one named last changes fastest.
Arguments:
- tokens: bfloat16 [16384, 4096], P(('dp', 'seq', 'tp')), parts along dimension 0, may hold values from -6 to 6
- pre_gain: float32 [4096], replicated, may hold values from 0.25 to 1.75
- proj_inner: bfloat16 [4096, 4096], P(None, 'tp'), may hold values from -0.09375 to 0.09375
- proj_gate: bfloat16 [4096, 4096], P(None, 'tp'), may hold values from -0.09375 to 0.09375
- proj_states: bfloat16 [4096, 1024], P(None, 'tp'), may hold values from -0.09375 to 0.09375
- proj_step: bfloat16 [4096, 64], P(None, 'tp'), may hold values from -0.09375 to 0.09375
- step_bias: float32 [64], P('tp'), may hold values from -5 to -3
- log_rate: float32 [64], P('tp'), as said below
- conv_inner: float32 [4, 4096], P(None, 'tp'), may hold values from -3 to 3
- conv_states: float32 [4, 1024], P(None, 'tp'), may hold values from -3 to 3
- skip_gain: float32 [64], P('tp'), may hold values from 1 to 4
- norm_gain: float32 [4096], P('tp'), may hold values from 0.25 to 1.75
- proj_output: bfloat16 [4096, 4096], P('tp'), may hold values from -0.09375 to 0.09375
Outputs:
- layer_out: bfloat16 [16384, 4096], P(('dp', 'seq', 'tp')), parts along dimension 0
There are 8 independent parts, one for each index of `dp`. A program takes and returns all parts, laid end to end along the dimension named above; an argument that names none is the same for every part. Nothing has to cross between parts.
Inputs may be any that keep to these rules, and one draw needn't show every extreme that they name: exp(log_rate) lies between 0.1 / (0.035 * 2048) and 1 / (25 * 0.035).
All inputs are finite; a program needn't handle non-finite values.
Results may differ from a plain program's by a relative error of at most 0.017.
Values may be sent and summed in bfloat16 or wider, within the bound.
No kernel may reach another device: no remote copies, remote signals or barrier semaphores. Data moves between devices by JAX's collectives and lax.ppermute only.
A program may use at most 64 MiB of HBM per device.

v0:
```python
from functools import partial
import math

import jax
import jax.numpy as jnp
from jax import lax
from jax.sharding import PartitionSpec as P

HEAD_DIM = 64
STATE = 128
GROUP_HEADS = 16
BLOCK = 128
GROUPS = 4


epsilon = 1e-05
highest = lax.Precision.HIGHEST


def from_behind(value, axis, steps):
    count = lax.axis_size(axis)
    initial, last = (max(0, -steps), min(count, count - steps))
    return lax.ppermute(value, axis, [(source, source + steps) for source in range(initial, last)])


def in_order(tiles, dim):
    tiles = jnp.moveaxis(tiles, 0, dim)
    dims = tiles.shape
    return tiles.reshape(*dims[:dim], dims[dim] * dims[dim + 1], *dims[dim + 2 :])


def from_everyone(x, axis):
    copies = jnp.broadcast_to(x, (lax.axis_size(axis), *x.shape))
    return lax.all_to_all(copies, axis, split_axis=0, concat_axis=0, tiled=True)


def collect(x, axis, dim):
    return in_order(from_everyone(x, axis), dim)


def sent_together(arrays, axis, dim, along):
    widths = [math.prod(a.shape[along:]) for a in arrays]
    both = jnp.concatenate(
        [a.reshape(*a.shape[:along], w) for a, w in zip(arrays, widths)], axis=along
    )
    out = lax.all_gather(both, axis, axis=dim, tiled=True)
    tiles = jnp.split(out, [sum(widths[:k]) for k in range(1, len(widths))], axis=along)
    return tuple((b.reshape(*out.shape[:along], *a.shape[along:]) for a, b in zip(arrays, tiles)))


def causal_conv(values, kernel_taps, before):
    length = values.shape[0]
    padded = jnp.concatenate((before, values), axis=0)
    running_sum = jnp.zeros(values.shape, jnp.float32)
    for offset in range(kernel_taps.shape[0]):
        running_sum = running_sum + kernel_taps[offset] * padded[offset : offset + length]
    return running_sum


def block_step(carry_state, inputs, copies):
    values, step_size, log_decay, in_states, out_states = inputs
    block_len = values.shape[0]
    running = jnp.cumsum(log_decay, axis=0)
    scores = jnp.einsum("tgn,sgn->gts", out_states, in_states, precision=highest)
    scores = jnp.tile(scores, (copies, 1, 1))
    places = jnp.arange(block_len)
    lower_mask = (places[:, None] >= places[None, :])[None]
    spread = running.T[:, :, None] - running.T[:, None, :]
    decay_table = jnp.where(lower_mask, jnp.exp(jnp.where(lower_mask, spread, 0.0)), 0.0)
    weights = scores * decay_table * step_size.T[:, None, :]
    within = jnp.einsum("hts,shp->thp", weights, values, precision=highest)
    out_heads = jnp.tile(out_states, (1, copies, 1))
    in_heads = jnp.tile(in_states, (1, copies, 1))
    carried = (
        jnp.einsum("thn,hpn->thp", out_heads, carry_state, precision=highest)
        * jnp.exp(running)[:, :, None]
    )
    tail_decay = jnp.exp(running[-1][None, :] - running) * step_size
    scaled = values * tail_decay[:, :, None]
    new_state = jnp.exp(running[-1])[:, None, None] * carry_state + jnp.einsum(
        "shp,shn->hpn", scaled, in_heads, precision=highest
    )
    return (new_state, within + carried)


def scan_blocks(
    values, step_size, log_decay, in_states, out_states, carry_state, block_len, copies
):
    row_count, head_count, head_dim = values.shape
    block_count = row_count // block_len

    def split_blocks(source):
        return source.reshape((block_count, block_len) + source.shape[1:])

    final_state, outputs = lax.scan(
        partial(block_step, copies=copies),
        carry_state,
        (
            split_blocks(values),
            split_blocks(step_size),
            split_blocks(log_decay),
            split_blocks(in_states),
            split_blocks(out_states),
        ),
    )
    return (final_state, outputs.reshape(row_count, head_count, head_dim))


def body(
    tokens,
    pre_gain,
    proj_inner,
    proj_gate,
    proj_states,
    proj_step,
    step_bias,
    log_rate,
    conv_inner,
    conv_states,
    skip_gain,
    norm_gain,
    proj_output,
):
    tokens_wide = tokens.astype(jnp.float32)
    normed = (
        tokens_wide
        * lax.rsqrt(jnp.mean(tokens_wide * tokens_wide, axis=1, keepdims=True) + epsilon)
        * pre_gain
    ).astype(jnp.bfloat16)
    inner_width = proj_inner.shape[1]
    state_width = proj_states.shape[1]
    heads_local = proj_step.shape[1]
    copies = heads_local // GROUPS
    row_piece = lax.all_gather(normed, "tp", axis=0, tiled=True)
    projected = jnp.concatenate(
        (
            jnp.dot(row_piece, proj_inner, preferred_element_type=jnp.float32),
            jnp.dot(row_piece, proj_gate, preferred_element_type=jnp.float32),
            jnp.dot(row_piece, proj_states, preferred_element_type=jnp.float32),
            jnp.dot(row_piece, proj_step, preferred_element_type=jnp.float32),
        ),
        axis=1,
    )
    row_count = projected.shape[0]
    inner_proj = projected[:, :inner_width].astype(jnp.bfloat16)
    gate_proj = projected[:, inner_width : 2 * inner_width].astype(jnp.bfloat16)
    state_proj = projected[:, 2 * inner_width : 2 * inner_width + state_width].astype(jnp.bfloat16)
    step_size = jax.nn.softplus(projected[:, 2 * inner_width + state_width :] + step_bias)
    log_decay = -jnp.exp(log_rate) * step_size
    margin = conv_inner.shape[0] - 1
    before_inner, before_states = from_behind(
        (inner_proj[row_count - margin :], state_proj[row_count - margin :]), "seq", 1
    )
    mixed_inner = jax.nn.silu(
        causal_conv(inner_proj.astype(jnp.float32), conv_inner, before_inner.astype(jnp.float32))
    ).astype(jnp.bfloat16)
    mixed_local = jax.nn.silu(
        causal_conv(state_proj.astype(jnp.float32), conv_states, before_states.astype(jnp.float32))
    ).astype(jnp.bfloat16)
    mixed_all = collect(mixed_local, "tp", 1)
    values = mixed_inner.astype(jnp.float32).reshape(row_count, heads_local, HEAD_DIM)
    paired = mixed_all.astype(jnp.float32).reshape(row_count, GROUPS, 2, STATE)
    in_states = paired[:, :, 0]
    out_states = paired[:, :, 1]
    zero_state = jnp.zeros((heads_local, HEAD_DIM, STATE), jnp.float32)
    final_state, scanned = scan_blocks(
        values, step_size, log_decay, in_states, out_states, zero_state, BLOCK, copies
    )
    decay_sum = jnp.sum(log_decay, axis=0)
    decay_sums, summaries = tuple(
        (
            part.astype(jnp.float32)
            for part in sent_together(
                (decay_sum[None].astype(jnp.bfloat16), final_state[None].astype(jnp.bfloat16)),
                "seq",
                0,
                2,
            )
        )
    )
    position = lax.axis_index("seq")
    device_ids = jnp.arange(decay_sums.shape[0])
    earlier_mask = (device_ids < position)[:, None]
    before_me = jnp.sum(jnp.where(earlier_mask, decay_sums, 0.0), axis=0)
    reach_end = jnp.cumsum(decay_sums, axis=0)
    weights = jnp.where(
        earlier_mask, jnp.exp(jnp.where(earlier_mask, before_me[None] - reach_end, 0.0)), 0.0
    )
    incoming = jnp.einsum("jh,jhpn->hpn", weights, summaries, precision=highest)
    running = jnp.cumsum(log_decay, axis=0)
    out_heads = jnp.tile(out_states, (1, copies, 1))
    carried = (
        jnp.einsum("thn,hpn->thp", out_heads, incoming, precision=highest)
        * jnp.exp(running)[:, :, None]
    )
    ssd_out = scanned + carried + skip_gain[None, :, None] * values
    gated_out = ssd_out * jax.nn.silu(gate_proj.astype(jnp.float32)).reshape(
        row_count, heads_local, HEAD_DIM
    )
    head_squares = jnp.sum(gated_out * gated_out, axis=2)
    every_square = collect(head_squares, "tp", 1)
    group_totals = jnp.sum(
        every_square.reshape(row_count, every_square.shape[1] // GROUPS, GROUPS), axis=1
    )
    mean_square = (group_totals / (GROUP_HEADS * HEAD_DIM))[:, None, :, None]
    grouped = gated_out.reshape(row_count, copies, GROUPS, HEAD_DIM)
    normal_out = grouped * lax.rsqrt(mean_square + epsilon)
    mixed_out = (normal_out.reshape(row_count, inner_width) * norm_gain).astype(jnp.bfloat16)
    summed = lax.psum_scatter(
        jnp.dot(mixed_out, proj_output, preferred_element_type=jnp.float32).astype(jnp.bfloat16),
        "tp",
        scatter_dimension=0,
        tiled=True,
    ).astype(jnp.float32)
    return (tokens_wide + summed).astype(jnp.bfloat16)


def solution(mesh):
    placed = (
        P(("dp", "seq", "tp"), None),
        P(),
        P(None, "tp"),
        P(None, "tp"),
        P(None, "tp"),
        P(None, "tp"),
        P("tp"),
        P("tp"),
        P(None, "tp"),
        P(None, "tp"),
        P("tp"),
        P("tp"),
        P("tp", None),
    )
    return jax.shard_map(
        body, mesh=mesh, in_specs=placed, out_specs=P(("dp", "seq", "tp"), None), check_vma=False
    )
```

profile of v0, /device:TPU:56, one launch (start us, length us, event | category | flops | bytes accessed | tf_op | source)
XLA Modules:
  0.0 279.5 jit_solution(1686199102111141543)
XLA Ops:
  6.5 1.2 fusion.28
  7.7 1.7 fusion.30
  9.5 0.7 exponential_negate_fusion
  10.1 0.8 slice_bitcast_fusion.6
  11.0 82.9 %all-gather.2.cloned.1.call-done = bf16[256,4096]{1,0:T(8,128)(2,1)} async-done(((bf16[16,4096]{1,0:T(8,128)(2,1)}), bf16[256,4096]{1,0:T(8,128)(2,1)}) %all-gather.2.cloned.1.call-update) | async-done | bytes 2097168 | tf_op jit(solution)/shard_map/all_gather | solution.py:134
  93.9 2.4 fusion.52
  96.3 0.1 slice.94
  96.4 1.3 collective-permute-start.1
  97.7 0.8 collective-permute-done.1
  98.5 0.2 multiply_convert_fusion.1
  98.7 0.8 broadcast_in_dim.77
  99.5 7.7 %all-to-all-start = ((bf16[16,256,64]{1,2,0:T(8,128)(2,1)}), bf16[16,256,64]{1,2,0:T(8,128)(2,1)S(1)}, u32[]{:S(2)}, u32[]{:S(2)}) async-start(bf16[16,256,64]{1,2,0:T(8,128)(2,1)} %broadcast_in_dim.77), calls=%async_computation | async-start | bytes 1048576 | tf_op jit(solution)/shard_map/all_to_all | solution.py:34
  107.4 2.4 fusion.48
  109.8 1.2 reduce-window.6
  111.1 0.1 copy.88
  111.3 0.1 copy.89
  111.4 3.8 %fusion.53 = (f32[256,256]{1,0:T(8,128)}, bf16[256,256]{1,0:T(8,128)(2,1)S(1)}) fusion(bf16[256,4096]{1,0:T(8,128)(2,1)} %all-gather.2.cloned.1.call-done, bf16[4096,256]{1,0:T(8,128)(2,1)} %param.17), kind=kOutput, calls=%fused_computation.109 | convolution fusion | flops 537001984 | bytes 4587520 | tf_op jit(solution)/shard_map/dot_general | solution.py:137
  115.2 3.8 %collective-permute-start = (bf16[3,256]{1,0:T(4,128)(2,1)S(1)}, bf16[3,256]{1,0:T(4,128)(2,1)S(1)}, u32[]{:S(2)}, u32[]{:S(2)}) collective-permute-start(bf16[3,256]{1,0:T(4,128)(2,1)S(1)} %slice.89), channel_id=1, source_target_pairs={{0,16},{16,32},{32,48},{48,64},{64,80},{80,96},{96,112},{1,17},{17... | collective-permute-start | bytes 4616 | tf_op jit(solution)/shard_map/ppermute | solution.py:23
  119.1 0.7 divide_multiply_fusion
  119.8 0.1 exponential_bitcast_fusion
  119.9 0.1 copy.85
  120.0 0.1 copy.97
  120.1 0.1 copy.100
  120.3 0.8 copy.92
  121.1 1.6 fusion.34
  122.7 0.8 copy.90
  123.5 1.0 reshape.147
  124.6 1.2 copy.80
  125.8 6.5 %all-to-all-done = bf16[16,256,64]{1,2,0:T(8,128)(2,1)S(1)} async-done(((bf16[16,256,64]{1,2,0:T(8,128)(2,1)}), bf16[16,256,64]{1,2,0:T(8,128)(2,1)S(1)}, u32[]{:S(2)}, u32[]{:S(2)}) %all-to-all-start) | async-done | bytes 524320 | tf_op jit(solution)/shard_map/all_to_all | solution.py:34
  132.3 1.1 fusion.50
  133.4 2.1 reshape_squeeze.7
  135.5 2.1 reshape_squeeze.6
  137.6 17.5 %while.13 = (s32[]{:T(128)}, f32[4,64,128]{2,1,0:T(8,128)S(1)}, f32[2,128,4,64]{1,0,3,2:T(2,128)}, f32[2,128,4]{2,1,0:T(8,128)S(1)}, f32[2,128,4,64]{1,3,2,0:T(8...) while((s32[]{:T(128)}, f32[4,64,128]{2,1,0:T(8,128)S(1)}, ...), condition=%wide.region_3.4_spmd.clone, body=%wide.region_1.3_spmd.clone.sunk | while | flops 252297728 | bytes 4010732 | solution.py:95
  137.6 0.2 reduce_window_sum.40
  137.9 0.1 copy.125
  138.1 1.8 constant_dynamic-slice_fusion.3
  139.9 0.6 fusion.91
  140.5 0.6 convolution_bitcast_fusion.4
  141.1 0.4 fusion.92
  141.5 0.6 convolution_add_fusion.3
  142.1 4.2 %dynamic_update_slice.6 = f32[2,128,4,64]{1,0,3,2:T(2,128)} dynamic-update-slice(f32[2,128,4,64]{1,0,3,2:T(2,128)} %get-tuple-element.225, f32[1,128,4,64]{1,0,3,2:T(1,128)S(1)} %bitcast.175, s32[]{:T(128)S(6)} %copy.132, s32[]{:T(128)} %constant.47.clone.1..sunk, s32[]{:T(128)} %constant.47.clone.1..sunk, s32[]{:T(128)} %constant.47.clone.1..sunk) | dynamic-update-slice | bytes 262148 | tf_op jit(solution)/shard_map/while/body/jit(dynamic_update_index_in_dim)/dynamic_update_slice | solution.py:95
  146.4 0.2 reduce_window_sum.40
  146.6 0.1 copy.125
  146.9 1.8 constant_dynamic-slice_fusion.3
  148.7 0.6 fusion.91
  149.3 0.6 convolution_bitcast_fusion.4
  149.9 0.4 fusion.92
  150.3 0.6 convolution_add_fusion.3
  150.9 4.2 %dynamic_update_slice.6 = f32[2,128,4,64]{1,0,3,2:T(2,128)} dynamic-update-slice(f32[2,128,4,64]{1,0,3,2:T(2,128)} %get-tuple-element.225, f32[1,128,4,64]{1,0,3,2:T(1,128)S(1)} %bitcast.175, s32[]{:T(128)S(6)} %copy.132, s32[]{:T(128)} %constant.47.clone.1..sunk, s32[]{:T(128)} %constant.47.clone.1..sunk, s32[]{:T(128)} %constant.47.clone.1..sunk) | dynamic-update-slice | bytes 262148 | tf_op jit(solution)/shard_map/while/body/jit(dynamic_update_index_in_dim)/dynamic_update_slice | solution.py:95
  155.2 0.1 pad_maximum_fusion.1
  155.3 19.3 %all_gather.7 = bf16[8,4,8193]{2,1,0:T(4,128)(2,1)S(1)} all-gather(bf16[1,4,8193]{2,1,0:T(4,128)(2,1)S(1)} %pad_maximum_fusion.1), channel_id=1, replica_groups=mesh['dp'=8,'seq'=8,'tp'=16] {'seq'}, dimensions={0}, use_global_device_ids=true | all-gather | bytes 589896 | tf_op jit(solution)/shard_map/all_gather | solution.py:46
  174.6 1.2 split.9
  175.7 0.9 reshape.136
  176.6 0.1 copy.105
  176.7 1.6 reshape.138
  178.3 0.1 select_reduce_fusion
  178.5 0.2 reduce_window_sum.35
  178.7 0.7 fusion.19
  179.4 1.4 multiply_reduce_fusion
  180.8 19.7 %all_to_all.10 = f32[16,256,4]{1,2,0:T(4,128)S(1)} all-to-all(f32[16,256,4]{1,2,0:T(4,128)S(1)} %broadcast_in_dim.80), channel_id=1, replica_groups=mesh['dp'=8,'seq'=8,'tp'=16] {'tp'}, dimensions={0} | all-to-all | bytes 131072 | tf_op jit(solution)/shard_map/all_to_all | solution.py:34
  200.6 0.1 fusion.33
  200.7 2.1 convolution_convert_fusion
  202.8 68.2 %reduce-scatter.2.cloned.1.call-done = bf16[16,4096]{1,0:T(8,128)(2,1)} async-done(((bf16[256,4096]{1,0:T(8,128)(2,1)}), bf16[16,4096]{1,0:T(8,128)(2,1)}) %reduce-scatter.2.cloned.1.call-update) | async-done | bytes 131088 | tf_op jit(solution)/shard_map/reduce_scatter | solution.py:209
  271.1 1.6 fusion.31
  (66 shorter events, 1.1 us)
Async XLA Ops:
  6.5 194.2 %copy-start = (bf16[256,4096]{1,0:T(8,128)(2,1)S(1)}, bf16[256,4096]{1,0:T(8,128)(2,1)}, u32[]{:S(2)}) copy-start(bf16[256,4096]{1,0:T(8,128)(2,1)} %param.27) | copy-start | bytes 6291460
  6.5 87.3 %all-gather.2.cloned.1.call-start = ((), (), s32[]{:S(2)}) async-start(), calls=%async_computation.3 | async-start | bytes 2228224 | tf_op jit(solution)/shard_map/all_gather | solution.py:134
  11.0 96.4 %copy-start.6 = (f32[4,256]{1,0:T(4,128)S(1)}, f32[4,256]{1,0:T(4,128)}, u32[]{:S(2)}) copy-start(f32[4,256]{1,0:T(4,128)} %param.23) | copy-start | bytes 12292
  11.0 96.4 %copy-start.5 = (bf16[4096,4]{0,1:T(4,128)(2,1)S(1)}, bf16[4096,4]{0,1:T(4,128)(2,1)}, u32[]{:S(2)}) copy-start(bf16[4096,4]{0,1:T(4,128)(2,1)} %param.20) | copy-start | bytes 98308
  11.0 96.4 %copy-start.8 = (f32[4]{0:T(128)S(1)}, f32[4]{0:T(128)}, u32[]{:S(2)}) copy-start(f32[4]{0:T(128)} %param.21) | copy-start | bytes 52
  96.4 2.1 collective-permute-start.1
  99.5 32.7 %all-to-all-start = ((bf16[16,256,64]{1,2,0:T(8,128)(2,1)}), bf16[16,256,64]{1,2,0:T(8,128)(2,1)S(1)}, u32[]{:S(2)}, u32[]{:S(2)}) async-start(bf16[16,256,64]{1,2,0:T(8,128)(2,1)} %broadcast_in_dim.77), calls=%async_computation | async-start | bytes 1048576 | tf_op jit(solution)/shard_map/all_to_all | solution.py:34
  107.3 163.8 %reduce-scatter.2.cloned.1.call-start = ((), (), s32[]{:S(2)}) async-start(), calls=%async_computation.4 | async-start | bytes 2228224 | tf_op jit(solution)/shard_map/reduce_scatter | solution.py:209
  111.4 7.7 %copy-start.1 = (bf16[256,4096]{1,0:T(8,128)(2,1)S(1)}, bf16[256,4096]{1,0:T(8,128)(2,1)}, u32[]{:S(2)}) copy-start(bf16[256,4096]{1,0:T(8,128)(2,1)} %all-gather.2.cloned.1.call-done) | copy-start | bytes 6291460
  111.4 7.7 %copy-start.10 = (bf16[4096,256]{1,0:T(8,128)(2,1)S(1)}, bf16[4096,256]{1,0:T(8,128)(2,1)}, u32[]{:S(2)}) copy-start(bf16[4096,256]{1,0:T(8,128)(2,1)} %param.18) | copy-start | bytes 6291460
  115.2 5.9 %collective-permute-start = (bf16[3,256]{1,0:T(4,128)(2,1)S(1)}, bf16[3,256]{1,0:T(4,128)(2,1)S(1)}, u32[]{:S(2)}, u32[]{:S(2)}) collective-permute-start(bf16[3,256]{1,0:T(4,128)(2,1)S(1)} %slice.89), channel_id=1, source_target_pairs={{0,16},{16,32},{32,48},{48,64},{64,80},{80,96},{96,112},{1,17},{17... | collective-permute-start | bytes 4616 | tf_op jit(solution)/shard_map/ppermute | solution.py:23
  155.1 20.6 %copy-start.4 = (f32[2,128,4,64]{1,0,3,2:T(2,128)S(1)}, f32[2,128,4,64]{1,0,3,2:T(2,128)}, u32[]{:S(2)}) copy-start(f32[2,128,4,64]{1,0,3,2:T(2,128)} %get-tuple-element.48) | copy-start | bytes 786436
  155.1 24.3 %copy-start.3 = (f32[256,256]{0,1:T(8,128)S(1)}, f32[256,256]{0,1:T(8,128)}, u32[]{:S(2)}) copy-start(f32[256,256]{0,1:T(8,128)} %copy.92) | copy-start | bytes 786436
  155.1 24.3 %copy-start.9 = (f32[4]{0:T(128)S(1)}, f32[4]{0:T(128)}, u32[]{:S(2)}) copy-start(f32[4]{0:T(128)} %param.25) | copy-start | bytes 52
  176.6 24.0 %copy-start.7 = (f32[256]{0:T(256)S(1)}, f32[256]{0:T(256)}, u32[]{:S(2)}) copy-start(f32[256]{0:T(256)} %param.26) | copy-start | bytes 3076
  202.8 68.3 %copy-start.2 = (bf16[16,4096]{1,0:T(8,128)(2,1)S(1)}, bf16[16,4096]{1,0:T(8,128)(2,1)}, u32[]{:S(2)}) copy-start(bf16[16,4096]{1,0:T(8,128)(2,1)} %param.15) | copy-start | bytes 393220
Sparse Core Ops, SparseCore 0:
  10.0 83.8 all-gather.1
  202.9 68.0 reduce-scatter.1
where the time goes:
time: 281 us; the launch traced here: 279 us
  waiting for transfers between devices  159 us (57%)
  blocking collectives  39 us (14%)
  local copies, waits for them, and re-layouts  28 us (10%)
  matrix products  17.9 us (6%)
  between operations  13.7 us (5%)
  starting transfers between devices  12.9 us (5%)
  other arithmetic  9.43 us (3%)
    all_gather x1, waiting for transfers between devices, body(): row_piece = lax.all_gather(normed, 'tp', axis=0, tiled=True)  82.9 us
    reduce_scatter x1, waiting for transfers between devices, body(): lax.psum_scatter(jnp.dot(mixed_out, proj_output, preferred_element_type=j...  68.2 us
    all_to_all x1, blocking collectives, from_everyone(): return lax.all_to_all(copies, axis, split_axis=0, concat_axis=0, tiled=True)  19.7 us
    all_gather x1, blocking collectives, sent_together(): out = lax.all_gather(both, axis, axis=dim, tiled=True)  19.3 us
    dynamic_update_slice x2, local copies, waits for them, and re-layouts, scan_blocks(): lax.scan(partial(block_step, copies=copies), carry_state, (split_blocks(v...  8.37 us
    all_to_all x1, starting transfers between devices, from_everyone(): return lax.all_to_all(copies, axis, split_axis=0, concat_axis=0, tiled=True)  7.72 us
    all_to_all x1, waiting for transfers between devices, from_everyone(): return lax.all_to_all(copies, axis, split_axis=0, concat_axis=0, tiled=True)  6.53 us
  transfers between devices with their start and end apart: 5, of which 4 were waited for; matrix products, arithmetic and copies ran while one was open for 6% of the time, Pallas kernels for 0%

commit v1 on v0

--- a/solution.py
+++ b/solution.py
@@ -46,6 +46,49 @@
     out = lax.all_gather(both, axis, axis=dim, tiled=True)
     tiles = jnp.split(out, [sum(widths[:k]) for k in range(1, len(widths))], axis=along)
     return tuple((b.reshape(*out.shape[:along], *a.shape[along:]) for a, b in zip(arrays, tiles)))
+
+
+def gather_rows(x):
+    rows, width = x.shape
+    count = lax.axis_size("tp")
+    chunk = (2**20 // (2 * rows * count) - 1) // 128 * 128
+    whole = width // chunk
+    rest = from_everyone(x[:, whole * chunk :], "tp").reshape(count * rows, width - whole * chunk)
+    parts = [
+        lax.all_gather(x[:, k * chunk : (k + 1) * chunk], "tp", axis=0, tiled=True)
+        for k in range(whole)
+    ]
+    return jnp.concatenate(parts + [rest], axis=1)
+
+
+def ring_scatter(partial, axis):
+    count = lax.axis_size(axis)
+    me = lax.axis_index(axis)
+    up = [(k, (k + 1) % count) for k in range(count)]
+    down = [(k, (k - 1) % count) for k in range(count)]
+    far = count // 2
+    near = count - 1 - far
+
+    def piece(offset):
+        return lax.dynamic_index_in_dim(partial, (me + offset) % count, 0, keepdims=False)
+
+    rising = piece(far)
+    falling = piece(-near)
+    for step in range(1, far + 1):
+        rising = lax.ppermute(rising, axis, up)
+        if step <= near:
+            falling = lax.ppermute(falling, axis, down)
+        if step < far:
+            rising = (
+                rising.astype(jnp.float32) + piece(far - step).astype(jnp.float32)
+            ).astype(partial.dtype)
+        if step < near:
+            falling = (
+                falling.astype(jnp.float32) + piece(step - near).astype(jnp.float32)
+            ).astype(partial.dtype)
+    return (
+        piece(0).astype(jnp.float32) + rising.astype(jnp.float32) + falling.astype(jnp.float32)
+    )
 
 
 def causal_conv(values, kernel_taps, before):
@@ -131,7 +174,7 @@
     state_width = proj_states.shape[1]
     heads_local = proj_step.shape[1]
     copies = heads_local // GROUPS
-    row_piece = lax.all_gather(normed, "tp", axis=0, tiled=True)
+    row_piece = gather_rows(normed)
     projected = jnp.concatenate(
         (
             jnp.dot(row_piece, proj_inner, preferred_element_type=jnp.float32),
@@ -148,9 +191,12 @@
     step_size = jax.nn.softplus(projected[:, 2 * inner_width + state_width :] + step_bias)
     log_decay = -jnp.exp(log_rate) * step_size
     margin = conv_inner.shape[0] - 1
-    before_inner, before_states = from_behind(
-        (inner_proj[row_count - margin :], state_proj[row_count - margin :]), "seq", 1
-    )
+    before = from_behind(
+        jnp.concatenate((inner_proj[row_count - margin :], state_proj[row_count - margin :]), axis=1),
+        "seq",
+        1,
+    )
+    before_inner, before_states = before[:, :inner_width], before[:, inner_width:]
     mixed_inner = jax.nn.silu(
         causal_conv(inner_proj.astype(jnp.float32), conv_inner, before_inner.astype(jnp.float32))
     ).astype(jnp.bfloat16)
@@ -206,12 +252,9 @@
     grouped = gated_out.reshape(row_count, copies, GROUPS, HEAD_DIM)
     normal_out = grouped * lax.rsqrt(mean_square + epsilon)
     mixed_out = (normal_out.reshape(row_count, inner_width) * norm_gain).astype(jnp.bfloat16)
-    summed = lax.psum_scatter(
-        jnp.dot(mixed_out, proj_output, preferred_element_type=jnp.float32).astype(jnp.bfloat16),
-        "tp",
-        scatter_dimension=0,
-        tiled=True,
-    ).astype(jnp.float32)
+    partial = jnp.dot(mixed_out, proj_output, preferred_element_type=jnp.float32)
+    partial = partial.astype(jnp.bfloat16).reshape(-1, tokens.shape[0], tokens.shape[1])
+    summed = ring_scatter(partial, "tp")
     return (tokens_wide + summed).astype(jnp.bfloat16)
 
 

time: 281 us -> 299 us (1.064)
  waiting for transfers between devices: 159 us -> 52.8 us
  starting transfers between devices: 12.9 us -> 89.6 us
  blocking collectives: 39 us -> 93.3 us
  between operations: 13.7 us -> 0.82 us
  other arithmetic: 9.43 us -> 14.2 us
    all_gather x1 -> x0, waiting for transfers between devices: 82.9 us -> none  [body(): row_piece = lax.all_gather(normed, 'tp', axis=0, tiled=True)]
    all_gather x0 -> x2, blocking collectives: none -> 73.5 us  [gather_rows(): lax.all_gather(x[:, k * chunk:(k + 1) * chunk], 'tp', axis=0, tiled=True)]
    reduce_scatter x1 -> x0, waiting for transfers between devices: 68.2 us -> none  [body(): lax.psum_scatter(jnp.dot(mixed_out, proj_output, preferred_element_type=j...]
    ppermute x0 -> x15, starting transfers between devices: none -> 53.2 us  [the longest x7 33.7 us: ring_scatter(): falling = lax.ppermute(falling, axis, down)]
    all_to_all x1 -> x3, starting transfers between devices: 7.72 us -> 35 us  [from_everyone(): return lax.all_to_all(copies, axis, split_axis=0, concat_axis=0, tiled=True)]
    ppermute x0 -> x15, waiting for transfers between devices: none -> 23.5 us  [the longest x8 13.9 us: ring_scatter(): rising = lax.ppermute(rising, axis, up)]
    all_to_all x1 -> x3, waiting for transfers between devices: 6.53 us -> 28.4 us  [from_everyone(): return lax.all_to_all(copies, axis, split_axis=0, concat_axis=0, tiled=True)]
    all_to_all x1 -> x0, blocking collectives: 19.7 us -> none  [from_everyone(): return lax.all_to_all(copies, axis, split_axis=0, concat_axis=0, tiled=True)]
  transfers between devices with their start and end apart: 5 -> 19, of which waited for: 4 -> 17; matrix products, arithmetic and copies ran while one was open for 6% -> 4% of each run, Pallas kernels for 0% -> 0%
where the time goes in v1:
time: 299 us; the launch traced here: 297 us
  blocking collectives  93.3 us (31%)
  starting transfers between devices  89.6 us (30%)
  waiting for transfers between devices  52.8 us (18%)
  local copies, waits for them, and re-layouts  28.9 us (10%)
  matrix products  17.3 us (6%)
  other arithmetic  14.2 us (5%)
    all_gather x2, blocking collectives, gather_rows(): lax.all_gather(x[:, k * chunk:(k + 1) * chunk], 'tp', axis=0, tiled=True)  73.5 us
    all_to_all x3, starting transfers between devices, from_everyone(): return lax.all_to_all(copies, axis, split_axis=0, concat_axis=0, tiled=True)  35 us
    ppermute x7, starting transfers between devices, ring_scatter(): falling = lax.ppermute(falling, axis, down)  33.7 us
    all_to_all x3, waiting for transfers between devices, from_everyone(): return lax.all_to_all(copies, axis, split_axis=0, concat_axis=0, tiled=True)  28.4 us
    all_gather x1, blocking collectives, sent_together(): out = lax.all_gather(both, axis, axis=dim, tiled=True)  19.9 us
    ppermute x8, starting transfers between devices, ring_scatter(): rising = lax.ppermute(rising, axis, up)  19.5 us
    ppermute x8, waiting for transfers between devices, ring_scatter(): rising = lax.ppermute(rising, axis, up)  13.9 us
    ppermute x7, waiting for transfers between devices, ring_scatter(): falling = lax.ppermute(falling, axis, down)  9.61 us
  transfers between devices with their start and end apart: 19, of which 17 were waited for; matrix products, arithmetic and copies ran while one was open for 4% of the time, Pallas kernels for 0%

profile of v1, /device:TPU:56, one launch (start us, length us, event | category | flops | bytes accessed | tf_op | source)
XLA Modules:
  0.0 297.0 jit_solution(12564160073921169001)
XLA Ops:
  0.0 1.2 fusion.17
  1.2 1.0 fusion.19
  2.9 18.9 %all-to-all-start = ((bf16[16,16,256]{2,1,0:T(8,128)(2,1)}), bf16[16,16,256]{2,1,0:T(8,128)(2,1)S(1)}, u32[]{:S(2)}, u32[]{:S(2)}) async-start(bf16[16,16,256]{2,1,0:T(8,128)(2,1)} %broadcast_in_dim.80), calls=%async_computation | async-start | bytes 262144 | tf_op jit(solution)/shard_map/all_to_all | solution.py:34
  21.8 38.2 %all_gather.9 = bf16[256,1920]{1,0:T(8,128)(2,1)S(1)} all-gather(bf16[16,1920]{1,0:T(8,128)(2,1)S(1)} %get-tuple-element.165), channel_id=1, replica_groups=mesh['dp'=8,'seq'=8,'tp'=16] {'tp'}, dimensions={0}, use_global_device_ids=true | all-gather | bytes 1044480 | tf_op jit(solution)/shard_map/all_gather | solution.py:58
  60.0 35.3 %all_gather.10 = bf16[256,1920]{1,0:T(8,128)(2,1)} all-gather(bf16[16,1920]{1,0:T(8,128)(2,1)S(1)} %get-tuple-element.166), channel_id=1, replica_groups=mesh['dp'=8,'seq'=8,'tp'=16] {'tp'}, dimensions={0}, use_global_device_ids=true | all-gather | bytes 1044480 | tf_op jit(solution)/shard_map/all_gather | solution.py:58
  95.3 2.2 fusion.63
  97.7 1.6 fusion.64
  99.4 1.3 collective-permute-start
  102.7 9.4 %all-to-all-start.1 = ((bf16[16,256,64]{1,2,0:T(8,128)(2,1)}), bf16[16,256,64]{1,2,0:T(8,128)(2,1)S(1)}, u32[]{:S(2)}, u32[]{:S(2)}) async-start(bf16[16,256,64]{1,2,0:T(8,128)(2,1)} %broadcast_in_dim.81), calls=%async_computation.1 | async-start | bytes 1048576 | tf_op jit(solution)/shard_map/all_to_all | solution.py:34
  112.1 2.3 fusion.58
  114.6 1.2 reduce-window.6
  117.2 3.9 %divide_multiply_fusion = f32[256,256]{0,1:T(8,128)} fusion(bf16[4096,256]{1,0:T(8,128)(2,1)} %param.18, bf16[256,256]{1,0:T(8,128)(2,1)S(1)} %bitcast.242, bf16[256,1920]{1,0:T(8,128)(2,1)} %all_gather.10, bf16[256,1920]{1,0:T(8,128)(2,1)} %copy-done.5), kind=kOutput, calls=%fused_computation.88 | convolution fusion | flops 543555584 | bytes 4456448 | tf_op jit(solution)/shard_map/dot_general | solution.py:181
  121.8 15.2 %all-to-all-done.1 = bf16[16,256,64]{1,2,0:T(8,128)(2,1)S(1)} async-done(((bf16[16,256,64]{1,2,0:T(8,128)(2,1)}), bf16[16,256,64]{1,2,0:T(8,128)(2,1)S(1)}, u32[]{:S(2)}, u32[]{:S(2)}) %all-to-all-start.1) | async-done | bytes 524320 | tf_op jit(solution)/shard_map/all_to_all | solution.py:34
  137.0 1.1 fusion.60
  138.1 2.1 reshape_squeeze.7
  140.2 2.1 reshape_squeeze.6
  142.3 19.5 %while.13 = (s32[]{:T(128)}, f32[4,64,128]{2,1,0:T(8,128)S(1)}, f32[2,128,4,64]{1,0,3,2:T(2,128)}, f32[2,128,4]{2,1,0:T(8,128)}, f32[2,128,4,64]{1,0,3,2:T(2,128...) while((s32[]{:T(128)}, f32[4,64,128]{2,1,0:T(8,128)S(1)}, ...), condition=%wide.region_3.4_spmd.clone, body=%wide.region_1.3_spmd.clone.sunk | while | flops 252297728 | bytes 4272376 | solution.py:138
  143.9 1.8 constant_dynamic-slice_fusion.5
  147.9 4.2 %dynamic_update_slice.6 = f32[2,128,4,64]{1,0,3,2:T(2,128)} dynamic-update-slice(f32[2,128,4,64]{1,0,3,2:T(2,128)} %get-tuple-element.257, f32[1,128,4,64]{1,0,3,2:T(1,128)S(1)} %bitcast.222, s32[]{:T(128)S(6)} %copy.172, s32[]{:T(128)} %constant.168.clone.1..sunk, s32[]{:T(128)} %constant.168.clone.1..sunk, s32[]{:T(128)} %constant.168.clone.1..sunk) | dynamic-update-slice | bytes 262148 | tf_op jit(solution)/shard_map/while/body/jit(dynamic_update_index_in_dim)/dynamic_update_slice | solution.py:138
  153.6 1.8 constant_dynamic-slice_fusion.5
  157.6 4.2 %dynamic_update_slice.6 = f32[2,128,4,64]{1,0,3,2:T(2,128)} dynamic-update-slice(f32[2,128,4,64]{1,0,3,2:T(2,128)} %get-tuple-element.257, f32[1,128,4,64]{1,0,3,2:T(1,128)S(1)} %bitcast.222, s32[]{:T(128)S(6)} %copy.172, s32[]{:T(128)} %constant.168.clone.1..sunk, s32[]{:T(128)} %constant.168.clone.1..sunk, s32[]{:T(128)} %constant.168.clone.1..sunk) | dynamic-update-slice | bytes 262148 | tf_op jit(solution)/shard_map/while/body/jit(dynamic_update_index_in_dim)/dynamic_update_slice | solution.py:138
  162.0 19.9 %all_gather.11 = bf16[8,4,8193]{2,1,0:T(4,128)(2,1)S(1)} all-gather(bf16[1,4,8193]{2,1,0:T(4,128)(2,1)S(1)} %pad_maximum_fusion.3), channel_id=1, replica_groups=mesh['dp'=8,'seq'=8,'tp'=16] {'seq'}, dimensions={0}, use_global_device_ids=true | all-gather | bytes 589896 | tf_op jit(solution)/shard_map/all_gather | solution.py:46
  181.9 1.2 split.9
  184.1 1.6 reshape.173
  186.8 1.4 multiply_reduce_fusion
  188.8 6.8 %all-to-all-start.2 = ((f32[16,256,4]{1,2,0:T(4,128)}), f32[16,256,4]{1,2,0:T(4,128)S(1)}, u32[]{:S(2)}, u32[]{:S(2)}) async-start(f32[16,256,4]{1,2,0:T(4,128)} %broadcast_in_dim.84), calls=%async_computation.2 | async-start | bytes 131072 | tf_op jit(solution)/shard_map/all_to_all | solution.py:34
  195.6 13.2 %all-to-all-done.2 = f32[16,256,4]{1,2,0:T(4,128)S(1)} async-done(((f32[16,256,4]{1,2,0:T(4,128)}), f32[16,256,4]{1,2,0:T(4,128)S(1)}, u32[]{:S(2)}, u32[]{:S(2)}) %all-to-all-start.2) | async-done | bytes 65568 | tf_op jit(solution)/shard_map/all_to_all | solution.py:34
  209.8 1.3 copy-done.1
  211.1 2.9 collective-permute-start.1
  214.0 4.2 %collective-permute-start.9 = (bf16[16,4096]{1,0:T(8,128)(2,1)S(1)}, bf16[16,4096]{1,0:T(8,128)(2,1)S(1)}, u32[]{:S(2)}, u32[]{:S(2)}) collective-permute-start(bf16[16,4096]{1,0:T(8,128)(2,1)S(1)} %get-tuple-element.162), channel_id=1, source_target_pairs={{0,15},{1,0},{2,1},{3,2},{4,3},{5,4},{6,5},{7,6},{8,7},{9,8},{10,9... | collective-permute-start | bytes 393224 | tf_op jit(solution)/shard_map/ppermute | solution.py:80
  218.2 1.0 collective-permute-done.1
  220.1 1.9 collective-permute-start.2
  222.1 6.1 %collective-permute-done.2 = bf16[16,4096]{1,0:T(8,128)(2,1)S(1)} collective-permute-done((bf16[16,4096]{1,0:T(8,128)(2,1)S(1)}, bf16[16,4096]{1,0:T(8,128)(2,1)S(1)}, u32[]{:S(2)}, u32[]{:S(2)}) %collective-permute-start.2) | collective-permute-done | bytes 131104 | tf_op jit(solution)/shard_map/ppermute | solution.py:78
  228.2 1.0 fusion.40
  229.3 1.9 collective-permute-start.3
  231.2 5.1 %collective-permute-start.10 = (bf16[16,4096]{1,0:T(8,128)(2,1)S(1)}, bf16[16,4096]{1,0:T(8,128)(2,1)S(1)}, u32[]{:S(2)}, u32[]{:S(2)}) collective-permute-start(bf16[16,4096]{1,0:T(8,128)(2,1)S(1)} %get-tuple-element.160), channel_id=1, source_target_pairs={{0,15},{1,0},{2,1},{3,2},{4,3},{5,4},{6,5},{7,6},{8,7},{9,8},{10,9... | collective-permute-start | bytes 393224 | tf_op jit(solution)/shard_map/ppermute | solution.py:80
  236.4 1.0 collective-permute-done.3
  237.3 1.5 collective-permute-done.10
  238.8 1.0 fusion.39
  239.9 1.9 collective-permute-start.4
  241.8 5.6 %collective-permute-start.11 = (bf16[16,4096]{1,0:T(8,128)(2,1)S(1)}, bf16[16,4096]{1,0:T(8,128)(2,1)S(1)}, u32[]{:S(2)}, u32[]{:S(2)}) collective-permute-start(bf16[16,4096]{1,0:T(8,128)(2,1)S(1)} %get-tuple-element.158), channel_id=1, source_target_pairs={{0,15},{1,0},{2,1},{3,2},{4,3},{5,4},{6,5},{7,6},{8,7},{9,8},{10,9... | collective-permute-start | bytes 393224 | tf_op jit(solution)/shard_map/ppermute | solution.py:80
  247.4 1.0 collective-permute-done.4
  248.4 1.5 collective-permute-done.11
  249.9 1.0 fusion.38
  250.9 2.1 collective-permute-start.5
  253.0 5.3 %collective-permute-start.12 = (bf16[16,4096]{1,0:T(8,128)(2,1)S(1)}, bf16[16,4096]{1,0:T(8,128)(2,1)S(1)}, u32[]{:S(2)}, u32[]{:S(2)}) collective-permute-start(bf16[16,4096]{1,0:T(8,128)(2,1)S(1)} %get-tuple-element.156), channel_id=1, source_target_pairs={{0,15},{1,0},{2,1},{3,2},{4,3},{5,4},{6,5},{7,6},{8,7},{9,8},{10,9... | collective-permute-start | bytes 393224 | tf_op jit(solution)/shard_map/ppermute | solution.py:80
  258.4 1.0 collective-permute-done.5
  259.4 1.5 collective-permute-done.12
  260.9 1.0 fusion.37
  261.9 2.9 collective-permute-start.6
  264.9 4.5 %collective-permute-start.13 = (bf16[16,4096]{1,0:T(8,128)(2,1)S(1)}, bf16[16,4096]{1,0:T(8,128)(2,1)S(1)}, u32[]{:S(2)}, u32[]{:S(2)}) collective-permute-start(bf16[16,4096]{1,0:T(8,128)(2,1)S(1)} %get-tuple-element.154), channel_id=1, source_target_pairs={{0,15},{1,0},{2,1},{3,2},{4,3},{5,4},{6,5},{7,6},{8,7},{9,8},{10,9... | collective-permute-start | bytes 393224 | tf_op jit(solution)/shard_map/ppermute | solution.py:80
  269.5 1.0 collective-permute-done.6
  270.4 1.9 collective-permute-done.13
  272.3 1.0 fusion.36
  273.4 2.9 collective-permute-start.7
  276.2 4.4 %collective-permute-start.14 = (bf16[16,4096]{1,0:T(8,128)(2,1)S(1)}, bf16[16,4096]{1,0:T(8,128)(2,1)S(1)}, u32[]{:S(2)}, u32[]{:S(2)}) collective-permute-start(bf16[16,4096]{1,0:T(8,128)(2,1)S(1)} %get-tuple-element.152), channel_id=1, source_target_pairs={{0,15},{1,0},{2,1},{3,2},{4,3},{5,4},{6,5},{7,6},{8,7},{9,8},{10,9... | collective-permute-start | bytes 393224 | tf_op jit(solution)/shard_map/ppermute | solution.py:80
  280.6 2.0 collective-permute-done.7
  282.6 1.7 collective-permute-done.14
  284.3 1.0 fusion.35
  285.4 2.9 collective-permute-start.8
  288.3 4.6 %collective-permute-start.15 = (bf16[16,4096]{1,0:T(8,128)(2,1)S(1)}, bf16[16,4096]{1,0:T(8,128)(2,1)S(1)}, u32[]{:S(2)}, u32[]{:S(2)}) collective-permute-start(bf16[16,4096]{1,0:T(8,128)(2,1)S(1)} %get-tuple-element.150), channel_id=1, source_target_pairs={{0,15},{1,0},{2,1},{3,2},{4,3},{5,4},{6,5},{7,6},{8,7},{9,8},{10,9... | collective-permute-start | bytes 393224 | tf_op jit(solution)/shard_map/ppermute | solution.py:80
  292.9 1.0 collective-permute-done.8
  293.9 1.5 collective-permute-done.15
  295.4 1.6 fusion.20
  (116 shorter events, 17.3 us)
Async XLA Ops:
  0.0 209.0 %copy-start = (bf16[256,4096]{1,0:T(8,128)(2,1)S(1)}, bf16[256,4096]{1,0:T(8,128)(2,1)}, u32[]{:S(2)}) copy-start(bf16[256,4096]{1,0:T(8,128)(2,1)} %param.27) | copy-start | bytes 6291460
  0.0 60.0 %copy-start.10 = (f32[4,64]{1,0:T(4,128)S(1)}, f32[4,64]{1,0:T(4,128)}, u32[]{:S(2)}) copy-start(f32[4,64]{1,0:T(4,128)} %param.24) | copy-start | bytes 3076
  2.9 92.4 %all-to-all-start = ((bf16[16,16,256]{2,1,0:T(8,128)(2,1)}), bf16[16,16,256]{2,1,0:T(8,128)(2,1)S(1)}, u32[]{:S(2)}, u32[]{:S(2)}) async-start(bf16[16,16,256]{2,1,0:T(8,128)(2,1)} %broadcast_in_dim.80), calls=%async_computation | async-start | bytes 262144 | tf_op jit(solution)/shard_map/all_to_all | solution.py:34
  60.0 37.6 %copy-start.5 = (bf16[256,1920]{1,0:T(8,128)(2,1)}, bf16[256,1920]{1,0:T(8,128)(2,1)S(1)}, u32[]{:S(2)}) copy-start(bf16[256,1920]{1,0:T(8,128)(2,1)S(1)} %all_gather.9) | copy-start | bytes 2949124
  95.3 2.3 copy-start.6
  95.3 2.4 copy-start.13
  99.3 12.8 %copy-start.15 = (f32[4]{0:T(128)S(1)}, f32[4]{0:T(128)}, u32[]{:S(2)}) copy-start(f32[4]{0:T(128)} %param.22) | copy-start | bytes 52
  99.3 12.8 %copy-start.9 = (f32[4,256]{1,0:T(4,128)S(1)}, f32[4,256]{1,0:T(4,128)}, u32[]{:S(2)}) copy-start(f32[4,256]{1,0:T(4,128)} %param.23) | copy-start | bytes 12292
  99.3 12.8 %copy-start.14 = (bf16[4096,4]{0,1:T(4,128)(2,1)S(1)}, bf16[4096,4]{0,1:T(4,128)(2,1)}, u32[]{:S(2)}) copy-start(bf16[4096,4]{0,1:T(4,128)(2,1)} %param.20) | copy-start | bytes 98308
  99.3 12.8 %copy-start.16 = (f32[4]{0:T(128)S(1)}, f32[4]{0:T(128)}, u32[]{:S(2)}) copy-start(f32[4]{0:T(128)} %param.21) | copy-start | bytes 52
  99.4 2.2 collective-permute-start
  102.7 34.3 %all-to-all-start.1 = ((bf16[16,256,64]{1,2,0:T(8,128)(2,1)}), bf16[16,256,64]{1,2,0:T(8,128)(2,1)S(1)}, u32[]{:S(2)}, u32[]{:S(2)}) async-start(bf16[16,256,64]{1,2,0:T(8,128)(2,1)} %broadcast_in_dim.81), calls=%async_computation.1 | async-start | bytes 1048576 | tf_op jit(solution)/shard_map/all_to_all | solution.py:34
  117.2 3.9 %copy-start.8 = (f32[256,256]{0,1:T(8,128)S(1)}, f32[256,256]{0,1:T(8,128)}, u32[]{:S(2)}) copy-start(f32[256,256]{0,1:T(8,128)} %get-tuple-element.179) | copy-start | bytes 786436
  121.6 20.7 %copy-start.2 = (f32[256,256]{0,1:T(8,128)}, f32[256,256]{0,1:T(8,128)S(1)}, u32[]{:S(2)}) copy-start(f32[256,256]{0,1:T(8,128)S(1)} %fusion.44) | copy-start | bytes 786436
  161.8 21.2 %copy-start.7 = (f32[2,128,4,64]{1,0,3,2:T(2,128)S(1)}, f32[2,128,4,64]{1,0,3,2:T(2,128)}, u32[]{:S(2)}) copy-start(f32[2,128,4,64]{1,0,3,2:T(2,128)} %get-tuple-element.48) | copy-start | bytes 786436
  161.8 24.9 %copy-start.3 = (f32[256,256]{0,1:T(8,128)S(1)}, f32[256,256]{0,1:T(8,128)}, u32[]{:S(2)}) copy-start(f32[256,256]{0,1:T(8,128)} %copy-done.2) | copy-start | bytes 786436
  161.8 24.9 %copy-start.12 = (f32[4]{0:T(128)S(1)}, f32[4]{0:T(128)}, u32[]{:S(2)}) copy-start(f32[4]{0:T(128)} %param.25) | copy-start | bytes 52
  183.9 25.0 %copy-start.11 = (f32[256]{0:T(256)S(1)}, f32[256]{0:T(256)}, u32[]{:S(2)}) copy-start(f32[256]{0:T(256)} %param.26) | copy-start | bytes 3076
  188.8 20.1 %all-to-all-start.2 = ((f32[16,256,4]{1,2,0:T(4,128)}), f32[16,256,4]{1,2,0:T(4,128)S(1)}, u32[]{:S(2)}, u32[]{:S(2)}) async-start(f32[16,256,4]{1,2,0:T(4,128)} %broadcast_in_dim.84), calls=%async_computation.2 | async-start | bytes 131072 | tf_op jit(solution)/shard_map/all_to_all | solution.py:34
  209.8 1.3 copy-start.1
  211.1 8.1 %collective-permute-start.1 = (bf16[16,4096]{1,0:T(8,128)(2,1)S(1)}, bf16[16,4096]{1,0:T(8,128)(2,1)S(1)}, u32[]{:S(2)}, u32[]{:S(2)}) collective-permute-start(bf16[16,4096]{1,0:T(8,128)(2,1)S(1)} %get-tuple-element.161), channel_id=1, source_target_pairs={{0,1},{1,2},{2,3},{3,4},{4,5},{5,6},{6,7},{7,8},{8,9},{9,10},{10,1... | collective-permute-start | bytes 393224 | tf_op jit(solution)/shard_map/ppermute | solution.py:78
  214.0 8.1 %collective-permute-start.9 = (bf16[16,4096]{1,0:T(8,128)(2,1)S(1)}, bf16[16,4096]{1,0:T(8,128)(2,1)S(1)}, u32[]{:S(2)}, u32[]{:S(2)}) collective-permute-start(bf16[16,4096]{1,0:T(8,128)(2,1)S(1)} %get-tuple-element.162), channel_id=1, source_target_pairs={{0,15},{1,0},{2,1},{3,2},{4,3},{5,4},{6,5},{7,6},{8,7},{9,8},{10,9... | collective-permute-start | bytes 393224 | tf_op jit(solution)/shard_map/ppermute | solution.py:80
  220.1 8.1 %collective-permute-start.2 = (bf16[16,4096]{1,0:T(8,128)(2,1)S(1)}, bf16[16,4096]{1,0:T(8,128)(2,1)S(1)}, u32[]{:S(2)}, u32[]{:S(2)}) collective-permute-start(bf16[16,4096]{1,0:T(8,128)(2,1)S(1)} %fusion.41), channel_id=1, source_target_pairs={{0,1},{1,2},{2,3},{3,4},{4,5},{5,6},{6,7},{7,8},{8,9},{9,10},{10,1... | collective-permute-start | bytes 393224 | tf_op jit(solution)/shard_map/ppermute | solution.py:78
  229.3 8.1 %collective-permute-start.3 = (bf16[16,4096]{1,0:T(8,128)(2,1)S(1)}, bf16[16,4096]{1,0:T(8,128)(2,1)S(1)}, u32[]{:S(2)}, u32[]{:S(2)}) collective-permute-start(bf16[16,4096]{1,0:T(8,128)(2,1)S(1)} %get-tuple-element.159), channel_id=1, source_target_pairs={{0,1},{1,2},{2,3},{3,4},{4,5},{5,6},{6,7},{7,8},{8,9},{9,10},{10,1... | collective-permute-start | bytes 393224 | tf_op jit(solution)/shard_map/ppermute | solution.py:78
  231.2 7.6 %collective-permute-start.10 = (bf16[16,4096]{1,0:T(8,128)(2,1)S(1)}, bf16[16,4096]{1,0:T(8,128)(2,1)S(1)}, u32[]{:S(2)}, u32[]{:S(2)}) collective-permute-start(bf16[16,4096]{1,0:T(8,128)(2,1)S(1)} %get-tuple-element.160), channel_id=1, source_target_pairs={{0,15},{1,0},{2,1},{3,2},{4,3},{5,4},{6,5},{7,6},{8,7},{9,8},{10,9... | collective-permute-start | bytes 393224 | tf_op jit(solution)/shard_map/ppermute | solution.py:80
  236.4 59.0 %copy-start.4 = (bf16[16,4096]{1,0:T(8,128)(2,1)S(1)}, bf16[16,4096]{1,0:T(8,128)(2,1)}, u32[]{:S(2)}) copy-start(bf16[16,4096]{1,0:T(8,128)(2,1)} %param.15) | copy-start | bytes 393220
  239.9 8.5 %collective-permute-start.4 = (bf16[16,4096]{1,0:T(8,128)(2,1)S(1)}, bf16[16,4096]{1,0:T(8,128)(2,1)S(1)}, u32[]{:S(2)}, u32[]{:S(2)}) collective-permute-start(bf16[16,4096]{1,0:T(8,128)(2,1)S(1)} %get-tuple-element.157), channel_id=1, source_target_pairs={{0,1},{1,2},{2,3},{3,4},{4,5},{5,6},{6,7},{7,8},{8,9},{9,10},{10,1... | collective-permute-start | bytes 393224 | tf_op jit(solution)/shard_map/ppermute | solution.py:78
  241.8 8.1 %collective-permute-start.11 = (bf16[16,4096]{1,0:T(8,128)(2,1)S(1)}, bf16[16,4096]{1,0:T(8,128)(2,1)S(1)}, u32[]{:S(2)}, u32[]{:S(2)}) collective-permute-start(bf16[16,4096]{1,0:T(8,128)(2,1)S(1)} %get-tuple-element.158), channel_id=1, source_target_pairs={{0,15},{1,0},{2,1},{3,2},{4,3},{5,4},{6,5},{7,6},{8,7},{9,8},{10,9... | collective-permute-start | bytes 393224 | tf_op jit(solution)/shard_map/ppermute | solution.py:80
  250.9 8.5 %collective-permute-start.5 = (bf16[16,4096]{1,0:T(8,128)(2,1)S(1)}, bf16[16,4096]{1,0:T(8,128)(2,1)S(1)}, u32[]{:S(2)}, u32[]{:S(2)}) collective-permute-start(bf16[16,4096]{1,0:T(8,128)(2,1)S(1)} %get-tuple-element.155), channel_id=1, source_target_pairs={{0,1},{1,2},{2,3},{3,4},{4,5},{5,6},{6,7},{7,8},{8,9},{9,10},{10,1... | collective-permute-start | bytes 393224 | tf_op jit(solution)/shard_map/ppermute | solution.py:78
  253.0 7.8 %collective-permute-start.12 = (bf16[16,4096]{1,0:T(8,128)(2,1)S(1)}, bf16[16,4096]{1,0:T(8,128)(2,1)S(1)}, u32[]{:S(2)}, u32[]{:S(2)}) collective-permute-start(bf16[16,4096]{1,0:T(8,128)(2,1)S(1)} %get-tuple-element.156), channel_id=1, source_target_pairs={{0,15},{1,0},{2,1},{3,2},{4,3},{5,4},{6,5},{7,6},{8,7},{9,8},{10,9... | collective-permute-start | bytes 393224 | tf_op jit(solution)/shard_map/ppermute | solution.py:80
  261.9 8.5 %collective-permute-start.6 = (bf16[16,4096]{1,0:T(8,128)(2,1)S(1)}, bf16[16,4096]{1,0:T(8,128)(2,1)S(1)}, u32[]{:S(2)}, u32[]{:S(2)}) collective-permute-start(bf16[16,4096]{1,0:T(8,128)(2,1)S(1)} %get-tuple-element.153), channel_id=1, source_target_pairs={{0,1},{1,2},{2,3},{3,4},{4,5},{5,6},{6,7},{7,8},{8,9},{9,10},{10,1... | collective-permute-start | bytes 393224 | tf_op jit(solution)/shard_map/ppermute | solution.py:78
  264.9 7.4 %collective-permute-start.13 = (bf16[16,4096]{1,0:T(8,128)(2,1)S(1)}, bf16[16,4096]{1,0:T(8,128)(2,1)S(1)}, u32[]{:S(2)}, u32[]{:S(2)}) collective-permute-start(bf16[16,4096]{1,0:T(8,128)(2,1)S(1)} %get-tuple-element.154), channel_id=1, source_target_pairs={{0,15},{1,0},{2,1},{3,2},{4,3},{5,4},{6,5},{7,6},{8,7},{9,8},{10,9... | collective-permute-start | bytes 393224 | tf_op jit(solution)/shard_map/ppermute | solution.py:80
  273.4 9.2 %collective-permute-start.7 = (bf16[16,4096]{1,0:T(8,128)(2,1)S(1)}, bf16[16,4096]{1,0:T(8,128)(2,1)S(1)}, u32[]{:S(2)}, u32[]{:S(2)}) collective-permute-start(bf16[16,4096]{1,0:T(8,128)(2,1)S(1)} %get-tuple-element.151), channel_id=1, source_target_pairs={{0,1},{1,2},{2,3},{3,4},{4,5},{5,6},{6,7},{7,8},{8,9},{9,10},{10,1... | collective-permute-start | bytes 393224 | tf_op jit(solution)/shard_map/ppermute | solution.py:78
  276.2 8.1 %collective-permute-start.14 = (bf16[16,4096]{1,0:T(8,128)(2,1)S(1)}, bf16[16,4096]{1,0:T(8,128)(2,1)S(1)}, u32[]{:S(2)}, u32[]{:S(2)}) collective-permute-start(bf16[16,4096]{1,0:T(8,128)(2,1)S(1)} %get-tuple-element.152), channel_id=1, source_target_pairs={{0,15},{1,0},{2,1},{3,2},{4,3},{5,4},{6,5},{7,6},{8,7},{9,8},{10,9... | collective-permute-start | bytes 393224 | tf_op jit(solution)/shard_map/ppermute | solution.py:80
  285.4 8.5 %collective-permute-start.8 = (bf16[16,4096]{1,0:T(8,128)(2,1)S(1)}, bf16[16,4096]{1,0:T(8,128)(2,1)S(1)}, u32[]{:S(2)}, u32[]{:S(2)}) collective-permute-start(bf16[16,4096]{1,0:T(8,128)(2,1)S(1)} %get-tuple-element.149), channel_id=1, source_target_pairs={{0,1},{1,2},{2,3},{3,4},{4,5},{5,6},{6,7},{7,8},{8,9},{9,10},{10,1... | collective-permute-start | bytes 393224 | tf_op jit(solution)/shard_map/ppermute | solution.py:78
  288.3 7.1 %collective-permute-start.15 = (bf16[16,4096]{1,0:T(8,128)(2,1)S(1)}, bf16[16,4096]{1,0:T(8,128)(2,1)S(1)}, u32[]{:S(2)}, u32[]{:S(2)}) collective-permute-start(bf16[16,4096]{1,0:T(8,128)(2,1)S(1)} %get-tuple-element.150), channel_id=1, source_target_pairs={{0,15},{1,0},{2,1},{3,2},{4,3},{5,4},{6,5},{7,6},{8,7},{9,8},{10,9... | collective-permute-start | bytes 393224 | tf_op jit(solution)/shard_map/ppermute | solution.py:80

commit v2 on v0

v2 whole, which is shorter than its diff:
```python
import jax
import jax.numpy as jnp
from jax import lax
from jax.experimental import pallas as pl
from jax.experimental.pallas import tpu as pltpu
from jax.sharding import PartitionSpec as P

HEAD_DIM = 64
STATE = 128
GROUP_HEADS = 16
TAPS = 4
TAIL_ROWS = 8
GROUPS = 4


epsilon = 1e-05
highest = lax.Precision.HIGHEST


def from_behind(value, axis, steps):
    count = lax.axis_size(axis)
    initial, last = (max(0, -steps), min(count, count - steps))
    return lax.ppermute(value, axis, [(source, source + steps) for source in range(initial, last)])


def split_dot(exact, wide, dims, exact_first):
    upper = wide.astype(jnp.bfloat16)
    lower = (wide - upper.astype(jnp.float32)).astype(jnp.bfloat16)

    def product(part):
        pair = (exact, part) if exact_first else (part, exact)
        return lax.dot_general(*pair, (dims, ((), ())), preferred_element_type=jnp.float32)

    return product(upper) + product(lower)


def head_lanes(columns, width):
    rows = columns.shape[0]
    return jnp.concatenate(
        [jnp.broadcast_to(columns[:, h : h + 1], (rows, width)) for h in range(GROUPS)], axis=1
    )


def local_scan_kernel(
    inner_ref, halo_ref, taps_ref, states_ref, step_ref, decay_ref, skip_ref,
    local_ref, message_ref, reach_ref, padded,
):
    length = inner_ref.shape[0]
    margin = TAPS - 1
    padded[TAIL_ROWS - margin : TAIL_ROWS, :] = halo_ref[...].astype(jnp.float32)
    padded[TAIL_ROWS:, :] = inner_ref[...].astype(jnp.float32)
    conv = jnp.zeros(inner_ref.shape, jnp.float32)
    for tap in range(TAPS):
        start = TAIL_ROWS - margin + tap
        conv = conv + taps_ref[tap : tap + 1, :] * padded[start : start + length, :]
    mixed = (conv / (1.0 + jnp.exp(-conv))).astype(jnp.bfloat16)
    rows = lax.broadcasted_iota(jnp.int32, (length, length), 0)
    cols = lax.broadcasted_iota(jnp.int32, (length, length), 1)
    lower_mask = rows >= cols
    blank = jnp.zeros((128 - GROUPS, length), jnp.float32)
    step_rows = step_ref[...]
    reach_rows = jnp.dot(
        jnp.concatenate((decay_ref[...], blank), axis=0),
        (rows <= cols).astype(jnp.float32),
        precision=highest,
        preferred_element_type=jnp.float32,
    )
    reach = reach_rows.T
    step = jnp.concatenate((step_rows, blank), axis=0).T
    reach_ref[...] = reach
    final = reach[length - 1 :, :]
    tail = jnp.exp(final - reach) * step
    mixed_wide = mixed.astype(jnp.float32)
    scaled = mixed_wide * head_lanes(tail, HEAD_DIM)
    outs = []
    ends = []
    for g in range(GROUPS):
        low = g * HEAD_DIM
        in_states = states_ref[2 * g * STATE : (2 * g + 1) * STATE, :]
        out_states = states_ref[(2 * g + 1) * STATE : (2 * g + 2) * STATE, :]
        scores = lax.dot_general(
            out_states, in_states, (((0,), (0,)), ((), ())), preferred_element_type=jnp.float32
        )
        spread = jnp.where(lower_mask, reach[:, g : g + 1] - reach_rows[g : g + 1, :], 0.0)
        decay_table = jnp.where(lower_mask, jnp.exp(spread), 0.0)
        weights = scores * decay_table * step_rows[g : g + 1, :]
        outs.append(split_dot(mixed[:, low : low + HEAD_DIM], weights, ((1,), (0,)), False))
        ends.append(split_dot(in_states, scaled[:, low : low + HEAD_DIM], ((1,), (0,)), True))
    local_ref[...] = jnp.concatenate(outs, axis=1) + skip_ref[...] * mixed_wide
    message_ref[0, :STATE, :] = jnp.concatenate(ends, axis=1).astype(jnp.bfloat16)
    total = head_lanes(final, HEAD_DIM)
    upper = total.astype(jnp.bfloat16)
    lower = (total - upper.astype(jnp.float32)).astype(jnp.bfloat16)
    zeros = jnp.zeros((TAIL_ROWS - 1, total.shape[1]), jnp.bfloat16)
    message_ref[0, STATE : STATE + TAIL_ROWS, :] = jnp.concatenate((upper, zeros), axis=0)
    message_ref[0, STATE + TAIL_ROWS :, :] = jnp.concatenate((lower, zeros), axis=0)


def carry_kernel(
    position_ref, messages_ref, states_ref, reach_ref, local_ref, gate_ref, gated_ref, squares_ref
):
    position = position_ref[0]
    width = local_ref.shape[1]
    carry = jnp.zeros((STATE, width), jnp.float32)
    for k in range(messages_ref.shape[0] - 1):
        total = messages_ref[k, STATE : STATE + TAIL_ROWS, :].astype(jnp.float32)
        total = total + messages_ref[k, STATE + TAIL_ROWS :, :].astype(jnp.float32)
        moved = jnp.exp(total[:1, :]) * carry + messages_ref[k, :STATE, :].astype(jnp.float32)
        carry = jnp.where(k < position, moved, carry)
    outs = []
    for g in range(GROUPS):
        low = g * HEAD_DIM
        out_states = states_ref[(2 * g + 1) * STATE : (2 * g + 2) * STATE, :]
        outs.append(split_dot(out_states, carry[:, low : low + HEAD_DIM], ((0,), (0,)), True))
    carried = jnp.concatenate(outs, axis=1) * head_lanes(jnp.exp(reach_ref[...]), HEAD_DIM)
    gate = gate_ref[...].astype(jnp.float32)
    gated = (local_ref[...] + carried) * (gate / (1.0 + jnp.exp(-gate)))
    gated_ref[...] = gated
    owner = lax.broadcasted_iota(jnp.int32, (TAIL_ROWS, width), 1) // HEAD_DIM
    heads = lax.broadcasted_iota(jnp.int32, (TAIL_ROWS, width), 0)
    sums = lax.dot_general(
        (owner == heads).astype(jnp.float32),
        gated * gated,
        (((1,), (1,)), ((), ())),
        precision=highest,
        preferred_element_type=jnp.float32,
    )
    squares_ref[0] = sums[:GROUPS, :]


def in_vmem(count):
    return [pl.BlockSpec(memory_space=pltpu.VMEM)] * count


def local_scan(inner, halo, taps, states, step, decay, skip, interpret=False):
    length, width = inner.shape
    return pl.pallas_call(
        local_scan_kernel,
        out_shape=(
            jax.ShapeDtypeStruct((length, width), jnp.float32),
            jax.ShapeDtypeStruct((1, STATE + 2 * TAIL_ROWS, width), jnp.bfloat16),
            jax.ShapeDtypeStruct((length, 128), jnp.float32),
        ),
        in_specs=in_vmem(7),
        out_specs=tuple(in_vmem(3)),
        scratch_shapes=[pltpu.VMEM((length + TAIL_ROWS, width), jnp.float32)],
        interpret=interpret,
        name="local_scan",
    )(inner, halo, taps, states, step, decay, skip)


def carry_in(position, messages, states, reach, local, gate, interpret=False):
    length, width = local.shape
    return pl.pallas_call(
        carry_kernel,
        out_shape=(
            jax.ShapeDtypeStruct((length, width), jnp.float32),
            jax.ShapeDtypeStruct((1, GROUPS, length), jnp.float32),
        ),
        in_specs=[pl.BlockSpec(memory_space=pltpu.SMEM)] + in_vmem(5),
        out_specs=tuple(in_vmem(2)),
        interpret=interpret,
        name="carry_in",
    )(position, messages, states, reach, local, gate)


def body(
    tokens,
    pre_gain,
    proj_inner,
    proj_gate,
    proj_states,
    proj_step,
    step_bias,
    log_rate,
    conv_inner,
    conv_states,
    skip_gain,
    norm_gain,
    proj_output,
):
    tokens_wide = tokens.astype(jnp.float32)
    normed = (
        tokens_wide
        * lax.rsqrt(jnp.mean(tokens_wide * tokens_wide, axis=1, keepdims=True) + epsilon)
        * pre_gain
    ).astype(jnp.bfloat16)
    inner_width = proj_inner.shape[1]
    state_width = proj_states.shape[1]
    row_piece = lax.all_gather(normed, "tp", axis=0, tiled=True)
    row_count = row_piece.shape[0]
    margin = TAPS - 1

    def project(weight):
        return jnp.dot(row_piece, weight, preferred_element_type=jnp.float32)

    def project_across(weight):
        return lax.dot_general(
            weight, row_piece, (((0,), (1,)), ((), ())), preferred_element_type=jnp.float32
        )

    state_proj = project_across(proj_states).astype(jnp.bfloat16)
    inner_proj = project(proj_inner).astype(jnp.bfloat16)
    gate_proj = project(proj_gate).astype(jnp.bfloat16)
    step_size = jax.nn.softplus(project_across(proj_step) + step_bias[:, None])
    log_decay = -jnp.exp(log_rate)[:, None] * step_size
    before = from_behind(
        jnp.concatenate((inner_proj[row_count - margin :], state_proj[:, row_count - margin :].T), axis=1),
        "seq",
        1,
    )
    before_inner, before_states = before[:, :inner_width], before[:, inner_width:].T
    padded = jnp.concatenate((before_states, state_proj), axis=1).astype(jnp.float32)
    mixed_local = jnp.zeros(state_proj.shape, jnp.float32)
    for tap in range(TAPS):
        mixed_local = mixed_local + conv_states[tap][:, None] * padded[:, tap : tap + row_count]
    mixed_local = jax.nn.silu(mixed_local).astype(jnp.bfloat16)
    mixed_all = lax.all_gather(mixed_local[None], "tp", axis=0, tiled=True)
    mixed_all = mixed_all.reshape(-1, row_count)
    skip_row = jnp.repeat(skip_gain, HEAD_DIM)[None]
    local, message, reach = local_scan(
        inner_proj, before_inner, conv_inner, mixed_all, step_size, log_decay, skip_row
    )
    messages = lax.all_gather(message, "seq", axis=0, tiled=True)
    position = lax.axis_index("seq").astype(jnp.int32).reshape(1)
    gated_out, head_squares = carry_in(position, messages, mixed_all, reach, local, gate_proj)
    every_square = lax.all_gather(head_squares, "tp", axis=0, tiled=True)
    mean_square = jnp.sum(every_square, axis=0) / (GROUP_HEADS * HEAD_DIM)
    scale = jnp.repeat(lax.rsqrt(mean_square + epsilon).T, HEAD_DIM, axis=1)
    mixed_out = (gated_out * scale * norm_gain).astype(jnp.bfloat16)
    summed = lax.psum_scatter(
        jnp.dot(mixed_out, proj_output, preferred_element_type=jnp.float32).astype(jnp.bfloat16),
        "tp",
        scatter_dimension=0,
        tiled=True,
    ).astype(jnp.float32)
    return (tokens_wide + summed).astype(jnp.bfloat16)


def solution(mesh):
    placed = (
        P(("dp", "seq", "tp"), None),
        P(),
        P(None, "tp"),
        P(None, "tp"),
        P(None, "tp"),
        P(None, "tp"),
        P("tp"),
        P("tp"),
        P(None, "tp"),
        P(None, "tp"),
        P("tp"),
        P("tp"),
        P("tp", None),
    )
    return jax.shard_map(
        body, mesh=mesh, in_specs=placed, out_specs=P(("dp", "seq", "tp"), None), check_vma=False
    )
```

time: 281 us -> 274 us (0.975)
  blocking collectives: 39 us -> 76.1 us
  local copies, waits for them, and re-layouts: 28 us -> 4 us
  starting transfers between devices: 12.9 us -> 1.34 us
  matrix products: 17.9 us -> 10.9 us
  Pallas kernels: 0 us -> 6.45 us
  other arithmetic: 9.43 us -> 5.43 us
  waiting for transfers between devices: 159 us -> 155 us
    all_gather x1 -> x3, blocking collectives: 19.3 us -> 76.1 us  [the longest x1 33.7 us: body(): mixed_all = lax.all_gather(mixed_local[None], 'tp', axis=0, tiled=True)]
    all_to_all x1 -> x0, blocking collectives: 19.7 us -> none  [from_everyone(): return lax.all_to_all(copies, axis, split_axis=0, concat_axis=0, tiled=True)]
    dynamic_update_slice x2 -> x0, local copies, waits for them, and re-layouts: 8.37 us -> none  [scan_blocks(): lax.scan(partial(block_step, copies=copies), carry_state, (split_blocks(v...]
    dot_general x14 -> x4, matrix products: 15.8 us -> 7.94 us  [the longest x2 4.09 us: project(): return jnp.dot(row_piece, weight, preferred_element_type=jnp.float32)]
    all_to_all x1 -> x0, starting transfers between devices: 7.72 us -> none  [from_everyone(): return lax.all_to_all(copies, axis, split_axis=0, concat_axis=0, tiled=True)]
    all_to_all x1 -> x0, waiting for transfers between devices: 6.53 us -> none  [from_everyone(): return lax.all_to_all(copies, axis, split_axis=0, concat_axis=0, tiled=True)]
    pallas_call x0 -> x2, Pallas kernels: none -> 6.45 us  [the longest x1 3.61 us: local_scan(): pl.pallas_call(local_scan_kernel, out_shape=(jax.ShapeDtypeStruct((length...]
    reduce_scatter x1, waiting for transfers between devices: 68.2 us -> 73.4 us  [body(): lax.psum_scatter(jnp.dot(mixed_out, proj_output, preferred_element_type=j...]
  transfers between devices with their start and end apart: 5 -> 3, of which waited for: 4 -> 2; matrix products, arithmetic and copies ran while one was open for 6% -> 2% of each run, Pallas kernels for 0% -> 0%
where the time goes in v2:
time: 274 us; the launch traced here: 273 us
  waiting for transfers between devices  155 us (57%)
  blocking collectives  76.1 us (28%)
  between operations  13.5 us (5%)
  matrix products  10.9 us (4%)
  Pallas kernels  6.45 us (2%)
  other arithmetic  5.43 us (2%)
  local copies, waits for them, and re-layouts  4 us (1%)
    all_gather x1, waiting for transfers between devices, body(): row_piece = lax.all_gather(normed, 'tp', axis=0, tiled=True)  81.5 us
    reduce_scatter x1, waiting for transfers between devices, body(): lax.psum_scatter(jnp.dot(mixed_out, proj_output, preferred_element_type=j...  73.4 us
    all_gather x1, blocking collectives, body(): mixed_all = lax.all_gather(mixed_local[None], 'tp', axis=0, tiled=True)  33.7 us
    all_gather x1, blocking collectives, body(): every_square = lax.all_gather(head_squares, 'tp', axis=0, tiled=True)  26.6 us
    all_gather x1, blocking collectives, body(): messages = lax.all_gather(message, 'seq', axis=0, tiled=True)  15.9 us
  transfers between devices with their start and end apart: 3, of which 2 were waited for; matrix products, arithmetic and copies ran while one was open for 2% of the time, Pallas kernels for 0%

profile of v2, /device:TPU:56, one launch (start us, length us, event | category | flops | bytes accessed | tf_op | source)
XLA Modules:
  0.0 272.8 jit_solution(15155274540277429367)
XLA Ops:
  6.5 0.0 copy-start
  6.5 0.0 all-gather.3.cloned.1.call-start
  6.5 1.2 fusion.2
  7.7 1.7 fusion.4
  9.4 0.0 all-gather.3.cloned.1.call-update
  9.4 0.0 reduce-scatter.2.cloned.1.call-start
  9.5 0.7 broadcast_in_dim.7
  10.2 0.6 broadcast_in_dim_reshape.3.skip_ref
  10.9 0.7 exponential_negate_fusion
  11.5 0.8 slice_bitcast_fusion.5
  12.4 81.5 %all-gather.3.cloned.1.call-done = bf16[256,4096]{1,0:T(8,128)(2,1)} async-done(((bf16[16,4096]{1,0:T(8,128)(2,1)}), bf16[256,4096]{1,0:T(8,128)(2,1)}) %all-gather.3.cloned.1.call-update) | async-done | bytes 2097168 | tf_op jit(solution)/shard_map/all_gather | solution.py:190
  93.9 0.0 copy-start.1
  93.9 2.6 fusion
  96.5 0.1 slice_bitcast_fusion.1
  96.5 0.0 copy-done.1
  96.5 0.0 copy-start.6
  96.6 2.7 %convolution_convert_fusion.2 = bf16[256,256]{0,1:T(8,128)(2,1)S(1)} fusion(bf16[256,4096]{1,0:T(8,128)(2,1)S(1)} %copy-done.1, bf16[4096,256]{1,0:T(8,128)(2,1)} %param.15), kind=kOutput, calls=%fused_computation.2 | convolution fusion | flops 536936448 | bytes 4325376 | tf_op jit(solution)/shard_map/dot_general | solution.py:195
  99.3 0.1 slice.48
  99.4 0.0 copy-start.3
  99.4 0.0 copy-start.5
  99.4 1.3 collective-permute-start
  100.7 0.0 copy-done.6
  100.8 1.4 convolution_convert_fusion.1.gate_ref
  102.1 0.0 copy-done.3
  102.1 0.0 copy-done.5
  102.1 1.3 broadcast_multiply_fusion
  103.4 0.8 copy.26.inner_ref
  104.1 0.0 collective-permute-done
  104.2 0.7 copy.27.halo_ref
  104.8 0.1 maximum_convert_fusion
  104.9 0.2 multiply_convert_fusion.2
  105.1 33.7 %all-gather.states_ref = bf16[1024,256]{1,0:T(8,128)(2,1)} all-gather(bf16[64,256]{1,0:T(8,128)(2,1)S(1)} %multiply_convert_fusion.2), channel_id=2, replica_groups=mesh['dp'=8,'seq'=8,'tp'=16] {'tp'}, dimensions={0}, use_global_device_ids=true | all-gather | bytes 557056 | tf_op jit(solution)/shard_map/all_gather | solution.py:218
  138.8 0.0 copy-start.4
  138.8 3.6 %local_scan.1 = (f32[256,256]{1,0:T(8,128)}, bf16[1,144,256]{2,1,0:T(8,128)(2,1)}, f32[256,128]{1,0:T(8,128)}) custom-call(bf16[256,256]{1,0:T(8,128)(2,1)} %copy.26.inner_ref, bf16[3,256]{1,0:T(4,128)(2,1)} %copy.27.halo_ref, f32[4,256]{1,0:T(4,128)} %taps_ref.1, bf16[1024,256]{1,0:T(8,128)(2,1)} %all-gather.states_ref, ...), custom_call_target="tpu_custom_call" | custom-call | tf_op jit(solution)/shard_map/local_scan/pallas_call | solution.py:137
  142.4 15.9 %all_gather.14.messages_ref = bf16[8,144,256]{2,1,0:T(8,128)(2,1)} all-gather(bf16[1,144,256]{2,1,0:T(8,128)(2,1)} %get-tuple-element.10), channel_id=1, replica_groups=mesh['dp'=8,'seq'=8,'tp'=16] {'seq'}, dimensions={0}, use_global_device_ids=true | all-gather | bytes 663552 | tf_op jit(solution)/shard_map/all_gather | solution.py:224
  158.3 2.8 %carry_in.1 = (f32[256,256]{1,0:T(8,128)}, f32[1,4,256]{2,1,0:T(4,128)}) custom-call(s32[1]{0:T(128)} %bitcast.position_ref, bf16[8,144,256]{2,1,0:T(8,128)(2,1)} %all_gather.14.messages_ref, bf16[1024,256]{1,0:T(8,128)(2,1)} %all-gather.states_ref, f32[256,128]{1,0:T(8,128)} %get-tuple-element.11.reach_ref, f32[256,256]{1,0:T(8,128)} %get-tuple-element.12.local_ref, ...), custom_call_target="tpu_custom_call" | custom-call | tf_op jit(solution)/shard_map/carry_in/pallas_call | solution.py:154
  161.1 26.6 %all_gather.15 = f32[16,4,256]{2,1,0:T(4,128)S(1)} all-gather(f32[1,4,256]{2,1,0:T(4,128)} %get-tuple-element.14), channel_id=1, replica_groups=mesh['dp'=8,'seq'=8,'tp'=16] {'tp'}, dimensions={0}, use_global_device_ids=true | all-gather | bytes 69632 | tf_op jit(solution)/shard_map/all_gather | solution.py:227
  187.7 0.1 copy.28
  187.9 0.0 copy-done
  187.9 0.0 copy-done.4
  187.9 3.0 %convolution_convert_fusion = bf16[256,4096]{1,0:T(8,128)(2,1)} fusion(bf16[256,4096]{1,0:T(8,128)(2,1)S(1)} %copy-done, f32[256,256]{1,0:T(8,128)} %get-tuple-element.13, f32[256,256]{1,0:T(8,128)S(1)} %copy.28, f32[256]{0:T(256)S(1)} %copy-done.4), kind=kOutput, calls=%fused_computation | convolution fusion | flops 538116096 | bytes 4719616 | tf_op jit(solution)/shard_map/dot_general | solution.py:232
  190.9 0.0 copy-start.2
  190.9 0.0 reduce-scatter.2.cloned.1.call-update
  190.9 73.4 %reduce-scatter.2.cloned.1.call-done = bf16[16,4096]{1,0:T(8,128)(2,1)} async-done(((bf16[256,4096]{1,0:T(8,128)(2,1)}), bf16[16,4096]{1,0:T(8,128)(2,1)}) %reduce-scatter.2.cloned.1.call-update) | async-done | bytes 131088 | tf_op jit(solution)/shard_map/reduce_scatter | solution.py:231
  264.4 0.0 copy-done.2
  264.4 1.6 fusion.5
  (7 shorter events, 0.1 us)
Async XLA Ops:
  6.5 181.3 %copy-start = (bf16[256,4096]{1,0:T(8,128)(2,1)S(1)}, bf16[256,4096]{1,0:T(8,128)(2,1)}, u32[]{:S(2)}) copy-start(bf16[256,4096]{1,0:T(8,128)(2,1)} %param.25) | copy-start | bytes 6291460
  6.5 87.3 %all-gather.3.cloned.1.call-start = ((), (), s32[]{:S(2)}) async-start(), calls=%async_computation.1 | async-start | bytes 2228224 | tf_op jit(solution)/shard_map/all_gather | solution.py:190
  9.4 254.9 %reduce-scatter.2.cloned.1.call-start = ((), (), s32[]{:S(2)}) async-start(), calls=%async_computation.2 | async-start | bytes 2228224 | tf_op jit(solution)/shard_map/reduce_scatter | solution.py:231
  93.9 2.7 copy-start.1
  96.5 4.2 %copy-start.6 = (bf16[4096,256]{1,0:T(8,128)(2,1)S(1)}, bf16[4096,256]{1,0:T(8,128)(2,1)}, u32[]{:S(2)}) copy-start(bf16[4096,256]{1,0:T(8,128)(2,1)} %param.16) | copy-start | bytes 6291460
  99.4 2.7 copy-start.3
  99.4 2.7 copy-start.5
  99.4 4.7 %collective-permute-start = (bf16[3,320]{0,1:T(8,128)(2,1)S(1)}, bf16[3,320]{0,1:T(8,128)(2,1)S(1)}, u32[]{:S(2)}, u32[]{:S(2)}) collective-permute-start(bf16[3,320]{0,1:T(8,128)(2,1)S(1)} %pad_maximum_fusion), channel_id=1, source_target_pairs={{0,16},{16,32},{32,48},{48,64},{64,80},{80,96},{96,112},{1,17},{17... | collective-permute-start | bytes 5768 | tf_op jit(solution)/shard_map/ppermute | solution.py:23
  138.8 49.1 %copy-start.4 = (f32[256]{0:T(256)S(1)}, f32[256]{0:T(256)}, u32[]{:S(2)}) copy-start(f32[256]{0:T(256)} %param.24) | copy-start | bytes 3076
  190.9 73.5 %copy-start.2 = (bf16[16,4096]{1,0:T(8,128)(2,1)S(1)}, bf16[16,4096]{1,0:T(8,128)(2,1)}, u32[]{:S(2)}) copy-start(bf16[16,4096]{1,0:T(8,128)(2,1)} %param.13) | copy-start | bytes 393220
Sparse Core Ops, SparseCore 0:
  10.0 83.8 all-gather.2
  191.1 73.2 reduce-scatter.1

commit v3 on v2

--- a/solution.py
+++ b/solution.py
@@ -21,6 +21,11 @@
     count = lax.axis_size(axis)
     initial, last = (max(0, -steps), min(count, count - steps))
     return lax.ppermute(value, axis, [(source, source + steps) for source in range(initial, last)])
+
+
+def from_everyone(x, axis):
+    copies = jnp.broadcast_to(x, (lax.axis_size(axis), *x.shape))
+    return lax.all_to_all(copies, axis, split_axis=0, concat_axis=0, tiled=True)
 
 
 def split_dot(exact, wide, dims, exact_first):
@@ -185,38 +190,39 @@
         * lax.rsqrt(jnp.mean(tokens_wide * tokens_wide, axis=1, keepdims=True) + epsilon)
         * pre_gain
     ).astype(jnp.bfloat16)
-    inner_width = proj_inner.shape[1]
-    state_width = proj_states.shape[1]
-    row_piece = lax.all_gather(normed, "tp", axis=0, tiled=True)
-    row_count = row_piece.shape[0]
+    count = lax.axis_size("tp")
+    own_rows, features = tokens.shape
+    row_count = count * own_rows
+    fit = (2**20 // (2 * row_count) - 1) // 128 * 128
+    cut = features - fit
+    first_rows = lax.all_gather(normed[:, :cut], "tp", axis=0, tiled=True)
+    last_rows = lax.all_gather(normed[:, cut:], "tp", axis=0, tiled=True)
     margin = TAPS - 1
 
     def project(weight):
-        return jnp.dot(row_piece, weight, preferred_element_type=jnp.float32)
+        late = jnp.dot(last_rows, weight[cut:], preferred_element_type=jnp.float32)
+        return late + jnp.dot(first_rows, weight[:cut], preferred_element_type=jnp.float32)
 
     def project_across(weight):
-        return lax.dot_general(
-            weight, row_piece, (((0,), (1,)), ((), ())), preferred_element_type=jnp.float32
+        dims = (((0,), (1,)), ((), ()))
+        late = lax.dot_general(weight[cut:], last_rows, dims, preferred_element_type=jnp.float32)
+        return late + lax.dot_general(
+            weight[:cut], first_rows, dims, preferred_element_type=jnp.float32
         )
 
     state_proj = project_across(proj_states).astype(jnp.bfloat16)
+    before_states = from_behind(state_proj[:, row_count - margin :], "seq", 1)
     inner_proj = project(proj_inner).astype(jnp.bfloat16)
     gate_proj = project(proj_gate).astype(jnp.bfloat16)
     step_size = jax.nn.softplus(project_across(proj_step) + step_bias[:, None])
     log_decay = -jnp.exp(log_rate)[:, None] * step_size
-    before = from_behind(
-        jnp.concatenate((inner_proj[row_count - margin :], state_proj[:, row_count - margin :].T), axis=1),
-        "seq",
-        1,
-    )
-    before_inner, before_states = before[:, :inner_width], before[:, inner_width:].T
+    before_inner = from_behind(inner_proj[row_count - margin :], "seq", 1)
     padded = jnp.concatenate((before_states, state_proj), axis=1).astype(jnp.float32)
     mixed_local = jnp.zeros(state_proj.shape, jnp.float32)
     for tap in range(TAPS):
         mixed_local = mixed_local + conv_states[tap][:, None] * padded[:, tap : tap + row_count]
     mixed_local = jax.nn.silu(mixed_local).astype(jnp.bfloat16)
-    mixed_all = lax.all_gather(mixed_local[None], "tp", axis=0, tiled=True)
-    mixed_all = mixed_all.reshape(-1, row_count)
+    mixed_all = from_everyone(mixed_local, "tp").reshape(-1, row_count)
     skip_row = jnp.repeat(skip_gain, HEAD_DIM)[None]
     local, message, reach = local_scan(
         inner_proj, before_inner, conv_inner, mixed_all, step_size, log_decay, skip_row
@@ -224,7 +230,7 @@
     messages = lax.all_gather(message, "seq", axis=0, tiled=True)
     position = lax.axis_index("seq").astype(jnp.int32).reshape(1)
     gated_out, head_squares = carry_in(position, messages, mixed_all, reach, local, gate_proj)
-    every_square = lax.all_gather(head_squares, "tp", axis=0, tiled=True)
+    every_square = from_everyone(head_squares[0], "tp")
     mean_square = jnp.sum(every_square, axis=0) / (GROUP_HEADS * HEAD_DIM)
     scale = jnp.repeat(lax.rsqrt(mean_square + epsilon).T, HEAD_DIM, axis=1)
     mixed_out = (gated_out * scale * norm_gain).astype(jnp.bfloat16)

time: 274 us -> 259 us (0.945)
  waiting for transfers between devices: 155 us -> 114 us
  blocking collectives: 76.1 us -> 88.8 us
  starting transfers between devices: 1.34 us -> 13.2 us
    all_gather x1, waiting for transfers between devices: 81.5 us -> 31.4 us  [body(): first_rows = lax.all_gather(normed[:, :cut], 'tp', axis=0, tiled=True)]
    all_to_all x0 -> x1, blocking collectives: none -> 20.3 us  [from_everyone(): return lax.all_to_all(copies, axis, split_axis=0, concat_axis=0, tiled=True)]
    all_to_all x0 -> x1, waiting for transfers between devices: none -> 13.4 us  [from_everyone(): return lax.all_to_all(copies, axis, split_axis=0, concat_axis=0, tiled=True)]
    all_gather x2 -> x1, blocking collectives: 60.3 us -> 48.8 us  [body(): last_rows = lax.all_gather(normed[:, cut:], 'tp', axis=0, tiled=True)]
    all_to_all x0 -> x1, starting transfers between devices: none -> 7.88 us  [from_everyone(): return lax.all_to_all(copies, axis, split_axis=0, concat_axis=0, tiled=True)]
    reduce_scatter x1, waiting for transfers between devices: 73.4 us -> 68.3 us  [body(): lax.psum_scatter(jnp.dot(mixed_out, proj_output, preferred_element_type=j...]
    ppermute x1 -> x2, starting transfers between devices: 1.29 us -> 5.26 us  [from_behind(): lax.ppermute(value, axis, [(source, source + steps) for source in range(i...]
    all_gather x1, blocking collectives: 15.9 us -> 19.8 us  [body(): messages = lax.all_gather(message, 'seq', axis=0, tiled=True)]
  transfers between devices with their start and end apart: 3 -> 5, of which waited for: 2 -> 4; matrix products, arithmetic and copies ran while one was open for 2% -> 3% of each run, Pallas kernels for 0% -> 0%
where the time goes in v3:
time: 259 us; the launch traced here: 258 us
  waiting for transfers between devices  114 us (44%)
  blocking collectives  88.8 us (34%)
  between operations  13.7 us (5%)
  starting transfers between devices  13.2 us (5%)
  matrix products  12.8 us (5%)
  Pallas kernels  6.48 us (3%)
  local copies, waits for them, and re-layouts  4.92 us (2%)
  other arithmetic  4.1 us (2%)
    reduce_scatter x1, waiting for transfers between devices, body(): lax.psum_scatter(jnp.dot(mixed_out, proj_output, preferred_element_type=j...  68.3 us
    all_gather x1, blocking collectives, body(): last_rows = lax.all_gather(normed[:, cut:], 'tp', axis=0, tiled=True)  48.8 us
    all_gather x1, waiting for transfers between devices, body(): first_rows = lax.all_gather(normed[:, :cut], 'tp', axis=0, tiled=True)  31.4 us
    all_to_all x1, blocking collectives, from_everyone(): return lax.all_to_all(copies, axis, split_axis=0, concat_axis=0, tiled=True)  20.3 us
    all_gather x1, blocking collectives, body(): messages = lax.all_gather(message, 'seq', axis=0, tiled=True)  19.8 us
    all_to_all x1, waiting for transfers between devices, from_everyone(): return lax.all_to_all(copies, axis, split_axis=0, concat_axis=0, tiled=True)  13.4 us
    all_to_all x1, starting transfers between devices, from_everyone(): return lax.all_to_all(copies, axis, split_axis=0, concat_axis=0, tiled=True)  7.88 us
    ppermute x2, starting transfers between devices, from_behind(): lax.ppermute(value, axis, [(source, source + steps) for source in range(i...  5.26 us
  transfers between devices with their start and end apart: 5, of which 4 were waited for; matrix products, arithmetic and copies ran while one was open for 3% of the time, Pallas kernels for 0%

profile of v3, /device:TPU:56, one launch (start us, length us, event | category | flops | bytes accessed | tf_op | source)
XLA Modules:
  0.0 258.0 jit_solution(5214550596416488808)
XLA Ops:
  6.5 0.0 copy-start
  6.5 0.0 all-gather.2.cloned.1.call-start
  6.5 1.2 fusion.13
  7.8 1.0 fusion.15
  8.8 0.0 copy-start.11
  8.8 0.6 slice.81
  9.4 0.0 all-gather.2.cloned.1.call-update
  9.5 48.8 %all_gather.9 = bf16[256,1920]{1,0:T(8,128)(2,1)S(1)} all-gather(bf16[16,1920]{1,0:T(8,128)(2,1)S(1)} %slice.80), channel_id=1, replica_groups=mesh['dp'=8,'seq'=8,'tp'=16] {'tp'}, dimensions={0}, use_global_device_ids=true | all-gather | bytes 1044480 | tf_op jit(solution)/shard_map/all_gather | solution.py:199
  58.3 0.9 copy-done.3
  59.2 1.4 fusion.17
  60.6 0.0 copy-start.12
  60.6 0.0 copy-start.15
  60.6 31.4 %all-gather.2.cloned.1.call-done = bf16[256,2176]{1,0:T(8,128)(2,1)} async-done(((bf16[16,2176]{1,0:T(8,128)(2,1)}), bf16[256,2176]{1,0:T(8,128)(2,1)}) %all-gather.2.cloned.1.call-update) | async-done | bytes 1114128 | tf_op jit(solution)/shard_map/all_gather | solution.py:198
  92.0 0.0 copy-done.6
  92.0 1.7 fusion.5
  93.7 0.1 slice.83
  93.8 1.3 collective-permute-start.1
  95.1 0.0 copy-done.11
  95.1 0.8 collective-permute-done.1
  95.9 0.1 maximum_convert_fusion
  96.0 0.2 multiply_convert_fusion.2
  96.2 0.8 broadcast_in_dim.8
  97.0 7.9 %all-to-all-start = ((bf16[16,64,256]{2,1,0:T(8,128)(2,1)}), bf16[16,64,256]{2,1,0:T(8,128)(2,1)S(1)}, u32[]{:S(2)}, u32[]{:S(2)}) async-start(bf16[16,64,256]{2,1,0:T(8,128)(2,1)} %broadcast_in_dim.8), calls=%async_computation | async-start | bytes 1048576 | tf_op jit(solution)/shard_map/all_to_all | solution.py:28
  104.9 0.0 reduce-scatter.2.cloned.1.call-start
  105.0 0.0 copy-done.12
  105.0 0.1 broadcast_in_dim.18
  105.1 0.6 broadcast_in_dim_reshape.3.skip_ref
  105.7 0.0 copy-done.15
  105.7 0.0 copy-start.2
  105.7 0.0 copy-start.13
  105.7 2.1 fusion.8
  107.8 0.0 copy-done.4
  107.8 0.0 copy-start.8
  107.8 1.6 fusion.10
  109.5 0.0 copy-done.2
  109.5 0.0 copy-done.13
  109.5 0.0 copy-start.14
  109.5 0.5 fusion.inner_ref
  110.0 0.0 copy-start.7
  110.0 0.0 copy-start.16
  110.0 4.0 %collective-permute-start = (bf16[3,256]{1,0:T(4,128)(2,1)S(1)}, bf16[3,256]{1,0:T(4,128)(2,1)S(1)}, u32[]{:S(2)}, u32[]{:S(2)}) collective-permute-start(bf16[3,256]{1,0:T(4,128)(2,1)S(1)} %slice.82), channel_id=1, source_target_pairs={{0,16},{16,32},{32,48},{48,64},{64,80},{80,96},{96,112},{1,17},{17... | collective-permute-start | bytes 4616 | tf_op jit(solution)/shard_map/ppermute | solution.py:23
  114.0 0.0 copy-done.8
  114.0 0.4 fusion.23
  114.4 0.0 copy-done.14
  114.4 1.2 fusion.1.gate_ref
  115.6 0.0 copy-done.16
  115.6 1.0 broadcast_multiply_fusion
  116.6 0.0 copy-done.7
  116.6 0.0 collective-permute-done.halo_ref
  116.6 0.0 copy-start.10
  116.6 13.4 %all-to-all-done = bf16[16,64,256]{2,1,0:T(8,128)(2,1)S(1)} async-done(((bf16[16,64,256]{2,1,0:T(8,128)(2,1)}), bf16[16,64,256]{2,1,0:T(8,128)(2,1)S(1)}, u32[]{:S(2)}, u32[]{:S(2)}) %all-to-all-start) | async-done | bytes 524320 | tf_op jit(solution)/shard_map/all_to_all | solution.py:28
  130.0 0.0 copy-done.10
  130.0 0.8 copy-done.1
  130.8 3.6 %local_scan.1 = (f32[256,256]{1,0:T(8,128)}, bf16[1,144,256]{2,1,0:T(8,128)(2,1)}, f32[256,128]{1,0:T(8,128)}) custom-call(bf16[256,256]{1,0:T(8,128)(2,1)} %copy-done.7, bf16[3,256]{1,0:T(4,128)(2,1)} %copy-done.10, f32[4,256]{1,0:T(4,128)} %taps_ref.1, bf16[1024,256]{1,0:T(8,128)(2,1)} %bitcast.29, f32[4,256]{1,0:T(4,128)} %get-tuple-element.20.step_ref, ...), custom_call_target="tpu_custom_call" | custom-call | tf_op jit(solution)/shard_map/local_scan/pallas_call | solution.py:142
  134.4 19.8 %all_gather.11.messages_ref = bf16[8,144,256]{2,1,0:T(8,128)(2,1)} all-gather(bf16[1,144,256]{2,1,0:T(8,128)(2,1)} %get-tuple-element.10), channel_id=1, replica_groups=mesh['dp'=8,'seq'=8,'tp'=16] {'seq'}, dimensions={0}, use_global_device_ids=true | all-gather | bytes 663552 | tf_op jit(solution)/shard_map/all_gather | solution.py:230
  154.2 2.8 %carry_in.1 = (f32[256,256]{1,0:T(8,128)}, f32[1,4,256]{2,1,0:T(4,128)}) custom-call(s32[1]{0:T(128)} %bitcast.position_ref, bf16[8,144,256]{2,1,0:T(8,128)(2,1)} %all_gather.11.messages_ref, bf16[1024,256]{1,0:T(8,128)(2,1)} %bitcast.30, f32[256,128]{1,0:T(8,128)} %get-tuple-element.11.reach_ref, f32[256,256]{1,0:T(8,128)} %get-tuple-element.12.local_ref, ...), custom_call_target="tpu_custom_call" | custom-call | tf_op jit(solution)/shard_map/carry_in/pallas_call | solution.py:159
  157.0 0.7 broadcast_in_dim.19
  157.7 20.3 %all_to_all.10 = f32[16,4,256]{2,1,0:T(4,128)S(1)} all-to-all(f32[16,4,256]{2,1,0:T(4,128)S(1)} %broadcast_in_dim.19), channel_id=1, replica_groups=mesh['dp'=8,'seq'=8,'tp'=16] {'tp'}, dimensions={0} | all-to-all | bytes 131072 | tf_op jit(solution)/shard_map/all_to_all | solution.py:28
  178.1 0.1 copy.18
  178.2 3.0 %convolution_convert_fusion = bf16[256,4096]{1,0:T(8,128)(2,1)} fusion(bf16[256,4096]{1,0:T(8,128)(2,1)S(1)} %copy-done, f32[256,256]{1,0:T(8,128)} %get-tuple-element.13, f32[256,256]{1,0:T(8,128)S(1)} %copy.18, f32[256]{0:T(256)S(1)} %copy-done.9), kind=kOutput, calls=%fused_computation | convolution fusion | flops 538116096 | bytes 4719616 | tf_op jit(solution)/shard_map/dot_general | solution.py:238
  181.2 0.0 reduce-scatter.2.cloned.1.call-update
  181.2 68.3 %reduce-scatter.2.cloned.1.call-done = bf16[16,4096]{1,0:T(8,128)(2,1)} async-done(((bf16[256,4096]{1,0:T(8,128)(2,1)}), bf16[16,4096]{1,0:T(8,128)(2,1)}) %reduce-scatter.2.cloned.1.call-update) | async-done | bytes 131088 | tf_op jit(solution)/shard_map/reduce_scatter | solution.py:237
  249.5 0.0 copy-done.5
  249.5 1.6 fusion.16
  (16 shorter events, 0.1 us)
Async XLA Ops:
  6.5 171.7 %copy-start = (bf16[256,4096]{1,0:T(8,128)(2,1)S(1)}, bf16[256,4096]{1,0:T(8,128)(2,1)}, u32[]{:S(2)}) copy-start(bf16[256,4096]{1,0:T(8,128)(2,1)} %param.25) | copy-start | bytes 6291460
  6.5 85.5 %copy-start.6 = (bf16[4096,64]{0,1:T(8,128)(2,1)S(1)}, bf16[4096,64]{0,1:T(8,128)(2,1)}, u32[]{:S(2)}) copy-start(bf16[4096,64]{0,1:T(8,128)(2,1)} %param.17) | copy-start | bytes 1572868
  6.5 85.5 %all-gather.2.cloned.1.call-start = ((), (), s32[]{:S(2)}) async-start(), calls=%async_computation.3 | async-start | bytes 1183744 | tf_op jit(solution)/shard_map/all_gather | solution.py:198
  8.8 86.3 %copy-start.11 = (f32[4,64]{1,0:T(4,128)S(1)}, f32[4,64]{1,0:T(4,128)}, u32[]{:S(2)}) copy-start(f32[4,64]{1,0:T(4,128)} %param.22) | copy-start | bytes 3076
  58.3 1.0 copy-start.3
  60.6 44.4 %copy-start.12 = (f32[4]{0:T(128)S(1)}, f32[4]{0:T(128)}, u32[]{:S(2)}) copy-start(f32[4]{0:T(128)} %param.23) | copy-start | bytes 52
  60.6 45.1 %copy-start.15 = (f32[4]{0:T(128)S(1)}, f32[4]{0:T(128)}, u32[]{:S(2)}) copy-start(f32[4]{0:T(128)} %param.20) | copy-start | bytes 52
  93.8 2.1 collective-permute-start.1
  97.0 32.9 %all-to-all-start = ((bf16[16,64,256]{2,1,0:T(8,128)(2,1)}), bf16[16,64,256]{2,1,0:T(8,128)(2,1)S(1)}, u32[]{:S(2)}, u32[]{:S(2)}) async-start(bf16[16,64,256]{2,1,0:T(8,128)(2,1)} %broadcast_in_dim.8), calls=%async_computation | async-start | bytes 1048576 | tf_op jit(solution)/shard_map/all_to_all | solution.py:28
  104.9 144.6 %reduce-scatter.2.cloned.1.call-start = ((), (), s32[]{:S(2)}) async-start(), calls=%async_computation.4 | async-start | bytes 2228224 | tf_op jit(solution)/shard_map/reduce_scatter | solution.py:237
  105.7 2.1 copy-start.4
  105.7 3.8 %copy-start.2 = (bf16[256,2176]{1,0:T(8,128)(2,1)S(1)}, bf16[256,2176]{1,0:T(8,128)(2,1)}, u32[]{:S(2)}) copy-start(bf16[256,2176]{1,0:T(8,128)(2,1)} %all-gather.2.cloned.1.call-done) | copy-start | bytes 3342340
  105.7 3.8 %copy-start.13 = (bf16[4096,256]{1,0:T(8,128)(2,1)S(1)}, bf16[4096,256]{1,0:T(8,128)(2,1)}, u32[]{:S(2)}) copy-start(bf16[4096,256]{1,0:T(8,128)(2,1)} %param.15) | copy-start | bytes 6291460
  107.8 6.2 %copy-start.8 = (bf16[4096,4]{0,1:T(4,128)(2,1)S(1)}, bf16[4096,4]{0,1:T(4,128)(2,1)}, u32[]{:S(2)}) copy-start(bf16[4096,4]{0,1:T(4,128)(2,1)} %param.18) | copy-start | bytes 98308
  109.5 4.9 %copy-start.14 = (bf16[4096,256]{1,0:T(8,128)(2,1)S(1)}, bf16[4096,256]{1,0:T(8,128)(2,1)}, u32[]{:S(2)}) copy-start(bf16[4096,256]{1,0:T(8,128)(2,1)} %param.16) | copy-start | bytes 6291460
  110.0 6.6 %copy-start.7 = (bf16[256,256]{1,0:T(8,128)(2,1)}, bf16[256,256]{1,0:T(8,128)(2,1)S(1)}, u32[]{:S(2)}) copy-start(bf16[256,256]{1,0:T(8,128)(2,1)S(1)} %fusion.inner_ref) | copy-start | bytes 393220
  110.0 5.6 %copy-start.16 = (f32[4]{0:T(128)S(1)}, f32[4]{0:T(128)}, u32[]{:S(2)}) copy-start(f32[4]{0:T(128)} %param.19) | copy-start | bytes 52
  110.0 6.6 %collective-permute-start = (bf16[3,256]{1,0:T(4,128)(2,1)S(1)}, bf16[3,256]{1,0:T(4,128)(2,1)S(1)}, u32[]{:S(2)}, u32[]{:S(2)}) collective-permute-start(bf16[3,256]{1,0:T(4,128)(2,1)S(1)} %slice.82), channel_id=1, source_target_pairs={{0,16},{16,32},{32,48},{48,64},{64,80},{80,96},{96,112},{1,17},{17... | collective-permute-start | bytes 4616 | tf_op jit(solution)/shard_map/ppermute | solution.py:23
  116.6 61.6 %copy-start.9 = (f32[256]{0:T(256)S(1)}, f32[256]{0:T(256)}, u32[]{:S(2)}) copy-start(f32[256]{0:T(256)} %param.24) | copy-start | bytes 3076
  116.6 13.4 %copy-start.10 = (bf16[3,256]{1,0:T(4,128)(2,1)}, bf16[3,256]{1,0:T(4,128)(2,1)S(1)}, u32[]{:S(2)}) copy-start(bf16[3,256]{1,0:T(4,128)(2,1)S(1)} %collective-permute-done.halo_ref) | copy-start | bytes 4612
  130.0 0.8 copy-start.1
  181.2 68.3 %copy-start.5 = (bf16[16,4096]{1,0:T(8,128)(2,1)S(1)}, bf16[16,4096]{1,0:T(8,128)(2,1)}, u32[]{:S(2)}) copy-start(bf16[16,4096]{1,0:T(8,128)(2,1)} %param.13) | copy-start | bytes 393220
Sparse Core Ops, SparseCore 0:
  10.0 81.9 all-gather.1
  181.4 68.1 reduce-scatter.1

commit v4 on v3

--- a/solution.py
+++ b/solution.py
@@ -9,6 +9,7 @@
 STATE = 128
 GROUP_HEADS = 16
 TAPS = 4
+ORDER = (0, 4, 8, 12, 1, 5, 9, 13, 2, 6, 10, 14, 15, 3, 7, 11)
 TAIL_ROWS = 8
 GROUPS = 4
 
@@ -26,6 +27,64 @@
 def from_everyone(x, axis):
     copies = jnp.broadcast_to(x, (lax.axis_size(axis), *x.shape))
     return lax.all_to_all(copies, axis, split_axis=0, concat_axis=0, tiled=True)
+
+
+def shifted(x, axis, steps):
+    count = lax.axis_size(axis)
+    return lax.ppermute(x, axis, [(k, (k + steps) % count) for k in range(count)])
+
+
+def tree_gather(x, axis):
+    opposite = shifted(x, axis, 8)
+    behind = shifted(x, axis, 4)
+    ahead = shifted(x, axis, -4)
+    bundle = jnp.concatenate((x, ahead, opposite, behind), axis=0)
+    rows = x.shape[0]
+    half = x.shape[1] // 2
+    below = shifted(bundle, axis, 1)
+    above = shifted(bundle, axis, -1)
+    left = shifted(bundle[:, :half], axis, 2)
+    right = shifted(bundle[:, half:], axis, -2)
+    left = jnp.concatenate((left[rows:], left[:rows]), axis=0)
+    return bundle, above, jnp.concatenate((left, right), axis=1), below
+
+
+def tree_scatter(rows_of, weight, axis):
+    quarter = rows_of.shape[0] // 4
+    piece = quarter // 4
+    half = weight.shape[1] // 2
+    own, above, second, below = (rows_of[k * quarter : (k + 1) * quarter] for k in range(4))
+    turned = jnp.concatenate((second[3 * piece :], second[: 3 * piece]), axis=0)
+
+    def sent(rows, columns, steps):
+        part = jnp.dot(rows, columns, preferred_element_type=jnp.float32)
+        return shifted(part.astype(jnp.bfloat16), axis, steps).astype(jnp.float32)
+
+    rising = sent(above, weight, 1)
+    falling = sent(below, weight, -1)
+    left = sent(turned, weight[:, :half], -2)
+    right = sent(second, weight[:, half:], 2)
+    total = jnp.dot(own, weight, preferred_element_type=jnp.float32)
+    total = total + rising + falling + jnp.concatenate((left, right), axis=1)
+    passed = total[piece:].astype(jnp.bfloat16)
+    opposite = shifted(passed[piece : 2 * piece], axis, 8)
+    ahead = shifted(passed[:piece], axis, 4)
+    behind = shifted(passed[2 * piece :], axis, -4)
+    return (
+        total[:piece]
+        + opposite.astype(jnp.float32)
+        + ahead.astype(jnp.float32)
+        + behind.astype(jnp.float32)
+    )
+
+
+def placement(axis, piece):
+    count = lax.axis_size(axis)
+    size = count * piece
+    slot = jnp.arange(size)
+    source = (jnp.array(ORDER, jnp.int32)[slot // piece] + lax.axis_index(axis)) % count
+    row = source * piece + slot % piece
+    return (row[:, None] == jnp.arange(size)[None, :]).astype(jnp.bfloat16)
 
 
 def split_dot(exact, wide, dims, exact_first):
@@ -190,31 +249,34 @@
         * lax.rsqrt(jnp.mean(tokens_wide * tokens_wide, axis=1, keepdims=True) + epsilon)
         * pre_gain
     ).astype(jnp.bfloat16)
-    count = lax.axis_size("tp")
-    own_rows, features = tokens.shape
-    row_count = count * own_rows
-    fit = (2**20 // (2 * row_count) - 1) // 128 * 128
-    cut = features - fit
-    first_rows = lax.all_gather(normed[:, :cut], "tp", axis=0, tiled=True)
-    last_rows = lax.all_gather(normed[:, cut:], "tp", axis=0, tiled=True)
+    own_rows = tokens.shape[0]
     margin = TAPS - 1
+    place = placement("tp", own_rows)
+    row_count = place.shape[0]
+    across = (((0,), (1,)), ((), ()))
+    along = (((0,), (0,)), ((), ()))
+    flat = (((1,), (0,)), ((), ()))
+    pieces = tree_gather(normed, "tp")
+
+    def product(left, right, dims, precision=None):
+        return lax.dot_general(
+            left, right, dims, precision=precision, preferred_element_type=jnp.float32
+        )
 
     def project(weight):
-        late = jnp.dot(last_rows, weight[cut:], preferred_element_type=jnp.float32)
-        return late + jnp.dot(first_rows, weight[:cut], preferred_element_type=jnp.float32)
+        found = [product(rows, weight, flat).astype(jnp.bfloat16) for rows in pieces]
+        return product(place, jnp.concatenate(found, axis=0), along).astype(jnp.bfloat16)
 
     def project_across(weight):
-        dims = (((0,), (1,)), ((), ()))
-        late = lax.dot_general(weight[cut:], last_rows, dims, preferred_element_type=jnp.float32)
-        return late + lax.dot_general(
-            weight[:cut], first_rows, dims, preferred_element_type=jnp.float32
-        )
-
-    state_proj = project_across(proj_states).astype(jnp.bfloat16)
+        return jnp.concatenate([product(weight, rows, across) for rows in pieces], axis=1)
+
+    state_proj = product(project_across(proj_states).astype(jnp.bfloat16), place, flat)
+    state_proj = state_proj.astype(jnp.bfloat16)
     before_states = from_behind(state_proj[:, row_count - margin :], "seq", 1)
-    inner_proj = project(proj_inner).astype(jnp.bfloat16)
-    gate_proj = project(proj_gate).astype(jnp.bfloat16)
-    step_size = jax.nn.softplus(project_across(proj_step) + step_bias[:, None])
+    inner_proj = project(proj_inner)
+    gate_proj = project(proj_gate)
+    steps = product(project_across(proj_step), place.astype(jnp.float32), flat, highest)
+    step_size = jax.nn.softplus(steps + step_bias[:, None])
     log_decay = -jnp.exp(log_rate)[:, None] * step_size
     before_inner = from_behind(inner_proj[row_count - margin :], "seq", 1)
     padded = jnp.concatenate((before_states, state_proj), axis=1).astype(jnp.float32)
@@ -234,12 +296,8 @@
     mean_square = jnp.sum(every_square, axis=0) / (GROUP_HEADS * HEAD_DIM)
     scale = jnp.repeat(lax.rsqrt(mean_square + epsilon).T, HEAD_DIM, axis=1)
     mixed_out = (gated_out * scale * norm_gain).astype(jnp.bfloat16)
-    summed = lax.psum_scatter(
-        jnp.dot(mixed_out, proj_output, preferred_element_type=jnp.float32).astype(jnp.bfloat16),
-        "tp",
-        scatter_dimension=0,
-        tiled=True,
-    ).astype(jnp.float32)
+    rows_of = product(place, mixed_out, flat).astype(jnp.bfloat16)
+    summed = tree_scatter(rows_of, proj_output, "tp")
     return (tokens_wide + summed).astype(jnp.bfloat16)
 
 

time: 259 us -> 235 us (0.907)
  starting transfers between devices: 13.2 us -> 89.9 us
  blocking collectives: 88.8 us -> 40.5 us
  waiting for transfers between devices: 114 us -> 74 us
  between operations: 13.7 us -> 0.5 us
    ppermute x0 -> x14, starting transfers between devices: none -> 74 us  [shifted(): lax.ppermute(x, axis, [(k, (k + steps) % count) for k in range(count)])]
    reduce_scatter x1 -> x0, waiting for transfers between devices: 68.3 us -> none  [body(): lax.psum_scatter(jnp.dot(mixed_out, proj_output, preferred_element_type=j...]
    ppermute x0 -> x14, waiting for transfers between devices: none -> 56.7 us  [shifted(): lax.ppermute(x, axis, [(k, (k + steps) % count) for k in range(count)])]
    all_gather x1 -> x0, blocking collectives: 48.8 us -> none  [body(): last_rows = lax.all_gather(normed[:, cut:], 'tp', axis=0, tiled=True)]
    all_gather x1 -> x0, waiting for transfers between devices: 31.4 us -> none  [body(): first_rows = lax.all_gather(normed[:, :cut], 'tp', axis=0, tiled=True)]
    all_to_all x1, waiting for transfers between devices: 13.4 us -> 16.9 us  [from_everyone(): return lax.all_to_all(copies, axis, split_axis=0, concat_axis=0, tiled=True)]
    all_to_all x1, starting transfers between devices: 7.88 us -> 10.8 us  [from_everyone(): return lax.all_to_all(copies, axis, split_axis=0, concat_axis=0, tiled=True)]
    dot_general x9 -> x26, matrix products: 12.8 us -> 13.4 us  [the longest x21 9.59 us: product(): lax.dot_general(left, right, dims, precision=precision, preferred_element...]
  transfers between devices with their start and end apart: 5 -> 17, of which waited for: 4 -> 10; matrix products, arithmetic and copies ran while one was open for 3% -> 5% of each run, Pallas kernels for 0% -> 0%
where the time goes in v4:
time: 235 us; the launch traced here: 233 us
  starting transfers between devices  89.9 us (38%)
  waiting for transfers between devices  74 us (31%)
  blocking collectives  40.5 us (17%)
  matrix products  13.4 us (6%)
  Pallas kernels  6.43 us (3%)
  other arithmetic  4.28 us (2%)
  local copies, waits for them, and re-layouts  4.21 us (2%)
    ppermute x14, starting transfers between devices, shifted(): lax.ppermute(x, axis, [(k, (k + steps) % count) for k in range(count)])  74 us
    ppermute x14, waiting for transfers between devices, shifted(): lax.ppermute(x, axis, [(k, (k + steps) % count) for k in range(count)])  56.7 us
    all_gather x1, blocking collectives, body(): messages = lax.all_gather(message, 'seq', axis=0, tiled=True)  20.8 us
    all_to_all x1, blocking collectives, from_everyone(): return lax.all_to_all(copies, axis, split_axis=0, concat_axis=0, tiled=True)  19.7 us
    all_to_all x1, waiting for transfers between devices, from_everyone(): return lax.all_to_all(copies, axis, split_axis=0, concat_axis=0, tiled=True)  16.9 us
    all_to_all x1, starting transfers between devices, from_everyone(): return lax.all_to_all(copies, axis, split_axis=0, concat_axis=0, tiled=True)  10.8 us
    dot_general x21, matrix products, product(): lax.dot_general(left, right, dims, precision=precision, preferred_element...  9.59 us
    ppermute x2, starting transfers between devices, from_behind(): lax.ppermute(value, axis, [(source, source + steps) for source in range(i...  5.17 us
  transfers between devices with their start and end apart: 17, of which 10 were waited for; matrix products, arithmetic and copies ran while one was open for 5% of the time, Pallas kernels for 0%

profile of v4, /device:TPU:56, one launch (start us, length us, event | category | flops | bytes accessed | tf_op | source)
XLA Modules:
  0.0 233.1 jit_solution(3429354687641942768)
XLA Ops:
  0.0 1.2 fusion.6
  1.2 1.0 fusion.8
  2.2 10.9 %collective-permute-start.2 = (bf16[16,4096]{1,0:T(8,128)(2,1)S(1)}, bf16[16,4096]{1,0:T(8,128)(2,1)S(1)}, u32[]{:S(2)}, u32[]{:S(2)}) collective-permute-start(bf16[16,4096]{1,0:T(8,128)(2,1)S(1)} %fusion.8), channel_id=1, source_target_pairs={{0,4},{1,5},{2,6},{3,7},{4,8},{5,9},{6,10},{7,11},{8,12},{9,13},{1... | collective-permute-start | bytes 393224 | tf_op jit(solution)/shard_map/ppermute | solution.py:34
  13.2 14.6 %collective-permute-start.1 = (bf16[16,4096]{1,0:T(8,128)(2,1)S(1)}, bf16[16,4096]{1,0:T(8,128)(2,1)S(1)}, u32[]{:S(2)}, u32[]{:S(2)}) collective-permute-start(bf16[16,4096]{1,0:T(8,128)(2,1)S(1)} %fusion.8), channel_id=1, source_target_pairs={{0,8},{1,9},{2,10},{3,11},{4,12},{5,13},{6,14},{7,15},{8,0},{9,1},... | collective-permute-start | bytes 393224 | tf_op jit(solution)/shard_map/ppermute | solution.py:34
  27.7 3.6 %collective-permute-start = (bf16[16,4096]{1,0:T(8,128)(2,1)S(1)}, bf16[16,4096]{1,0:T(8,128)(2,1)S(1)}, u32[]{:S(2)}, u32[]{:S(2)}) collective-permute-start(bf16[16,4096]{1,0:T(8,128)(2,1)S(1)} %fusion.8), channel_id=1, source_target_pairs={{0,12},{1,13},{2,14},{3,15},{4,0},{5,1},{6,2},{7,3},{8,4},{9,5},{1... | collective-permute-start | bytes 393224 | tf_op jit(solution)/shard_map/ppermute | solution.py:34
  31.7 0.7 broadcast_in_dim.9
  32.4 0.7 broadcast_in_dim_reshape.3.skip_ref
  33.1 0.9 slice_bitcast_fusion.3
  34.0 0.7 exponential_negate_fusion
  34.7 12.6 %collective-permute-done.1 = bf16[16,4096]{1,0:T(8,128)(2,1)S(1)} collective-permute-done((bf16[16,4096]{1,0:T(8,128)(2,1)S(1)}, bf16[16,4096]{1,0:T(8,128)(2,1)S(1)}, u32[]{:S(2)}, u32[]{:S(2)}) %collective-permute-start.1) | collective-permute-done | bytes 131104 | tf_op jit(solution)/shard_map/ppermute | solution.py:34
  47.3 4.4 %collective-permute-done = bf16[16,4096]{1,0:T(8,128)(2,1)S(1)} collective-permute-done((bf16[16,4096]{1,0:T(8,128)(2,1)S(1)}, bf16[16,4096]{1,0:T(8,128)(2,1)S(1)}, u32[]{:S(2)}, u32[]{:S(2)}) %collective-permute-start) | collective-permute-done | bytes 131104 | tf_op jit(solution)/shard_map/ppermute | solution.py:34
  51.8 2.4 %collective-permute-start.6 = (bf16[64,4096]{1,0:T(8,128)(2,1)S(1)}, bf16[64,4096]{1,0:T(8,128)(2,1)S(1)}, u32[]{:S(2)}, u32[]{:S(2)}) collective-permute-start(bf16[64,4096]{1,0:T(8,128)(2,1)S(1)} %pad_maximum_fusion), channel_id=1, source_target_pairs={{0,1},{1,2},{2,3},{3,4},{4,5},{5,6},{6,7},{7,8},{8,9},{9,10},{10,1... | collective-permute-start | bytes 1572872 | tf_op jit(solution)/shard_map/ppermute | solution.py:34
  54.3 4.6 %collective-permute-start.3 = (bf16[64,4096]{1,0:T(8,128)(2,1)S(1)}, bf16[64,4096]{1,0:T(8,128)(2,1)S(1)}, u32[]{:S(2)}, u32[]{:S(2)}) collective-permute-start(bf16[64,4096]{1,0:T(8,128)(2,1)S(1)} %pad_maximum_fusion), channel_id=1, source_target_pairs={{0,15},{1,0},{2,1},{3,2},{4,3},{5,4},{6,5},{7,6},{8,7},{9,8},{10,9... | collective-permute-start | bytes 1572872 | tf_op jit(solution)/shard_map/ppermute | solution.py:34
  58.9 0.5 convolution_convert_fusion.11
  59.4 0.5 convolution_convert_fusion.15
  59.9 1.9 collective-permute-start.4
  61.8 6.0 %collective-permute-start.5 = (bf16[64,2048]{1,0:T(8,128)(2,1)S(1)}, bf16[64,2048]{1,0:T(8,128)(2,1)S(1)}, u32[]{:S(2)}, u32[]{:S(2)}) collective-permute-start(bf16[64,2048]{1,0:T(8,128)(2,1)S(1)} %get-tuple-element.19), channel_id=1, source_target_pairs={{0,14},{1,15},{2,0},{3,1},{4,2},{5,3},{6,4},{7,5},{8,6},{9,7},{10,... | collective-permute-start | bytes 786440 | tf_op jit(solution)/shard_map/ppermute | solution.py:34
  67.9 0.2 convolution_bitcast_fusion.3
  68.1 0.3 fusion
  68.4 7.2 %collective-permute-done.4 = bf16[64,2048]{1,0:T(8,128)(2,1)S(1)} collective-permute-done((bf16[64,2048]{1,0:T(8,128)(2,1)S(1)}, bf16[64,2048]{1,0:T(8,128)(2,1)S(1)}, u32[]{:S(2)}, u32[]{:S(2)}) %collective-permute-start.4) | collective-permute-done | bytes 262176 | tf_op jit(solution)/shard_map/ppermute | solution.py:34
  75.6 5.2 %collective-permute-done.5 = bf16[64,2048]{1,0:T(8,128)(2,1)S(1)} collective-permute-done((bf16[64,2048]{1,0:T(8,128)(2,1)S(1)}, bf16[64,2048]{1,0:T(8,128)(2,1)S(1)}, u32[]{:S(2)}, u32[]{:S(2)}) %collective-permute-start.5) | collective-permute-done | bytes 262176 | tf_op jit(solution)/shard_map/ppermute | solution.py:34
  80.9 0.5 convolution_convert_fusion.9
  81.3 0.2 convolution_bitcast_fusion.1
  81.6 0.3 fusion.2
  81.9 0.5 convolution_convert_fusion.13
  82.3 0.3 fusion.3
  82.6 0.3 fusion.1
  83.2 1.3 collective-permute-start.8
  84.5 0.5 convolution_convert_fusion.12
  85.0 0.3 collective-permute-done.8
  85.6 0.8 broadcast_in_dim.8
  86.5 10.8 %all-to-all-start = ((bf16[16,64,256]{2,1,0:T(8,128)(2,1)}), bf16[16,64,256]{2,1,0:T(8,128)(2,1)}, u32[]{:S(2)}, u32[]{:S(2)}) async-start(bf16[16,64,256]{2,1,0:T(8,128)(2,1)} %broadcast_in_dim.8), calls=%async_computation | async-start | bytes 1048576 | tf_op jit(solution)/shard_map/all_to_all | solution.py:29
  97.2 0.5 convolution_convert_fusion.14
  97.7 0.3 convolution_convert_fusion.6.inner_ref
  98.1 3.9 %collective-permute-start.7 = (bf16[3,256]{1,0:T(4,128)(2,1)S(1)}, bf16[3,256]{1,0:T(4,128)(2,1)S(1)}, u32[]{:S(2)}, u32[]{:S(2)}) collective-permute-start(bf16[3,256]{1,0:T(4,128)(2,1)S(1)} %slice.132), channel_id=1, source_target_pairs={{0,16},{16,32},{32,48},{48,64},{64,80},{80,96},{96,112},{1,17},{17... | collective-permute-start | bytes 4616 | tf_op jit(solution)/shard_map/ppermute | solution.py:24
  102.0 0.5 convolution_convert_fusion.8
  102.4 0.5 convolution_convert_fusion.10
  102.9 1.0 convolution_convert_fusion.5.gate_ref
  104.1 0.3 convolution_bitcast_fusion.2
  104.4 0.9 broadcast_multiply_fusion
  105.3 16.9 %all-to-all-done = bf16[16,64,256]{2,1,0:T(8,128)(2,1)} async-done(((bf16[16,64,256]{2,1,0:T(8,128)(2,1)}), bf16[16,64,256]{2,1,0:T(8,128)(2,1)}, u32[]{:S(2)}, u32[]{:S(2)}) %all-to-all-start) | async-done | bytes 524320 | tf_op jit(solution)/shard_map/all_to_all | solution.py:29
  122.2 3.6 %local_scan.1 = (f32[256,256]{1,0:T(8,128)}, bf16[1,144,256]{2,1,0:T(8,128)(2,1)}, f32[256,128]{1,0:T(8,128)}) custom-call(bf16[256,256]{1,0:T(8,128)(2,1)} %copy-done.7, bf16[3,256]{1,0:T(4,128)(2,1)} %copy-done.8, f32[4,256]{1,0:T(4,128)} %taps_ref.1, bf16[1024,256]{1,0:T(8,128)(2,1)} %bitcast.10.states_ref, f32[4,256]{1,0:T(4,128)} %get-tuple-element.25.step_ref, ...), custom_call_target="tpu_custom_call" | custom-call | tf_op jit(solution)/shard_map/local_scan/pallas_call | solution.py:201
  125.8 20.8 %all_gather.3.messages_ref = bf16[8,144,256]{2,1,0:T(8,128)(2,1)} all-gather(bf16[1,144,256]{2,1,0:T(8,128)(2,1)} %get-tuple-element.10), channel_id=1, replica_groups=mesh['dp'=8,'seq'=8,'tp'=16] {'seq'}, dimensions={0}, use_global_device_ids=true | all-gather | bytes 663552 | tf_op jit(solution)/shard_map/all_gather | solution.py:292
  146.6 2.8 %carry_in.1 = (f32[256,256]{1,0:T(8,128)}, f32[1,4,256]{2,1,0:T(4,128)}) custom-call(s32[1]{0:T(128)} %bitcast.1.position_ref, bf16[8,144,256]{2,1,0:T(8,128)(2,1)} %all_gather.3.messages_ref, bf16[1024,256]{1,0:T(8,128)(2,1)} %bitcast.10.states_ref, f32[256,128]{1,0:T(8,128)} %get-tuple-element.11.reach_ref, f32[256,256]{1,0:T(8,128)} %get-tuple-element.12.local_ref, ...), custom_call_target="tpu_custom_call" | custom-call | tf_op jit(solution)/shard_map/carry_in/pallas_call | solution.py:218
  149.4 0.7 broadcast_in_dim.10
  150.1 19.7 %all_to_all.10 = f32[16,4,256]{2,1,0:T(4,128)S(1)} all-to-all(f32[16,4,256]{2,1,0:T(4,128)S(1)} %broadcast_in_dim.10), channel_id=1, replica_groups=mesh['dp'=8,'seq'=8,'tp'=16] {'tp'}, dimensions={0} | all-to-all | bytes 131072 | tf_op jit(solution)/shard_map/all_to_all | solution.py:29
  170.0 1.3 convolution_convert_fusion.4
  171.4 2.1 convolution_convert_fusion
  173.4 0.5 convolution_convert_fusion.1
  173.9 2.9 %collective-permute-start.9 = (bf16[64,4096]{1,0:T(8,128)(2,1)S(1)}, bf16[64,4096]{1,0:T(8,128)(2,1)S(1)}, u32[]{:S(2)}, u32[]{:S(2)}) collective-permute-start(bf16[64,4096]{1,0:T(8,128)(2,1)S(1)} %convolution_convert_fusion.1), channel_id=1, source_target_pairs={{0,1},{1,2},{2,3},{3,4},{4,5},{5,6},{6,7},{7,8},{8,9},{9,10},{10,1... | collective-permute-start | bytes 1572872 | tf_op jit(solution)/shard_map/ppermute | solution.py:34
  176.8 4.2 %collective-permute-start.10 = (bf16[64,4096]{1,0:T(8,128)(2,1)S(1)}, bf16[64,4096]{1,0:T(8,128)(2,1)S(1)}, u32[]{:S(2)}, u32[]{:S(2)}) collective-permute-start(bf16[64,4096]{1,0:T(8,128)(2,1)S(1)} %convolution_convert_fusion), channel_id=1, source_target_pairs={{0,15},{1,0},{2,1},{3,2},{4,3},{5,4},{6,5},{7,6},{8,7},{9,8},{10,9... | collective-permute-start | bytes 1572872 | tf_op jit(solution)/shard_map/ppermute | solution.py:34
  181.0 0.3 convolution_convert_fusion.2
  181.3 2.0 collective-permute-start.12
  183.3 0.3 convolution_convert_fusion.3
  183.6 6.1 %collective-permute-start.11 = (bf16[64,2048]{1,0:T(8,128)(2,1)S(1)}, bf16[64,2048]{1,0:T(8,128)(2,1)S(1)}, u32[]{:S(2)}, u32[]{:S(2)}) collective-permute-start(bf16[64,2048]{1,0:T(8,128)(2,1)S(1)} %convolution_convert_fusion.3), channel_id=1, source_target_pairs={{0,14},{1,15},{2,0},{3,1},{4,2},{5,3},{6,4},{7,5},{8,6},{9,7},{10,... | collective-permute-start | bytes 786440 | tf_op jit(solution)/shard_map/ppermute | solution.py:34
  189.8 10.5 %collective-permute-done.12 = bf16[64,2048]{1,0:T(8,128)(2,1)S(1)} collective-permute-done((bf16[64,2048]{1,0:T(8,128)(2,1)S(1)}, bf16[64,2048]{1,0:T(8,128)(2,1)S(1)}, u32[]{:S(2)}, u32[]{:S(2)}) %collective-permute-start.12) | collective-permute-done | bytes 262176 | tf_op jit(solution)/shard_map/ppermute | solution.py:34
  200.3 2.0 collective-permute-done.11
  202.3 0.6 fusion.71
  203.0 4.9 %collective-permute-start.13 = (bf16[16,4096]{1,0:T(8,128)(2,1)S(1)}, bf16[16,4096]{1,0:T(8,128)(2,1)S(1)}, u32[]{:S(2)}, u32[]{:S(2)}) collective-permute-start(bf16[16,4096]{1,0:T(8,128)(2,1)S(1)} %get-tuple-element.15), channel_id=1, source_target_pairs={{0,8},{1,9},{2,10},{3,11},{4,12},{5,13},{6,14},{7,15},{8,0},{9,1},... | collective-permute-start | bytes 393224 | tf_op jit(solution)/shard_map/ppermute | solution.py:34
  207.9 5.9 %collective-permute-start.15 = (bf16[16,4096]{1,0:T(8,128)(2,1)S(1)}, bf16[16,4096]{1,0:T(8,128)(2,1)S(1)}, u32[]{:S(2)}, u32[]{:S(2)}) collective-permute-start(bf16[16,4096]{1,0:T(8,128)(2,1)S(1)} %get-tuple-element.16), channel_id=1, source_target_pairs={{0,12},{1,13},{2,14},{3,15},{4,0},{5,1},{6,2},{7,3},{8,4},{9,5},{1... | collective-permute-start | bytes 393224 | tf_op jit(solution)/shard_map/ppermute | solution.py:34
  213.8 3.9 %collective-permute-start.14 = (bf16[16,4096]{1,0:T(8,128)(2,1)S(1)}, bf16[16,4096]{1,0:T(8,128)(2,1)S(1)}, u32[]{:S(2)}, u32[]{:S(2)}) collective-permute-start(bf16[16,4096]{1,0:T(8,128)(2,1)S(1)} %get-tuple-element.17), channel_id=1, source_target_pairs={{0,4},{1,5},{2,6},{3,7},{4,8},{5,9},{6,10},{7,11},{8,12},{9,13},{1... | collective-permute-start | bytes 393224 | tf_op jit(solution)/shard_map/ppermute | solution.py:34
  217.7 3.1 %collective-permute-done.13 = bf16[16,4096]{1,0:T(8,128)(2,1)S(1)} collective-permute-done((bf16[16,4096]{1,0:T(8,128)(2,1)S(1)}, bf16[16,4096]{1,0:T(8,128)(2,1)S(1)}, u32[]{:S(2)}, u32[]{:S(2)}) %collective-permute-start.13) | collective-permute-done | bytes 131104 | tf_op jit(solution)/shard_map/ppermute | solution.py:34
  220.8 11.5 %collective-permute-done.15 = bf16[16,4096]{1,0:T(8,128)(2,1)S(1)} collective-permute-done((bf16[16,4096]{1,0:T(8,128)(2,1)S(1)}, bf16[16,4096]{1,0:T(8,128)(2,1)S(1)}, u32[]{:S(2)}, u32[]{:S(2)}) %collective-permute-start.15) | collective-permute-done | bytes 131104 | tf_op jit(solution)/shard_map/ppermute | solution.py:34
  232.4 0.7 fusion.9
  (58 shorter events, 1.5 us)
Async XLA Ops:
  0.0 59.4 %copy-start = (bf16[4096,256]{1,0:T(8,128)(2,1)S(1)}, bf16[4096,256]{1,0:T(8,128)(2,1)}, u32[]{:S(2)}) copy-start(bf16[4096,256]{1,0:T(8,128)(2,1)} %param.16) | copy-start | bytes 6291460
  2.2 32.4 %collective-permute-start.2 = (bf16[16,4096]{1,0:T(8,128)(2,1)S(1)}, bf16[16,4096]{1,0:T(8,128)(2,1)S(1)}, u32[]{:S(2)}, u32[]{:S(2)}) collective-permute-start(bf16[16,4096]{1,0:T(8,128)(2,1)S(1)} %fusion.8), channel_id=1, source_target_pairs={{0,4},{1,5},{2,6},{3,7},{4,8},{5,9},{6,10},{7,11},{8,12},{9,13},{1... | collective-permute-start | bytes 393224 | tf_op jit(solution)/shard_map/ppermute | solution.py:34
  13.2 34.2 %collective-permute-start.1 = (bf16[16,4096]{1,0:T(8,128)(2,1)S(1)}, bf16[16,4096]{1,0:T(8,128)(2,1)S(1)}, u32[]{:S(2)}, u32[]{:S(2)}) collective-permute-start(bf16[16,4096]{1,0:T(8,128)(2,1)S(1)} %fusion.8), channel_id=1, source_target_pairs={{0,8},{1,9},{2,10},{3,11},{4,12},{5,13},{6,14},{7,15},{8,0},{9,1},... | collective-permute-start | bytes 393224 | tf_op jit(solution)/shard_map/ppermute | solution.py:34
  27.7 24.0 %collective-permute-start = (bf16[16,4096]{1,0:T(8,128)(2,1)S(1)}, bf16[16,4096]{1,0:T(8,128)(2,1)S(1)}, u32[]{:S(2)}, u32[]{:S(2)}) collective-permute-start(bf16[16,4096]{1,0:T(8,128)(2,1)S(1)} %fusion.8), channel_id=1, source_target_pairs={{0,12},{1,13},{2,14},{3,15},{4,0},{5,1},{6,2},{7,3},{8,4},{9,5},{1... | collective-permute-start | bytes 393224 | tf_op jit(solution)/shard_map/ppermute | solution.py:34
  33.1 25.8 %copy-start.2 = (bf16[4096,256]{1,0:T(8,128)(2,1)S(1)}, bf16[4096,256]{1,0:T(8,128)(2,1)}, u32[]{:S(2)}) copy-start(bf16[4096,256]{1,0:T(8,128)(2,1)} %param.17) | copy-start | bytes 6291460
  51.8 16.0 %copy-start.6 = (bf16[4096,4]{0,1:T(4,128)(2,1)S(1)}, bf16[4096,4]{0,1:T(4,128)(2,1)}, u32[]{:S(2)}) copy-start(bf16[4096,4]{0,1:T(4,128)(2,1)} %param.19) | copy-start | bytes 98308
  51.8 30.5 %collective-permute-start.6 = (bf16[64,4096]{1,0:T(8,128)(2,1)S(1)}, bf16[64,4096]{1,0:T(8,128)(2,1)S(1)}, u32[]{:S(2)}, u32[]{:S(2)}) collective-permute-start(bf16[64,4096]{1,0:T(8,128)(2,1)S(1)} %pad_maximum_fusion), channel_id=1, source_target_pairs={{0,1},{1,2},{2,3},{3,4},{4,5},{5,6},{6,7},{7,8},{8,9},{9,10},{10,1... | collective-permute-start | bytes 1572872 | tf_op jit(solution)/shard_map/ppermute | solution.py:34
  54.3 28.3 %collective-permute-start.3 = (bf16[64,4096]{1,0:T(8,128)(2,1)S(1)}, bf16[64,4096]{1,0:T(8,128)(2,1)S(1)}, u32[]{:S(2)}, u32[]{:S(2)}) collective-permute-start(bf16[64,4096]{1,0:T(8,128)(2,1)S(1)} %pad_maximum_fusion), channel_id=1, source_target_pairs={{0,15},{1,0},{2,1},{3,2},{4,3},{5,4},{6,5},{7,6},{8,7},{9,8},{10,9... | collective-permute-start | bytes 1572872 | tf_op jit(solution)/shard_map/ppermute | solution.py:34
  59.4 8.7 %copy-start.4 = (bf16[4096,64]{0,1:T(8,128)(2,1)S(1)}, bf16[4096,64]{0,1:T(8,128)(2,1)}, u32[]{:S(2)}) copy-start(bf16[4096,64]{0,1:T(8,128)(2,1)} %param.18) | copy-start | bytes 1572868
  59.9 15.7 %collective-permute-start.4 = (bf16[64,2048]{1,0:T(8,128)(2,1)S(1)}, bf16[64,2048]{1,0:T(8,128)(2,1)S(1)}, u32[]{:S(2)}, u32[]{:S(2)}) collective-permute-start(bf16[64,2048]{1,0:T(8,128)(2,1)S(1)} %get-tuple-element.18), channel_id=1, source_target_pairs={{0,2},{1,3},{2,4},{3,5},{4,6},{5,7},{6,8},{7,9},{8,10},{9,11},{10,... | collective-permute-start | bytes 786440 | tf_op jit(solution)/shard_map/ppermute | solution.py:34
  61.8 19.0 %collective-permute-start.5 = (bf16[64,2048]{1,0:T(8,128)(2,1)S(1)}, bf16[64,2048]{1,0:T(8,128)(2,1)S(1)}, u32[]{:S(2)}, u32[]{:S(2)}) collective-permute-start(bf16[64,2048]{1,0:T(8,128)(2,1)S(1)} %get-tuple-element.19), channel_id=1, source_target_pairs={{0,14},{1,15},{2,0},{3,1},{4,2},{5,3},{6,4},{7,5},{8,6},{9,7},{10,... | collective-permute-start | bytes 786440 | tf_op jit(solution)/shard_map/ppermute | solution.py:34
  83.2 2.1 collective-permute-start.8
  86.5 35.7 %all-to-all-start = ((bf16[16,64,256]{2,1,0:T(8,128)(2,1)}), bf16[16,64,256]{2,1,0:T(8,128)(2,1)}, u32[]{:S(2)}, u32[]{:S(2)}) async-start(bf16[16,64,256]{2,1,0:T(8,128)(2,1)} %broadcast_in_dim.8), calls=%async_computation | async-start | bytes 1048576 | tf_op jit(solution)/shard_map/all_to_all | solution.py:29
  97.2 4.7 %copy-start.3 = (bf16[4096,256]{1,0:T(8,128)(2,1)S(1)}, bf16[4096,256]{1,0:T(8,128)(2,1)}, u32[]{:S(2)}) copy-start(bf16[4096,256]{1,0:T(8,128)(2,1)} %param.17) | copy-start | bytes 6291460
  98.0 4.9 %copy-start.7 = (bf16[256,256]{1,0:T(8,128)(2,1)}, bf16[256,256]{1,0:T(8,128)(2,1)S(1)}, u32[]{:S(2)}) copy-start(bf16[256,256]{1,0:T(8,128)(2,1)S(1)} %convolution_convert_fusion.6.inner_ref) | copy-start | bytes 393220
  98.1 7.2 %collective-permute-start.7 = (bf16[3,256]{1,0:T(4,128)(2,1)S(1)}, bf16[3,256]{1,0:T(4,128)(2,1)S(1)}, u32[]{:S(2)}, u32[]{:S(2)}) collective-permute-start(bf16[3,256]{1,0:T(4,128)(2,1)S(1)} %slice.132), channel_id=1, source_target_pairs={{0,16},{16,32},{32,48},{48,64},{64,80},{80,96},{96,112},{1,17},{17... | collective-permute-start | bytes 4616 | tf_op jit(solution)/shard_map/ppermute | solution.py:24
  102.4 2.0 copy-start.10
  104.4 65.6 %copy-start.9 = (f32[256]{0:T(256)S(1)}, f32[256]{0:T(256)}, u32[]{:S(2)}) copy-start(f32[256]{0:T(256)} %param.25) | copy-start | bytes 3076
  105.3 16.9 %copy-start.8 = (bf16[3,256]{1,0:T(4,128)(2,1)}, bf16[3,256]{1,0:T(4,128)(2,1)S(1)}, u32[]{:S(2)}) copy-start(bf16[3,256]{1,0:T(4,128)(2,1)S(1)} %collective-permute-done.7.halo_ref) | copy-start | bytes 4612
  170.0 3.4 %copy-start.1 = (bf16[256,4096]{1,0:T(8,128)(2,1)S(1)}, bf16[256,4096]{1,0:T(8,128)(2,1)}, u32[]{:S(2)}) copy-start(bf16[256,4096]{1,0:T(8,128)(2,1)} %param.26) | copy-start | bytes 6291460
  173.9 28.4 %collective-permute-start.9 = (bf16[64,4096]{1,0:T(8,128)(2,1)S(1)}, bf16[64,4096]{1,0:T(8,128)(2,1)S(1)}, u32[]{:S(2)}, u32[]{:S(2)}) collective-permute-start(bf16[64,4096]{1,0:T(8,128)(2,1)S(1)} %convolution_convert_fusion.1), channel_id=1, source_target_pairs={{0,1},{1,2},{2,3},{3,4},{4,5},{5,6},{6,7},{7,8},{8,9},{9,10},{10,1... | collective-permute-start | bytes 1572872 | tf_op jit(solution)/shard_map/ppermute | solution.py:34
  176.8 25.5 %collective-permute-start.10 = (bf16[64,4096]{1,0:T(8,128)(2,1)S(1)}, bf16[64,4096]{1,0:T(8,128)(2,1)S(1)}, u32[]{:S(2)}, u32[]{:S(2)}) collective-permute-start(bf16[64,4096]{1,0:T(8,128)(2,1)S(1)} %convolution_convert_fusion), channel_id=1, source_target_pairs={{0,15},{1,0},{2,1},{3,2},{4,3},{5,4},{6,5},{7,6},{8,7},{9,8},{10,9... | collective-permute-start | bytes 1572872 | tf_op jit(solution)/shard_map/ppermute | solution.py:34
  181.3 18.9 %collective-permute-start.12 = (bf16[64,2048]{1,0:T(8,128)(2,1)S(1)}, bf16[64,2048]{1,0:T(8,128)(2,1)S(1)}, u32[]{:S(2)}, u32[]{:S(2)}) collective-permute-start(bf16[64,2048]{1,0:T(8,128)(2,1)S(1)} %convolution_convert_fusion.2), channel_id=1, source_target_pairs={{0,2},{1,3},{2,4},{3,5},{4,6},{5,7},{6,8},{7,9},{8,10},{9,11},{10,... | collective-permute-start | bytes 786440 | tf_op jit(solution)/shard_map/ppermute | solution.py:34
  183.6 48.8 %copy-start.5 = (bf16[16,4096]{1,0:T(8,128)(2,1)S(1)}, bf16[16,4096]{1,0:T(8,128)(2,1)}, u32[]{:S(2)}) copy-start(bf16[16,4096]{1,0:T(8,128)(2,1)} %param.14) | copy-start | bytes 393220
  183.6 18.7 %collective-permute-start.11 = (bf16[64,2048]{1,0:T(8,128)(2,1)S(1)}, bf16[64,2048]{1,0:T(8,128)(2,1)S(1)}, u32[]{:S(2)}, u32[]{:S(2)}) collective-permute-start(bf16[64,2048]{1,0:T(8,128)(2,1)S(1)} %convolution_convert_fusion.3), channel_id=1, source_target_pairs={{0,14},{1,15},{2,0},{3,1},{4,2},{5,3},{6,4},{7,5},{8,6},{9,7},{10,... | collective-permute-start | bytes 786440 | tf_op jit(solution)/shard_map/ppermute | solution.py:34
  203.0 17.8 %collective-permute-start.13 = (bf16[16,4096]{1,0:T(8,128)(2,1)S(1)}, bf16[16,4096]{1,0:T(8,128)(2,1)S(1)}, u32[]{:S(2)}, u32[]{:S(2)}) collective-permute-start(bf16[16,4096]{1,0:T(8,128)(2,1)S(1)} %get-tuple-element.15), channel_id=1, source_target_pairs={{0,8},{1,9},{2,10},{3,11},{4,12},{5,13},{6,14},{7,15},{8,0},{9,1},... | collective-permute-start | bytes 393224 | tf_op jit(solution)/shard_map/ppermute | solution.py:34
  207.9 24.4 %collective-permute-start.15 = (bf16[16,4096]{1,0:T(8,128)(2,1)S(1)}, bf16[16,4096]{1,0:T(8,128)(2,1)S(1)}, u32[]{:S(2)}, u32[]{:S(2)}) collective-permute-start(bf16[16,4096]{1,0:T(8,128)(2,1)S(1)} %get-tuple-element.16), channel_id=1, source_target_pairs={{0,12},{1,13},{2,14},{3,15},{4,0},{5,1},{6,2},{7,3},{8,4},{9,5},{1... | collective-permute-start | bytes 393224 | tf_op jit(solution)/shard_map/ppermute | solution.py:34
  213.8 18.5 %collective-permute-start.14 = (bf16[16,4096]{1,0:T(8,128)(2,1)S(1)}, bf16[16,4096]{1,0:T(8,128)(2,1)S(1)}, u32[]{:S(2)}, u32[]{:S(2)}) collective-permute-start(bf16[16,4096]{1,0:T(8,128)(2,1)S(1)} %get-tuple-element.17), channel_id=1, source_target_pairs={{0,4},{1,5},{2,6},{3,7},{4,8},{5,9},{6,10},{7,11},{8,12},{9,13},{1... | collective-permute-start | bytes 393224 | tf_op jit(solution)/shard_map/ppermute | solution.py:34

commit v5 on v4

--- a/solution.py
+++ b/solution.py
@@ -56,14 +56,19 @@
     own, above, second, below = (rows_of[k * quarter : (k + 1) * quarter] for k in range(4))
     turned = jnp.concatenate((second[3 * piece :], second[: 3 * piece]), axis=0)
 
-    def sent(rows, columns, steps):
+    def sums(rows, columns):
         part = jnp.dot(rows, columns, preferred_element_type=jnp.float32)
-        return shifted(part.astype(jnp.bfloat16), axis, steps).astype(jnp.float32)
-
-    rising = sent(above, weight, 1)
-    falling = sent(below, weight, -1)
-    left = sent(turned, weight[:, :half], -2)
-    right = sent(second, weight[:, half:], 2)
+        return part.astype(jnp.bfloat16)
+
+    def sent(part, steps):
+        return shifted(part, axis, steps).astype(jnp.float32)
+
+    rising = sent(sums(above, weight), 1)
+    falling = sent(sums(below, weight), -1)
+    left = sent(sums(turned, weight[:, :half]), -2)
+    last = sums(second, weight[:, half:])
+    right = sent(last, 2)
+    own = lax.optimization_barrier((own, last))[0]
     total = jnp.dot(own, weight, preferred_element_type=jnp.float32)
     total = total + rising + falling + jnp.concatenate((left, right), axis=1)
     passed = total[piece:].astype(jnp.bfloat16)

time: 235 us -> 235 us (level)
  no operation moved by 1% of the time
where the time goes in v5:
time: 235 us; the launch traced here: 233 us
  starting transfers between devices  89.7 us (38%)
  waiting for transfers between devices  73.8 us (31%)
  blocking collectives  40.5 us (17%)
  matrix products  13.4 us (6%)
  Pallas kernels  6.43 us (3%)
  other arithmetic  4.28 us (2%)
  local copies, waits for them, and re-layouts  4.21 us (2%)
    ppermute x14, starting transfers between devices, shifted(): lax.ppermute(x, axis, [(k, (k + steps) % count) for k in range(count)])  73.8 us
    ppermute x14, waiting for transfers between devices, shifted(): lax.ppermute(x, axis, [(k, (k + steps) % count) for k in range(count)])  56.6 us
    all_gather x1, blocking collectives, body(): messages = lax.all_gather(message, 'seq', axis=0, tiled=True)  20.8 us
    all_to_all x1, blocking collectives, from_everyone(): return lax.all_to_all(copies, axis, split_axis=0, concat_axis=0, tiled=True)  19.7 us
    all_to_all x1, waiting for transfers between devices, from_everyone(): return lax.all_to_all(copies, axis, split_axis=0, concat_axis=0, tiled=True)  16.9 us
    all_to_all x1, starting transfers between devices, from_everyone(): return lax.all_to_all(copies, axis, split_axis=0, concat_axis=0, tiled=True)  10.8 us
    dot_general x21, matrix products, product(): lax.dot_general(left, right, dims, precision=precision, preferred_element...  9.59 us
    ppermute x2, starting transfers between devices, from_behind(): lax.ppermute(value, axis, [(source, source + steps) for source in range(i...  5.17 us
  transfers between devices with their start and end apart: 17, of which 10 were waited for; matrix products, arithmetic and copies ran while one was open for 5% of the time, Pallas kernels for 0%

profile of v5, /device:TPU:56, one launch (start us, length us, event | category | flops | bytes accessed | tf_op | source)
XLA Modules:
  0.0 232.9 jit_solution(6997023173404106621)
XLA Ops:
  0.0 1.2 fusion.6
  1.2 1.0 fusion.8
  2.2 10.9 %collective-permute-start.2 = (bf16[16,4096]{1,0:T(8,128)(2,1)S(1)}, bf16[16,4096]{1,0:T(8,128)(2,1)S(1)}, u32[]{:S(2)}, u32[]{:S(2)}) collective-permute-start(bf16[16,4096]{1,0:T(8,128)(2,1)S(1)} %fusion.8), channel_id=1, source_target_pairs={{0,4},{1,5},{2,6},{3,7},{4,8},{5,9},{6,10},{7,11},{8,12},{9,13},{1... | collective-permute-start | bytes 393224 | tf_op jit(solution)/shard_map/ppermute | solution.py:34
  13.2 14.6 %collective-permute-start.1 = (bf16[16,4096]{1,0:T(8,128)(2,1)S(1)}, bf16[16,4096]{1,0:T(8,128)(2,1)S(1)}, u32[]{:S(2)}, u32[]{:S(2)}) collective-permute-start(bf16[16,4096]{1,0:T(8,128)(2,1)S(1)} %fusion.8), channel_id=1, source_target_pairs={{0,8},{1,9},{2,10},{3,11},{4,12},{5,13},{6,14},{7,15},{8,0},{9,1},... | collective-permute-start | bytes 393224 | tf_op jit(solution)/shard_map/ppermute | solution.py:34
  27.7 3.6 %collective-permute-start = (bf16[16,4096]{1,0:T(8,128)(2,1)S(1)}, bf16[16,4096]{1,0:T(8,128)(2,1)S(1)}, u32[]{:S(2)}, u32[]{:S(2)}) collective-permute-start(bf16[16,4096]{1,0:T(8,128)(2,1)S(1)} %fusion.8), channel_id=1, source_target_pairs={{0,12},{1,13},{2,14},{3,15},{4,0},{5,1},{6,2},{7,3},{8,4},{9,5},{1... | collective-permute-start | bytes 393224 | tf_op jit(solution)/shard_map/ppermute | solution.py:34
  31.7 0.7 broadcast_in_dim.9
  32.4 0.7 broadcast_in_dim_reshape.3.skip_ref
  33.1 0.9 slice_bitcast_fusion.3
  34.0 0.7 exponential_negate_fusion
  34.7 12.6 %collective-permute-done.1 = bf16[16,4096]{1,0:T(8,128)(2,1)S(1)} collective-permute-done((bf16[16,4096]{1,0:T(8,128)(2,1)S(1)}, bf16[16,4096]{1,0:T(8,128)(2,1)S(1)}, u32[]{:S(2)}, u32[]{:S(2)}) %collective-permute-start.1) | collective-permute-done | bytes 131104 | tf_op jit(solution)/shard_map/ppermute | solution.py:34
  47.3 4.4 %collective-permute-done = bf16[16,4096]{1,0:T(8,128)(2,1)S(1)} collective-permute-done((bf16[16,4096]{1,0:T(8,128)(2,1)S(1)}, bf16[16,4096]{1,0:T(8,128)(2,1)S(1)}, u32[]{:S(2)}, u32[]{:S(2)}) %collective-permute-start) | collective-permute-done | bytes 131104 | tf_op jit(solution)/shard_map/ppermute | solution.py:34
  51.8 2.4 %collective-permute-start.6 = (bf16[64,4096]{1,0:T(8,128)(2,1)S(1)}, bf16[64,4096]{1,0:T(8,128)(2,1)S(1)}, u32[]{:S(2)}, u32[]{:S(2)}) collective-permute-start(bf16[64,4096]{1,0:T(8,128)(2,1)S(1)} %pad_maximum_fusion), channel_id=1, source_target_pairs={{0,1},{1,2},{2,3},{3,4},{4,5},{5,6},{6,7},{7,8},{8,9},{9,10},{10,1... | collective-permute-start | bytes 1572872 | tf_op jit(solution)/shard_map/ppermute | solution.py:34
  54.3 4.6 %collective-permute-start.3 = (bf16[64,4096]{1,0:T(8,128)(2,1)S(1)}, bf16[64,4096]{1,0:T(8,128)(2,1)S(1)}, u32[]{:S(2)}, u32[]{:S(2)}) collective-permute-start(bf16[64,4096]{1,0:T(8,128)(2,1)S(1)} %pad_maximum_fusion), channel_id=1, source_target_pairs={{0,15},{1,0},{2,1},{3,2},{4,3},{5,4},{6,5},{7,6},{8,7},{9,8},{10,9... | collective-permute-start | bytes 1572872 | tf_op jit(solution)/shard_map/ppermute | solution.py:34
  58.9 0.5 convolution_convert_fusion.11
  59.4 0.5 convolution_convert_fusion.15
  59.9 1.9 collective-permute-start.4
  61.8 6.0 %collective-permute-start.5 = (bf16[64,2048]{1,0:T(8,128)(2,1)S(1)}, bf16[64,2048]{1,0:T(8,128)(2,1)S(1)}, u32[]{:S(2)}, u32[]{:S(2)}) collective-permute-start(bf16[64,2048]{1,0:T(8,128)(2,1)S(1)} %get-tuple-element.23), channel_id=1, source_target_pairs={{0,14},{1,15},{2,0},{3,1},{4,2},{5,3},{6,4},{7,5},{8,6},{9,7},{10,... | collective-permute-start | bytes 786440 | tf_op jit(solution)/shard_map/ppermute | solution.py:34
  67.9 0.2 convolution_bitcast_fusion.3
  68.1 0.3 fusion
  68.4 7.2 %collective-permute-done.4 = bf16[64,2048]{1,0:T(8,128)(2,1)S(1)} collective-permute-done((bf16[64,2048]{1,0:T(8,128)(2,1)S(1)}, bf16[64,2048]{1,0:T(8,128)(2,1)S(1)}, u32[]{:S(2)}, u32[]{:S(2)}) %collective-permute-start.4) | collective-permute-done | bytes 262176 | tf_op jit(solution)/shard_map/ppermute | solution.py:34
  75.6 5.2 %collective-permute-done.5 = bf16[64,2048]{1,0:T(8,128)(2,1)S(1)} collective-permute-done((bf16[64,2048]{1,0:T(8,128)(2,1)S(1)}, bf16[64,2048]{1,0:T(8,128)(2,1)S(1)}, u32[]{:S(2)}, u32[]{:S(2)}) %collective-permute-start.5) | collective-permute-done | bytes 262176 | tf_op jit(solution)/shard_map/ppermute | solution.py:34
  80.9 0.5 convolution_convert_fusion.9
  81.3 0.2 convolution_bitcast_fusion.1
  81.6 0.3 fusion.2
  81.9 0.5 convolution_convert_fusion.13
  82.3 0.3 fusion.3
  82.6 0.3 fusion.1
  83.2 1.3 collective-permute-start.8
  84.5 0.5 convolution_convert_fusion.12
  85.0 0.3 collective-permute-done.8
  85.6 0.8 broadcast_in_dim.8
  86.5 10.8 %all-to-all-start = ((bf16[16,64,256]{2,1,0:T(8,128)(2,1)}), bf16[16,64,256]{2,1,0:T(8,128)(2,1)}, u32[]{:S(2)}, u32[]{:S(2)}) async-start(bf16[16,64,256]{2,1,0:T(8,128)(2,1)} %broadcast_in_dim.8), calls=%async_computation | async-start | bytes 1048576 | tf_op jit(solution)/shard_map/all_to_all | solution.py:29
  97.2 0.5 convolution_convert_fusion.14
  97.7 0.3 convolution_convert_fusion.6.inner_ref
  98.1 3.9 %collective-permute-start.7 = (bf16[3,256]{1,0:T(4,128)(2,1)S(1)}, bf16[3,256]{1,0:T(4,128)(2,1)S(1)}, u32[]{:S(2)}, u32[]{:S(2)}) collective-permute-start(bf16[3,256]{1,0:T(4,128)(2,1)S(1)} %slice.132), channel_id=1, source_target_pairs={{0,16},{16,32},{32,48},{48,64},{64,80},{80,96},{96,112},{1,17},{17... | collective-permute-start | bytes 4616 | tf_op jit(solution)/shard_map/ppermute | solution.py:24
  102.0 0.5 convolution_convert_fusion.8
  102.4 0.5 convolution_convert_fusion.10
  102.9 1.0 convolution_convert_fusion.5.gate_ref
  104.1 0.3 convolution_bitcast_fusion.2
  104.4 0.9 broadcast_multiply_fusion
  105.3 16.9 %all-to-all-done = bf16[16,64,256]{2,1,0:T(8,128)(2,1)} async-done(((bf16[16,64,256]{2,1,0:T(8,128)(2,1)}), bf16[16,64,256]{2,1,0:T(8,128)(2,1)}, u32[]{:S(2)}, u32[]{:S(2)}) %all-to-all-start) | async-done | bytes 524320 | tf_op jit(solution)/shard_map/all_to_all | solution.py:29
  122.2 3.6 %local_scan.1 = (f32[256,256]{1,0:T(8,128)}, bf16[1,144,256]{2,1,0:T(8,128)(2,1)}, f32[256,128]{1,0:T(8,128)}) custom-call(bf16[256,256]{1,0:T(8,128)(2,1)} %copy-done.7, bf16[3,256]{1,0:T(4,128)(2,1)} %copy-done.8, f32[4,256]{1,0:T(4,128)} %taps_ref.1, bf16[1024,256]{1,0:T(8,128)(2,1)} %bitcast.10.states_ref, f32[4,256]{1,0:T(4,128)} %get-tuple-element.29.step_ref, ...), custom_call_target="tpu_custom_call" | custom-call | tf_op jit(solution)/shard_map/local_scan/pallas_call | solution.py:206
  125.8 20.8 %all_gather.3.messages_ref = bf16[8,144,256]{2,1,0:T(8,128)(2,1)} all-gather(bf16[1,144,256]{2,1,0:T(8,128)(2,1)} %get-tuple-element.11), channel_id=1, replica_groups=mesh['dp'=8,'seq'=8,'tp'=16] {'seq'}, dimensions={0}, use_global_device_ids=true | all-gather | bytes 663552 | tf_op jit(solution)/shard_map/all_gather | solution.py:297
  146.6 2.8 %carry_in.1 = (f32[256,256]{1,0:T(8,128)}, f32[1,4,256]{2,1,0:T(4,128)}) custom-call(s32[1]{0:T(128)} %bitcast.1.position_ref, bf16[8,144,256]{2,1,0:T(8,128)(2,1)} %all_gather.3.messages_ref, bf16[1024,256]{1,0:T(8,128)(2,1)} %bitcast.10.states_ref, f32[256,128]{1,0:T(8,128)} %get-tuple-element.12.reach_ref, f32[256,256]{1,0:T(8,128)} %get-tuple-element.13.local_ref, ...), custom_call_target="tpu_custom_call" | custom-call | tf_op jit(solution)/shard_map/carry_in/pallas_call | solution.py:223
  149.4 0.7 broadcast_in_dim.10
  150.1 19.7 %all_to_all.10 = f32[16,4,256]{2,1,0:T(4,128)S(1)} all-to-all(f32[16,4,256]{2,1,0:T(4,128)S(1)} %broadcast_in_dim.10), channel_id=1, replica_groups=mesh['dp'=8,'seq'=8,'tp'=16] {'tp'}, dimensions={0} | all-to-all | bytes 131072 | tf_op jit(solution)/shard_map/all_to_all | solution.py:29
  170.0 1.3 convolution_convert_fusion.4
  171.4 2.1 convolution_convert_fusion
  173.4 0.5 convolution_convert_fusion.1
  173.9 2.9 %collective-permute-start.9 = (bf16[64,4096]{1,0:T(8,128)(2,1)S(1)}, bf16[64,4096]{1,0:T(8,128)(2,1)S(1)}, u32[]{:S(2)}, u32[]{:S(2)}) collective-permute-start(bf16[64,4096]{1,0:T(8,128)(2,1)S(1)} %convolution_convert_fusion.1), channel_id=1, source_target_pairs={{0,1},{1,2},{2,3},{3,4},{4,5},{5,6},{6,7},{7,8},{8,9},{9,10},{10,1... | collective-permute-start | bytes 1572872 | tf_op jit(solution)/shard_map/ppermute | solution.py:34
  176.8 4.2 %collective-permute-start.10 = (bf16[64,4096]{1,0:T(8,128)(2,1)S(1)}, bf16[64,4096]{1,0:T(8,128)(2,1)S(1)}, u32[]{:S(2)}, u32[]{:S(2)}) collective-permute-start(bf16[64,4096]{1,0:T(8,128)(2,1)S(1)} %convolution_convert_fusion), channel_id=1, source_target_pairs={{0,15},{1,0},{2,1},{3,2},{4,3},{5,4},{6,5},{7,6},{8,7},{9,8},{10,9... | collective-permute-start | bytes 1572872 | tf_op jit(solution)/shard_map/ppermute | solution.py:34
  181.0 0.3 convolution_convert_fusion.3
  181.3 2.0 collective-permute-start.12
  183.3 0.3 convolution_convert_fusion.2
  183.6 6.0 %collective-permute-start.11 = (bf16[64,2048]{1,0:T(8,128)(2,1)S(1)}, bf16[64,2048]{1,0:T(8,128)(2,1)S(1)}, u32[]{:S(2)}, u32[]{:S(2)}) collective-permute-start(bf16[64,2048]{1,0:T(8,128)(2,1)S(1)} %convolution_convert_fusion.2), channel_id=1, source_target_pairs={{0,14},{1,15},{2,0},{3,1},{4,2},{5,3},{6,4},{7,5},{8,6},{9,7},{10,... | collective-permute-start | bytes 786440 | tf_op jit(solution)/shard_map/ppermute | solution.py:34
  189.6 10.6 %collective-permute-done.12 = bf16[64,2048]{1,0:T(8,128)(2,1)S(1)} collective-permute-done((bf16[64,2048]{1,0:T(8,128)(2,1)S(1)}, bf16[64,2048]{1,0:T(8,128)(2,1)S(1)}, u32[]{:S(2)}, u32[]{:S(2)}) %collective-permute-start.12) | collective-permute-done | bytes 262176 | tf_op jit(solution)/shard_map/ppermute | solution.py:34
  200.3 2.0 collective-permute-done.11
  202.3 0.6 fusion.65
  203.0 4.9 %collective-permute-start.13 = (bf16[16,4096]{1,0:T(8,128)(2,1)S(1)}, bf16[16,4096]{1,0:T(8,128)(2,1)S(1)}, u32[]{:S(2)}, u32[]{:S(2)}) collective-permute-start(bf16[16,4096]{1,0:T(8,128)(2,1)S(1)} %get-tuple-element.19), channel_id=1, source_target_pairs={{0,8},{1,9},{2,10},{3,11},{4,12},{5,13},{6,14},{7,15},{8,0},{9,1},... | collective-permute-start | bytes 393224 | tf_op jit(solution)/shard_map/ppermute | solution.py:34
  207.9 5.9 %collective-permute-start.15 = (bf16[16,4096]{1,0:T(8,128)(2,1)S(1)}, bf16[16,4096]{1,0:T(8,128)(2,1)S(1)}, u32[]{:S(2)}, u32[]{:S(2)}) collective-permute-start(bf16[16,4096]{1,0:T(8,128)(2,1)S(1)} %get-tuple-element.20), channel_id=1, source_target_pairs={{0,12},{1,13},{2,14},{3,15},{4,0},{5,1},{6,2},{7,3},{8,4},{9,5},{1... | collective-permute-start | bytes 393224 | tf_op jit(solution)/shard_map/ppermute | solution.py:34
  213.8 3.9 %collective-permute-start.14 = (bf16[16,4096]{1,0:T(8,128)(2,1)S(1)}, bf16[16,4096]{1,0:T(8,128)(2,1)S(1)}, u32[]{:S(2)}, u32[]{:S(2)}) collective-permute-start(bf16[16,4096]{1,0:T(8,128)(2,1)S(1)} %get-tuple-element.21), channel_id=1, source_target_pairs={{0,4},{1,5},{2,6},{3,7},{4,8},{5,9},{6,10},{7,11},{8,12},{9,13},{1... | collective-permute-start | bytes 393224 | tf_op jit(solution)/shard_map/ppermute | solution.py:34
  217.7 3.1 %collective-permute-done.13 = bf16[16,4096]{1,0:T(8,128)(2,1)S(1)} collective-permute-done((bf16[16,4096]{1,0:T(8,128)(2,1)S(1)}, bf16[16,4096]{1,0:T(8,128)(2,1)S(1)}, u32[]{:S(2)}, u32[]{:S(2)}) %collective-permute-start.13) | collective-permute-done | bytes 131104 | tf_op jit(solution)/shard_map/ppermute | solution.py:34
  220.8 11.3 %collective-permute-done.15 = bf16[16,4096]{1,0:T(8,128)(2,1)S(1)} collective-permute-done((bf16[16,4096]{1,0:T(8,128)(2,1)S(1)}, bf16[16,4096]{1,0:T(8,128)(2,1)S(1)}, u32[]{:S(2)}, u32[]{:S(2)}) %collective-permute-start.15) | collective-permute-done | bytes 131104 | tf_op jit(solution)/shard_map/ppermute | solution.py:34
  232.2 0.7 fusion.9
  (59 shorter events, 1.5 us)
Async XLA Ops:
  0.0 59.4 %copy-start = (bf16[4096,256]{1,0:T(8,128)(2,1)S(1)}, bf16[4096,256]{1,0:T(8,128)(2,1)}, u32[]{:S(2)}) copy-start(bf16[4096,256]{1,0:T(8,128)(2,1)} %param.16) | copy-start | bytes 6291460
  2.2 32.4 %collective-permute-start.2 = (bf16[16,4096]{1,0:T(8,128)(2,1)S(1)}, bf16[16,4096]{1,0:T(8,128)(2,1)S(1)}, u32[]{:S(2)}, u32[]{:S(2)}) collective-permute-start(bf16[16,4096]{1,0:T(8,128)(2,1)S(1)} %fusion.8), channel_id=1, source_target_pairs={{0,4},{1,5},{2,6},{3,7},{4,8},{5,9},{6,10},{7,11},{8,12},{9,13},{1... | collective-permute-start | bytes 393224 | tf_op jit(solution)/shard_map/ppermute | solution.py:34
  13.2 34.2 %collective-permute-start.1 = (bf16[16,4096]{1,0:T(8,128)(2,1)S(1)}, bf16[16,4096]{1,0:T(8,128)(2,1)S(1)}, u32[]{:S(2)}, u32[]{:S(2)}) collective-permute-start(bf16[16,4096]{1,0:T(8,128)(2,1)S(1)} %fusion.8), channel_id=1, source_target_pairs={{0,8},{1,9},{2,10},{3,11},{4,12},{5,13},{6,14},{7,15},{8,0},{9,1},... | collective-permute-start | bytes 393224 | tf_op jit(solution)/shard_map/ppermute | solution.py:34
  27.7 24.0 %collective-permute-start = (bf16[16,4096]{1,0:T(8,128)(2,1)S(1)}, bf16[16,4096]{1,0:T(8,128)(2,1)S(1)}, u32[]{:S(2)}, u32[]{:S(2)}) collective-permute-start(bf16[16,4096]{1,0:T(8,128)(2,1)S(1)} %fusion.8), channel_id=1, source_target_pairs={{0,12},{1,13},{2,14},{3,15},{4,0},{5,1},{6,2},{7,3},{8,4},{9,5},{1... | collective-permute-start | bytes 393224 | tf_op jit(solution)/shard_map/ppermute | solution.py:34
  33.1 25.8 %copy-start.2 = (bf16[4096,256]{1,0:T(8,128)(2,1)S(1)}, bf16[4096,256]{1,0:T(8,128)(2,1)}, u32[]{:S(2)}) copy-start(bf16[4096,256]{1,0:T(8,128)(2,1)} %param.17) | copy-start | bytes 6291460
  51.8 16.0 %copy-start.6 = (bf16[4096,4]{0,1:T(4,128)(2,1)S(1)}, bf16[4096,4]{0,1:T(4,128)(2,1)}, u32[]{:S(2)}) copy-start(bf16[4096,4]{0,1:T(4,128)(2,1)} %param.19) | copy-start | bytes 98308
  51.8 30.5 %collective-permute-start.6 = (bf16[64,4096]{1,0:T(8,128)(2,1)S(1)}, bf16[64,4096]{1,0:T(8,128)(2,1)S(1)}, u32[]{:S(2)}, u32[]{:S(2)}) collective-permute-start(bf16[64,4096]{1,0:T(8,128)(2,1)S(1)} %pad_maximum_fusion), channel_id=1, source_target_pairs={{0,1},{1,2},{2,3},{3,4},{4,5},{5,6},{6,7},{7,8},{8,9},{9,10},{10,1... | collective-permute-start | bytes 1572872 | tf_op jit(solution)/shard_map/ppermute | solution.py:34
  54.3 28.3 %collective-permute-start.3 = (bf16[64,4096]{1,0:T(8,128)(2,1)S(1)}, bf16[64,4096]{1,0:T(8,128)(2,1)S(1)}, u32[]{:S(2)}, u32[]{:S(2)}) collective-permute-start(bf16[64,4096]{1,0:T(8,128)(2,1)S(1)} %pad_maximum_fusion), channel_id=1, source_target_pairs={{0,15},{1,0},{2,1},{3,2},{4,3},{5,4},{6,5},{7,6},{8,7},{9,8},{10,9... | collective-permute-start | bytes 1572872 | tf_op jit(solution)/shard_map/ppermute | solution.py:34
  59.4 8.7 %copy-start.4 = (bf16[4096,64]{0,1:T(8,128)(2,1)S(1)}, bf16[4096,64]{0,1:T(8,128)(2,1)}, u32[]{:S(2)}) copy-start(bf16[4096,64]{0,1:T(8,128)(2,1)} %param.18) | copy-start | bytes 1572868
  59.9 15.7 %collective-permute-start.4 = (bf16[64,2048]{1,0:T(8,128)(2,1)S(1)}, bf16[64,2048]{1,0:T(8,128)(2,1)S(1)}, u32[]{:S(2)}, u32[]{:S(2)}) collective-permute-start(bf16[64,2048]{1,0:T(8,128)(2,1)S(1)} %get-tuple-element.22), channel_id=1, source_target_pairs={{0,2},{1,3},{2,4},{3,5},{4,6},{5,7},{6,8},{7,9},{8,10},{9,11},{10,... | collective-permute-start | bytes 786440 | tf_op jit(solution)/shard_map/ppermute | solution.py:34
  61.8 19.0 %collective-permute-start.5 = (bf16[64,2048]{1,0:T(8,128)(2,1)S(1)}, bf16[64,2048]{1,0:T(8,128)(2,1)S(1)}, u32[]{:S(2)}, u32[]{:S(2)}) collective-permute-start(bf16[64,2048]{1,0:T(8,128)(2,1)S(1)} %get-tuple-element.23), channel_id=1, source_target_pairs={{0,14},{1,15},{2,0},{3,1},{4,2},{5,3},{6,4},{7,5},{8,6},{9,7},{10,... | collective-permute-start | bytes 786440 | tf_op jit(solution)/shard_map/ppermute | solution.py:34
  83.2 2.1 collective-permute-start.8
  86.5 35.7 %all-to-all-start = ((bf16[16,64,256]{2,1,0:T(8,128)(2,1)}), bf16[16,64,256]{2,1,0:T(8,128)(2,1)}, u32[]{:S(2)}, u32[]{:S(2)}) async-start(bf16[16,64,256]{2,1,0:T(8,128)(2,1)} %broadcast_in_dim.8), calls=%async_computation | async-start | bytes 1048576 | tf_op jit(solution)/shard_map/all_to_all | solution.py:29
  97.2 4.7 %copy-start.3 = (bf16[4096,256]{1,0:T(8,128)(2,1)S(1)}, bf16[4096,256]{1,0:T(8,128)(2,1)}, u32[]{:S(2)}) copy-start(bf16[4096,256]{1,0:T(8,128)(2,1)} %param.17) | copy-start | bytes 6291460
  98.0 4.9 %copy-start.7 = (bf16[256,256]{1,0:T(8,128)(2,1)}, bf16[256,256]{1,0:T(8,128)(2,1)S(1)}, u32[]{:S(2)}) copy-start(bf16[256,256]{1,0:T(8,128)(2,1)S(1)} %convolution_convert_fusion.6.inner_ref) | copy-start | bytes 393220
  98.1 7.2 %collective-permute-start.7 = (bf16[3,256]{1,0:T(4,128)(2,1)S(1)}, bf16[3,256]{1,0:T(4,128)(2,1)S(1)}, u32[]{:S(2)}, u32[]{:S(2)}) collective-permute-start(bf16[3,256]{1,0:T(4,128)(2,1)S(1)} %slice.132), channel_id=1, source_target_pairs={{0,16},{16,32},{32,48},{48,64},{64,80},{80,96},{96,112},{1,17},{17... | collective-permute-start | bytes 4616 | tf_op jit(solution)/shard_map/ppermute | solution.py:24
  102.4 2.0 copy-start.10
  104.4 65.6 %copy-start.9 = (f32[256]{0:T(256)S(1)}, f32[256]{0:T(256)}, u32[]{:S(2)}) copy-start(f32[256]{0:T(256)} %param.25) | copy-start | bytes 3076
  105.3 16.9 %copy-start.8 = (bf16[3,256]{1,0:T(4,128)(2,1)}, bf16[3,256]{1,0:T(4,128)(2,1)S(1)}, u32[]{:S(2)}) copy-start(bf16[3,256]{1,0:T(4,128)(2,1)S(1)} %collective-permute-done.7.halo_ref) | copy-start | bytes 4612
  170.0 3.4 %copy-start.1 = (bf16[256,4096]{1,0:T(8,128)(2,1)S(1)}, bf16[256,4096]{1,0:T(8,128)(2,1)}, u32[]{:S(2)}) copy-start(bf16[256,4096]{1,0:T(8,128)(2,1)} %param.26) | copy-start | bytes 6291460
  173.9 28.4 %collective-permute-start.9 = (bf16[64,4096]{1,0:T(8,128)(2,1)S(1)}, bf16[64,4096]{1,0:T(8,128)(2,1)S(1)}, u32[]{:S(2)}, u32[]{:S(2)}) collective-permute-start(bf16[64,4096]{1,0:T(8,128)(2,1)S(1)} %convolution_convert_fusion.1), channel_id=1, source_target_pairs={{0,1},{1,2},{2,3},{3,4},{4,5},{5,6},{6,7},{7,8},{8,9},{9,10},{10,1... | collective-permute-start | bytes 1572872 | tf_op jit(solution)/shard_map/ppermute | solution.py:34
  176.8 25.5 %collective-permute-start.10 = (bf16[64,4096]{1,0:T(8,128)(2,1)S(1)}, bf16[64,4096]{1,0:T(8,128)(2,1)S(1)}, u32[]{:S(2)}, u32[]{:S(2)}) collective-permute-start(bf16[64,4096]{1,0:T(8,128)(2,1)S(1)} %convolution_convert_fusion), channel_id=1, source_target_pairs={{0,15},{1,0},{2,1},{3,2},{4,3},{5,4},{6,5},{7,6},{8,7},{9,8},{10,9... | collective-permute-start | bytes 1572872 | tf_op jit(solution)/shard_map/ppermute | solution.py:34
  181.3 18.9 %collective-permute-start.12 = (bf16[64,2048]{1,0:T(8,128)(2,1)S(1)}, bf16[64,2048]{1,0:T(8,128)(2,1)S(1)}, u32[]{:S(2)}, u32[]{:S(2)}) collective-permute-start(bf16[64,2048]{1,0:T(8,128)(2,1)S(1)} %convolution_convert_fusion.3), channel_id=1, source_target_pairs={{0,2},{1,3},{2,4},{3,5},{4,6},{5,7},{6,8},{7,9},{8,10},{9,11},{10,... | collective-permute-start | bytes 786440 | tf_op jit(solution)/shard_map/ppermute | solution.py:34
  183.6 18.7 %collective-permute-start.11 = (bf16[64,2048]{1,0:T(8,128)(2,1)S(1)}, bf16[64,2048]{1,0:T(8,128)(2,1)S(1)}, u32[]{:S(2)}, u32[]{:S(2)}) collective-permute-start(bf16[64,2048]{1,0:T(8,128)(2,1)S(1)} %convolution_convert_fusion.2), channel_id=1, source_target_pairs={{0,14},{1,15},{2,0},{3,1},{4,2},{5,3},{6,4},{7,5},{8,6},{9,7},{10,... | collective-permute-start | bytes 786440 | tf_op jit(solution)/shard_map/ppermute | solution.py:34
  189.6 42.5 %copy-start.5 = (bf16[16,4096]{1,0:T(8,128)(2,1)S(1)}, bf16[16,4096]{1,0:T(8,128)(2,1)}, u32[]{:S(2)}) copy-start(bf16[16,4096]{1,0:T(8,128)(2,1)} %param.14) | copy-start | bytes 393220
  203.0 17.8 %collective-permute-start.13 = (bf16[16,4096]{1,0:T(8,128)(2,1)S(1)}, bf16[16,4096]{1,0:T(8,128)(2,1)S(1)}, u32[]{:S(2)}, u32[]{:S(2)}) collective-permute-start(bf16[16,4096]{1,0:T(8,128)(2,1)S(1)} %get-tuple-element.19), channel_id=1, source_target_pairs={{0,8},{1,9},{2,10},{3,11},{4,12},{5,13},{6,14},{7,15},{8,0},{9,1},... | collective-permute-start | bytes 393224 | tf_op jit(solution)/shard_map/ppermute | solution.py:34
  207.9 24.2 %collective-permute-start.15 = (bf16[16,4096]{1,0:T(8,128)(2,1)S(1)}, bf16[16,4096]{1,0:T(8,128)(2,1)S(1)}, u32[]{:S(2)}, u32[]{:S(2)}) collective-permute-start(bf16[16,4096]{1,0:T(8,128)(2,1)S(1)} %get-tuple-element.20), channel_id=1, source_target_pairs={{0,12},{1,13},{2,14},{3,15},{4,0},{5,1},{6,2},{7,3},{8,4},{9,5},{1... | collective-permute-start | bytes 393224 | tf_op jit(solution)/shard_map/ppermute | solution.py:34
  213.8 18.3 %collective-permute-start.14 = (bf16[16,4096]{1,0:T(8,128)(2,1)S(1)}, bf16[16,4096]{1,0:T(8,128)(2,1)S(1)}, u32[]{:S(2)}, u32[]{:S(2)}) collective-permute-start(bf16[16,4096]{1,0:T(8,128)(2,1)S(1)} %get-tuple-element.21), channel_id=1, source_target_pairs={{0,4},{1,5},{2,6},{3,7},{4,8},{5,9},{6,10},{7,11},{8,12},{9,13},{1... | collective-permute-start | bytes 393224 | tf_op jit(solution)/shard_map/ppermute | solution.py:34

commit v6 on v5

--- a/solution.py
+++ b/solution.py
@@ -110,19 +110,20 @@
     )
 
 
-def local_scan_kernel(
-    inner_ref, halo_ref, taps_ref, states_ref, step_ref, decay_ref, skip_ref,
-    local_ref, message_ref, reach_ref, padded,
+def prepare_kernel(
+    inner_ref, halo_ref, taps_ref, step_ref, decay_ref, gate_ref,
+    mixed_ref, scaled_ref, table_ref, reach_ref, total_ref, gate_out_ref, padded,
 ):
-    length = inner_ref.shape[0]
+    length, width = inner_ref.shape
     margin = TAPS - 1
     padded[TAIL_ROWS - margin : TAIL_ROWS, :] = halo_ref[...].astype(jnp.float32)
     padded[TAIL_ROWS:, :] = inner_ref[...].astype(jnp.float32)
-    conv = jnp.zeros(inner_ref.shape, jnp.float32)
+    conv = jnp.zeros((length, width), jnp.float32)
     for tap in range(TAPS):
         start = TAIL_ROWS - margin + tap
         conv = conv + taps_ref[tap : tap + 1, :] * padded[start : start + length, :]
     mixed = (conv / (1.0 + jnp.exp(-conv))).astype(jnp.bfloat16)
+    mixed_ref[...] = mixed
     rows = lax.broadcasted_iota(jnp.int32, (length, length), 0)
     cols = lax.broadcasted_iota(jnp.int32, (length, length), 1)
     lower_mask = rows >= cols
@@ -136,11 +137,26 @@
     )
     reach = reach_rows.T
     step = jnp.concatenate((step_rows, blank), axis=0).T
-    reach_ref[...] = reach
     final = reach[length - 1 :, :]
     tail = jnp.exp(final - reach) * step
-    mixed_wide = mixed.astype(jnp.float32)
-    scaled = mixed_wide * head_lanes(tail, HEAD_DIM)
+    scaled_ref[...] = mixed.astype(jnp.float32) * head_lanes(tail, HEAD_DIM)
+    reach_ref[...] = head_lanes(jnp.exp(reach), HEAD_DIM)
+    for g in range(GROUPS):
+        spread = jnp.where(lower_mask, reach[:, g : g + 1] - reach_rows[g : g + 1, :], 0.0)
+        decay_table = jnp.where(lower_mask, jnp.exp(spread), 0.0)
+        table_ref[g] = decay_table * step_rows[g : g + 1, :]
+    total = head_lanes(final, HEAD_DIM)
+    upper = total.astype(jnp.bfloat16)
+    lower = (total - upper.astype(jnp.float32)).astype(jnp.bfloat16)
+    zeros = jnp.zeros((TAIL_ROWS - 1, width), jnp.bfloat16)
+    total_ref[...] = jnp.concatenate((upper, zeros, lower, zeros), axis=0)
+    gate = gate_ref[...].astype(jnp.float32)
+    gate_out_ref[...] = gate / (1.0 + jnp.exp(-gate))
+
+
+def local_scan_kernel(
+    mixed_ref, scaled_ref, table_ref, total_ref, skip_ref, states_ref, local_ref, message_ref
+):
     outs = []
     ends = []
     for g in range(GROUPS):
@@ -150,40 +166,42 @@
         scores = lax.dot_general(
             out_states, in_states, (((0,), (0,)), ((), ())), preferred_element_type=jnp.float32
         )
-        spread = jnp.where(lower_mask, reach[:, g : g + 1] - reach_rows[g : g + 1, :], 0.0)
-        decay_table = jnp.where(lower_mask, jnp.exp(spread), 0.0)
-        weights = scores * decay_table * step_rows[g : g + 1, :]
-        outs.append(split_dot(mixed[:, low : low + HEAD_DIM], weights, ((1,), (0,)), False))
-        ends.append(split_dot(in_states, scaled[:, low : low + HEAD_DIM], ((1,), (0,)), True))
+        weights = scores * table_ref[g]
+        outs.append(split_dot(mixed_ref[:, low : low + HEAD_DIM], weights, ((1,), (0,)), False))
+        ends.append(split_dot(in_states, scaled_ref[:, low : low + HEAD_DIM], ((1,), (0,)), True))
+    mixed_wide = mixed_ref[...].astype(jnp.float32)
     local_ref[...] = jnp.concatenate(outs, axis=1) + skip_ref[...] * mixed_wide
-    message_ref[0, :STATE, :] = jnp.concatenate(ends, axis=1).astype(jnp.bfloat16)
-    total = head_lanes(final, HEAD_DIM)
-    upper = total.astype(jnp.bfloat16)
-    lower = (total - upper.astype(jnp.float32)).astype(jnp.bfloat16)
-    zeros = jnp.zeros((TAIL_ROWS - 1, total.shape[1]), jnp.bfloat16)
-    message_ref[0, STATE : STATE + TAIL_ROWS, :] = jnp.concatenate((upper, zeros), axis=0)
-    message_ref[0, STATE + TAIL_ROWS :, :] = jnp.concatenate((lower, zeros), axis=0)
+    message_ref[:STATE, :] = jnp.concatenate(ends, axis=1).astype(jnp.bfloat16)
+    message_ref[STATE:, :] = total_ref[...]
 
 
 def carry_kernel(
-    position_ref, messages_ref, states_ref, reach_ref, local_ref, gate_ref, gated_ref, squares_ref
+    core_ref, near_ref, mid_ref, far_ref, partner_ref, states_ref, reach_ref, local_ref, gate_ref,
+    gated_ref, squares_ref,
 ):
-    position = position_ref[0]
+    core = core_ref[0]
     width = local_ref.shape[1]
+
+    def moved(message, carry):
+        total = message[STATE : STATE + TAIL_ROWS, :].astype(jnp.float32)
+        total = total + message[STATE + TAIL_ROWS :, :].astype(jnp.float32)
+        return jnp.exp(total[:1, :]) * carry + message[:STATE, :].astype(jnp.float32)
+
     carry = jnp.zeros((STATE, width), jnp.float32)
-    for k in range(messages_ref.shape[0] - 1):
-        total = messages_ref[k, STATE : STATE + TAIL_ROWS, :].astype(jnp.float32)
-        total = total + messages_ref[k, STATE + TAIL_ROWS :, :].astype(jnp.float32)
-        moved = jnp.exp(total[:1, :]) * carry + messages_ref[k, :STATE, :].astype(jnp.float32)
-        carry = jnp.where(k < position, moved, carry)
+    for pair_ref in (far_ref, mid_ref, near_ref):
+        own = pair_ref[0]
+        other = pair_ref[1]
+        first = jnp.where(core == 0, own, other)
+        second = jnp.where(core == 0, other, own)
+        carry = moved(second, moved(first, carry))
+    carry = jnp.where(core == 1, moved(partner_ref[...], carry), carry)
     outs = []
     for g in range(GROUPS):
         low = g * HEAD_DIM
         out_states = states_ref[(2 * g + 1) * STATE : (2 * g + 2) * STATE, :]
         outs.append(split_dot(out_states, carry[:, low : low + HEAD_DIM], ((0,), (0,)), True))
-    carried = jnp.concatenate(outs, axis=1) * head_lanes(jnp.exp(reach_ref[...]), HEAD_DIM)
-    gate = gate_ref[...].astype(jnp.float32)
-    gated = (local_ref[...] + carried) * (gate / (1.0 + jnp.exp(-gate)))
+    carried = jnp.concatenate(outs, axis=1) * reach_ref[...]
+    gated = (local_ref[...] + carried) * gate_ref[...]
     gated_ref[...] = gated
     owner = lax.broadcasted_iota(jnp.int32, (TAIL_ROWS, width), 1) // HEAD_DIM
     heads = lax.broadcasted_iota(jnp.int32, (TAIL_ROWS, width), 0)
@@ -194,43 +212,62 @@
         precision=highest,
         preferred_element_type=jnp.float32,
     )
-    squares_ref[0] = sums[:GROUPS, :]
+    squares_ref[...] = sums[:GROUPS, :]
 
 
 def in_vmem(count):
     return [pl.BlockSpec(memory_space=pltpu.VMEM)] * count
 
 
-def local_scan(inner, halo, taps, states, step, decay, skip, interpret=False):
+def prepare(inner, halo, taps, step, decay, gate, interpret=False):
     length, width = inner.shape
+    wide = jax.ShapeDtypeStruct((length, width), jnp.float32)
+    return pl.pallas_call(
+        prepare_kernel,
+        out_shape=(
+            jax.ShapeDtypeStruct((length, width), jnp.bfloat16),
+            wide,
+            jax.ShapeDtypeStruct((GROUPS, length, length), jnp.float32),
+            wide,
+            jax.ShapeDtypeStruct((2 * TAIL_ROWS, width), jnp.bfloat16),
+            wide,
+        ),
+        in_specs=in_vmem(6),
+        out_specs=tuple(in_vmem(6)),
+        scratch_shapes=[pltpu.VMEM((length + TAIL_ROWS, width), jnp.float32)],
+        interpret=interpret,
+        name="prepare",
+    )(inner, halo, taps, step, decay, gate)
+
+
+def local_scan(mixed, scaled, table, total, skip, states, interpret=False):
+    length, width = mixed.shape
     return pl.pallas_call(
         local_scan_kernel,
         out_shape=(
             jax.ShapeDtypeStruct((length, width), jnp.float32),
-            jax.ShapeDtypeStruct((1, STATE + 2 * TAIL_ROWS, width), jnp.bfloat16),
-            jax.ShapeDtypeStruct((length, 128), jnp.float32),
+            jax.ShapeDtypeStruct((STATE + 2 * TAIL_ROWS, width), jnp.bfloat16),
         ),
-        in_specs=in_vmem(7),
-        out_specs=tuple(in_vmem(3)),
-        scratch_shapes=[pltpu.VMEM((length + TAIL_ROWS, width), jnp.float32)],
+        in_specs=in_vmem(6),
+        out_specs=tuple(in_vmem(2)),
         interpret=interpret,
         name="local_scan",
-    )(inner, halo, taps, states, step, decay, skip)
-
-
-def carry_in(position, messages, states, reach, local, gate, interpret=False):
+    )(mixed, scaled, table, total, skip, states)
+
+
+def carry_in(core, near, mid, far, partner, states, reach, local, gate, interpret=False):
     length, width = local.shape
     return pl.pallas_call(
         carry_kernel,
         out_shape=(
             jax.ShapeDtypeStruct((length, width), jnp.float32),
-            jax.ShapeDtypeStruct((1, GROUPS, length), jnp.float32),
+            jax.ShapeDtypeStruct((GROUPS, length), jnp.float32),
         ),
-        in_specs=[pl.BlockSpec(memory_space=pltpu.SMEM)] + in_vmem(5),
+        in_specs=[pl.BlockSpec(memory_space=pltpu.SMEM)] + in_vmem(8),
         out_specs=tuple(in_vmem(2)),
         interpret=interpret,
         name="carry_in",
-    )(position, messages, states, reach, local, gate)
+    )(core, near, mid, far, partner, states, reach, local, gate)
 
 
 def body(
@@ -291,13 +328,19 @@
     mixed_local = jax.nn.silu(mixed_local).astype(jnp.bfloat16)
     mixed_all = from_everyone(mixed_local, "tp").reshape(-1, row_count)
     skip_row = jnp.repeat(skip_gain, HEAD_DIM)[None]
-    local, message, reach = local_scan(
-        inner_proj, before_inner, conv_inner, mixed_all, step_size, log_decay, skip_row
-    )
-    messages = lax.all_gather(message, "seq", axis=0, tiled=True)
-    position = lax.axis_index("seq").astype(jnp.int32).reshape(1)
-    gated_out, head_squares = carry_in(position, messages, mixed_all, reach, local, gate_proj)
-    every_square = from_everyone(head_squares[0], "tp")
+    mixed, scaled, table, reach, total, gate = prepare(
+        inner_proj, before_inner, conv_inner, step_size, log_decay, gate_proj
+    )
+    local, message = local_scan(mixed, scaled, table, total, skip_row, mixed_all)
+    shards = lax.axis_size("seq")
+    partner = lax.ppermute(message, "seq", [(k, k ^ 1) for k in range(shards)])
+    pair = jnp.stack((message, partner))
+    far, mid, near = (from_behind(pair, "seq", steps) for steps in (6, 4, 2))
+    core = (lax.axis_index("seq") % 2).astype(jnp.int32).reshape(1)
+    gated_out, head_squares = carry_in(
+        core, near, mid, far, partner, mixed_all, reach, local, gate
+    )
+    every_square = from_everyone(head_squares, "tp")
     mean_square = jnp.sum(every_square, axis=0) / (GROUP_HEADS * HEAD_DIM)
     scale = jnp.repeat(lax.rsqrt(mean_square + epsilon).T, HEAD_DIM, axis=1)
     mixed_out = (gated_out * scale * norm_gain).astype(jnp.bfloat16)

time: 235 us -> 237 us (level)
  the two profiles are of different devices: /device:TPU:56 before, /device:TPU:61 now
where the time goes in v6:
time: 237 us; the launch traced here: 236 us
  starting transfers between devices  103 us (43%)
  waiting for transfers between devices  80.8 us (34%)
  blocking collectives  17.7 us (7%)
  matrix products  13.4 us (6%)
  Pallas kernels  9.41 us (4%)
  local copies, waits for them, and re-layouts  5.48 us (2%)
  other arithmetic  5.2 us (2%)
    ppermute x14, starting transfers between devices, shifted(): lax.ppermute(x, axis, [(k, (k + steps) % count) for k in range(count)])  70.8 us
    ppermute x14, waiting for transfers between devices, shifted(): lax.ppermute(x, axis, [(k, (k + steps) % count) for k in range(count)])  59.9 us
    all_to_all x1, blocking collectives, from_everyone(): return lax.all_to_all(copies, axis, split_axis=0, concat_axis=0, tiled=True)  17.7 us
    ppermute x5, starting transfers between devices, from_behind(): lax.ppermute(value, axis, [(source, source + steps) for source in range(i...  12.8 us
    all_to_all x1, starting transfers between devices, from_everyone(): return lax.all_to_all(copies, axis, split_axis=0, concat_axis=0, tiled=True)  10.5 us
    all_to_all x1, waiting for transfers between devices, from_everyone(): return lax.all_to_all(copies, axis, split_axis=0, concat_axis=0, tiled=True)  10.3 us
    dot_general x21, matrix products, product(): lax.dot_general(left, right, dims, precision=precision, preferred_element...  9.58 us
    ppermute x5, waiting for transfers between devices, from_behind(): lax.ppermute(value, axis, [(source, source + steps) for source in range(i...  9.44 us
  transfers between devices with their start and end apart: 21, of which 12 were waited for; matrix products, arithmetic and copies ran while one was open for 5% of the time, Pallas kernels for 1%

profile of v6, /device:TPU:61, one launch (start us, length us, event | category | flops | bytes accessed | tf_op | source)
XLA Modules:
  0.0 235.7 jit_solution(12632993742128641575)
XLA Ops:
  0.0 1.2 fusion.6
  1.2 1.0 fusion.8
  2.2 10.6 %collective-permute-start.2 = (bf16[16,4096]{1,0:T(8,128)(2,1)S(1)}, bf16[16,4096]{1,0:T(8,128)(2,1)S(1)}, u32[]{:S(2)}, u32[]{:S(2)}) collective-permute-start(bf16[16,4096]{1,0:T(8,128)(2,1)S(1)} %fusion.8), channel_id=1, source_target_pairs={{0,4},{1,5},{2,6},{3,7},{4,8},{5,9},{6,10},{7,11},{8,12},{9,13},{1... | collective-permute-start | bytes 393224 | tf_op jit(solution)/shard_map/ppermute | solution.py:34
  12.9 14.3 %collective-permute-start.1 = (bf16[16,4096]{1,0:T(8,128)(2,1)S(1)}, bf16[16,4096]{1,0:T(8,128)(2,1)S(1)}, u32[]{:S(2)}, u32[]{:S(2)}) collective-permute-start(bf16[16,4096]{1,0:T(8,128)(2,1)S(1)} %fusion.8), channel_id=1, source_target_pairs={{0,8},{1,9},{2,10},{3,11},{4,12},{5,13},{6,14},{7,15},{8,0},{9,1},... | collective-permute-start | bytes 393224 | tf_op jit(solution)/shard_map/ppermute | solution.py:34
  27.2 3.4 %collective-permute-start = (bf16[16,4096]{1,0:T(8,128)(2,1)S(1)}, bf16[16,4096]{1,0:T(8,128)(2,1)S(1)}, u32[]{:S(2)}, u32[]{:S(2)}) collective-permute-start(bf16[16,4096]{1,0:T(8,128)(2,1)S(1)} %fusion.8), channel_id=1, source_target_pairs={{0,12},{1,13},{2,14},{3,15},{4,0},{5,1},{6,2},{7,3},{8,4},{9,5},{1... | collective-permute-start | bytes 393224 | tf_op jit(solution)/shard_map/ppermute | solution.py:34
  30.9 0.7 broadcast_in_dim.8
  31.6 0.7 broadcast_in_dim_reshape.3.skip_ref
  32.3 0.9 slice_bitcast_fusion.3
  33.2 0.7 exponential_negate_fusion
  33.8 12.6 %collective-permute-done.1 = bf16[16,4096]{1,0:T(8,128)(2,1)S(1)} collective-permute-done((bf16[16,4096]{1,0:T(8,128)(2,1)S(1)}, bf16[16,4096]{1,0:T(8,128)(2,1)S(1)}, u32[]{:S(2)}, u32[]{:S(2)}) %collective-permute-start.1) | collective-permute-done | bytes 131104 | tf_op jit(solution)/shard_map/ppermute | solution.py:34
  46.4 5.0 %collective-permute-done = bf16[16,4096]{1,0:T(8,128)(2,1)S(1)} collective-permute-done((bf16[16,4096]{1,0:T(8,128)(2,1)S(1)}, bf16[16,4096]{1,0:T(8,128)(2,1)S(1)}, u32[]{:S(2)}, u32[]{:S(2)}) %collective-permute-start) | collective-permute-done | bytes 131104 | tf_op jit(solution)/shard_map/ppermute | solution.py:34
  51.5 1.9 collective-permute-start.6
  53.4 4.6 %collective-permute-start.3 = (bf16[64,4096]{1,0:T(8,128)(2,1)S(1)}, bf16[64,4096]{1,0:T(8,128)(2,1)S(1)}, u32[]{:S(2)}, u32[]{:S(2)}) collective-permute-start(bf16[64,4096]{1,0:T(8,128)(2,1)S(1)} %pad_maximum_fusion), channel_id=1, source_target_pairs={{0,15},{1,0},{2,1},{3,2},{4,3},{5,4},{6,5},{7,6},{8,7},{9,8},{10,9... | collective-permute-start | bytes 1572872 | tf_op jit(solution)/shard_map/ppermute | solution.py:34
  58.0 0.5 convolution_convert_fusion.11
  58.5 0.5 convolution_convert_fusion.15
  59.0 1.9 collective-permute-start.4
  60.9 5.5 %collective-permute-start.5 = (bf16[64,2048]{1,0:T(8,128)(2,1)S(1)}, bf16[64,2048]{1,0:T(8,128)(2,1)S(1)}, u32[]{:S(2)}, u32[]{:S(2)}) collective-permute-start(bf16[64,2048]{1,0:T(8,128)(2,1)S(1)} %get-tuple-element.33), channel_id=1, source_target_pairs={{0,14},{1,15},{2,0},{3,1},{4,2},{5,3},{6,4},{7,5},{8,6},{9,7},{10,... | collective-permute-start | bytes 786440 | tf_op jit(solution)/shard_map/ppermute | solution.py:34
  66.9 8.3 %collective-permute-done.4 = bf16[64,2048]{1,0:T(8,128)(2,1)S(1)} collective-permute-done((bf16[64,2048]{1,0:T(8,128)(2,1)S(1)}, bf16[64,2048]{1,0:T(8,128)(2,1)S(1)}, u32[]{:S(2)}, u32[]{:S(2)}) %collective-permute-start.4) | collective-permute-done | bytes 262176 | tf_op jit(solution)/shard_map/ppermute | solution.py:34
  75.2 4.6 %collective-permute-done.5 = bf16[64,2048]{1,0:T(8,128)(2,1)S(1)} collective-permute-done((bf16[64,2048]{1,0:T(8,128)(2,1)S(1)}, bf16[64,2048]{1,0:T(8,128)(2,1)S(1)}, u32[]{:S(2)}, u32[]{:S(2)}) %collective-permute-start.5) | collective-permute-done | bytes 262176 | tf_op jit(solution)/shard_map/ppermute | solution.py:34
  79.8 0.5 convolution_convert_fusion.9
  80.8 0.5 convolution_convert_fusion.13
  82.2 4.4 %collective-permute-start.8 = (bf16[64,3]{1,0:T(8,128)(2,1)S(1)}, bf16[64,3]{1,0:T(8,128)(2,1)S(1)}, u32[]{:S(2)}, u32[]{:S(2)}) collective-permute-start(bf16[64,3]{1,0:T(8,128)(2,1)S(1)} %slice.133), channel_id=1, source_target_pairs={{0,16},{16,32},{32,48},{48,64},{64,80},{80,96},{96,112},{1,17},{17... | collective-permute-start | bytes 1160 | tf_op jit(solution)/shard_map/ppermute | solution.py:24
  86.6 0.5 convolution_convert_fusion.12
  87.1 0.4 collective-permute-done.8
  87.8 0.9 broadcast_in_dim.9
  88.6 10.5 %all-to-all-start = ((bf16[16,64,256]{2,1,0:T(8,128)(2,1)}), bf16[16,64,256]{2,1,0:T(8,128)(2,1)}, u32[]{:S(2)}, u32[]{:S(2)}) async-start(bf16[16,64,256]{2,1,0:T(8,128)(2,1)} %broadcast_in_dim.9), calls=%async_computation | async-start | bytes 1048576 | tf_op jit(solution)/shard_map/all_to_all | solution.py:29
  99.1 0.5 convolution_convert_fusion.14
  99.6 0.3 convolution_convert_fusion.6.inner_ref
  99.9 4.5 %collective-permute-start.7 = (bf16[3,256]{1,0:T(4,128)(2,1)S(1)}, bf16[3,256]{1,0:T(4,128)(2,1)S(1)}, u32[]{:S(2)}, u32[]{:S(2)}) collective-permute-start(bf16[3,256]{1,0:T(4,128)(2,1)S(1)} %slice.132), channel_id=1, source_target_pairs={{0,16},{16,32},{32,48},{48,64},{64,80},{80,96},{96,112},{1,17},{17... | collective-permute-start | bytes 4616 | tf_op jit(solution)/shard_map/ppermute | solution.py:24
  104.4 0.5 convolution_convert_fusion.8
  104.9 0.5 convolution_convert_fusion.10
  105.4 1.0 convolution_convert_fusion.5.gate_ref
  106.8 0.9 broadcast_multiply_fusion
  107.7 0.6 copy-done.12
  108.3 3.2 %prepare.1 = (bf16[256,256]{1,0:T(8,128)(2,1)}, f32[256,256]{1,0:T(8,128)}, f32[4,256,256]{2,1,0:T(8,128)}, f32[256,256]{1,0:T(8,128)}, bf16[16,256]{1,0:T(8,128)(2,1)}, /*index=5*/f32[256,256]{1,0:T(8,128)}) custom-call(bf16[256,256]{1,0:T(8,128)(2,1)} %copy-done.11, bf16[3,256]{1,0:T(4,128)(2,1)} %copy-done.12, f32[4,256]{1,0:T(4,128)} %taps_ref.1, ...), custom_call_target="tpu_custom_call" | custom-call | tf_op jit(solution)/shard_map/prepare/pallas_call | solution.py:225
  111.5 10.3 %all-to-all-done = bf16[16,64,256]{2,1,0:T(8,128)(2,1)} async-done(((bf16[16,64,256]{2,1,0:T(8,128)(2,1)}), bf16[16,64,256]{2,1,0:T(8,128)(2,1)}, u32[]{:S(2)}, u32[]{:S(2)}) %all-to-all-start) | async-done | bytes 524320 | tf_op jit(solution)/shard_map/all_to_all | solution.py:29
  121.9 3.3 %local_scan.1 = (f32[256,256]{1,0:T(8,128)}, bf16[144,256]{1,0:T(8,128)(2,1)}) custom-call(bf16[256,256]{1,0:T(8,128)(2,1)} %get-tuple-element.16.mixed_ref, f32[256,256]{1,0:T(8,128)} %get-tuple-element.17.scaled_ref, f32[4,256,256]{2,1,0:T(8,128)} %get-tuple-element.18.table_ref, bf16[16,256]{1,0:T(8,128)(2,1)} %get-tuple-element.19.total_ref, ...), custom_call_target="tpu_custom_call" | custom-call | tf_op jit(solution)/shard_map/local_scan/pallas_call | solution.py:245
  125.2 9.0 %collective-permute-start.9 = (bf16[144,256]{1,0:T(8,128)(2,1)}, bf16[144,256]{1,0:T(8,128)(2,1)S(1)}, u32[]{:S(2)}, u32[]{:S(2)}) collective-permute-start(bf16[144,256]{1,0:T(8,128)(2,1)} %get-tuple-element.20), channel_id=1, source_target_pairs={{0,16},{16,0},{32,48},{48,32},{64,80},{80,64},{96,112},{112,96},{1... | collective-permute-start | bytes 221192 | tf_op jit(solution)/shard_map/ppermute | solution.py:336
  134.3 1.1 collective-permute-done.9.partner_ref
  135.4 0.9 pad_maximum_fusion.2
  136.3 0.7 collective-permute-start.12
  137.0 1.3 collective-permute-start.11
  138.3 1.9 collective-permute-start.10
  140.2 5.2 %collective-permute-done.11.mid_ref = bf16[2,144,256]{2,1,0:T(8,128)(2,1)S(1)} collective-permute-done((bf16[2,144,256]{2,1,0:T(8,128)(2,1)S(1)}, bf16[2,144,256]{2,1,0:T(8,128)(2,1)S(1)}, u32[]{:S(2)}, u32[]{:S(2)}) %collective-permute-start.11) | collective-permute-done | bytes 147488 | tf_op jit(solution)/shard_map/ppermute | solution.py:24
  145.5 3.8 %collective-permute-done.10.near_ref = bf16[2,144,256]{2,1,0:T(8,128)(2,1)S(1)} collective-permute-done((bf16[2,144,256]{2,1,0:T(8,128)(2,1)S(1)}, bf16[2,144,256]{2,1,0:T(8,128)(2,1)S(1)}, u32[]{:S(2)}, u32[]{:S(2)}) %collective-permute-start.10) | collective-permute-done | bytes 147488 | tf_op jit(solution)/shard_map/ppermute | solution.py:24
  149.3 0.6 copy-done.10
  149.9 2.9 %carry_in.1 = (f32[256,256]{1,0:T(8,128)}, f32[4,256]{1,0:T(4,128)}) custom-call(s32[1]{0:T(128)} %bitcast.1.core_ref, bf16[2,144,256]{2,1,0:T(8,128)(2,1)} %copy-done.10, bf16[2,144,256]{2,1,0:T(8,128)(2,1)} %copy-done.9, bf16[2,144,256]{2,1,0:T(8,128)(2,1)} %copy-done.8, bf16[144,256]{1,0:T(8,128)(2,1)} %copy-done.7, ...), custom_call_target="tpu_custom_call" | custom-call | tf_op jit(solution)/shard_map/carry_in/pallas_call | solution.py:260
  152.8 0.7 broadcast_in_dim.10
  153.5 17.7 %all_to_all.10 = f32[16,4,256]{2,1,0:T(4,128)S(1)} all-to-all(f32[16,4,256]{2,1,0:T(4,128)S(1)} %broadcast_in_dim.10), channel_id=1, replica_groups=mesh['dp'=8,'seq'=8,'tp'=16] {'tp'}, dimensions={0} | all-to-all | bytes 131072 | tf_op jit(solution)/shard_map/all_to_all | solution.py:29
  171.5 1.3 convolution_convert_fusion.4
  172.8 2.1 convolution_convert_fusion
  174.9 0.5 convolution_convert_fusion.1
  175.4 2.8 %collective-permute-start.13 = (bf16[64,4096]{1,0:T(8,128)(2,1)S(1)}, bf16[64,4096]{1,0:T(8,128)(2,1)S(1)}, u32[]{:S(2)}, u32[]{:S(2)}) collective-permute-start(bf16[64,4096]{1,0:T(8,128)(2,1)S(1)} %convolution_convert_fusion.1), channel_id=1, source_target_pairs={{0,1},{1,2},{2,3},{3,4},{4,5},{5,6},{6,7},{7,8},{8,9},{9,10},{10,1... | collective-permute-start | bytes 1572872 | tf_op jit(solution)/shard_map/ppermute | solution.py:34
  178.2 3.7 %collective-permute-start.14 = (bf16[64,4096]{1,0:T(8,128)(2,1)S(1)}, bf16[64,4096]{1,0:T(8,128)(2,1)S(1)}, u32[]{:S(2)}, u32[]{:S(2)}) collective-permute-start(bf16[64,4096]{1,0:T(8,128)(2,1)S(1)} %convolution_convert_fusion), channel_id=1, source_target_pairs={{0,15},{1,0},{2,1},{3,2},{4,3},{5,4},{6,5},{7,6},{8,7},{9,8},{10,9... | collective-permute-start | bytes 1572872 | tf_op jit(solution)/shard_map/ppermute | solution.py:34
  182.2 1.9 collective-permute-start.16
  184.5 5.5 %collective-permute-start.15 = (bf16[64,2048]{1,0:T(8,128)(2,1)S(1)}, bf16[64,2048]{1,0:T(8,128)(2,1)S(1)}, u32[]{:S(2)}, u32[]{:S(2)}) collective-permute-start(bf16[64,2048]{1,0:T(8,128)(2,1)S(1)} %convolution_convert_fusion.2), channel_id=1, source_target_pairs={{0,14},{1,15},{2,0},{3,1},{4,2},{5,3},{6,4},{7,5},{8,6},{9,7},{10,... | collective-permute-start | bytes 786440 | tf_op jit(solution)/shard_map/ppermute | solution.py:34
  190.0 7.3 %collective-permute-done.16 = bf16[64,2048]{1,0:T(8,128)(2,1)S(1)} collective-permute-done((bf16[64,2048]{1,0:T(8,128)(2,1)S(1)}, bf16[64,2048]{1,0:T(8,128)(2,1)S(1)}, u32[]{:S(2)}, u32[]{:S(2)}) %collective-permute-start.16) | collective-permute-done | bytes 262176 | tf_op jit(solution)/shard_map/ppermute | solution.py:34
  197.3 4.9 %collective-permute-done.15 = bf16[64,2048]{1,0:T(8,128)(2,1)S(1)} collective-permute-done((bf16[64,2048]{1,0:T(8,128)(2,1)S(1)}, bf16[64,2048]{1,0:T(8,128)(2,1)S(1)}, u32[]{:S(2)}, u32[]{:S(2)}) %collective-permute-start.15) | collective-permute-done | bytes 262176 | tf_op jit(solution)/shard_map/ppermute | solution.py:34
  202.2 0.6 fusion.65
  202.9 5.6 %collective-permute-start.17 = (bf16[16,4096]{1,0:T(8,128)(2,1)S(1)}, bf16[16,4096]{1,0:T(8,128)(2,1)S(1)}, u32[]{:S(2)}, u32[]{:S(2)}) collective-permute-start(bf16[16,4096]{1,0:T(8,128)(2,1)S(1)} %get-tuple-element.29), channel_id=1, source_target_pairs={{0,8},{1,9},{2,10},{3,11},{4,12},{5,13},{6,14},{7,15},{8,0},{9,1},... | collective-permute-start | bytes 393224 | tf_op jit(solution)/shard_map/ppermute | solution.py:34
  208.5 5.7 %collective-permute-start.19 = (bf16[16,4096]{1,0:T(8,128)(2,1)S(1)}, bf16[16,4096]{1,0:T(8,128)(2,1)S(1)}, u32[]{:S(2)}, u32[]{:S(2)}) collective-permute-start(bf16[16,4096]{1,0:T(8,128)(2,1)S(1)} %get-tuple-element.30), channel_id=1, source_target_pairs={{0,12},{1,13},{2,14},{3,15},{4,0},{5,1},{6,2},{7,3},{8,4},{9,5},{1... | collective-permute-start | bytes 393224 | tf_op jit(solution)/shard_map/ppermute | solution.py:34
  214.2 3.5 %collective-permute-start.18 = (bf16[16,4096]{1,0:T(8,128)(2,1)S(1)}, bf16[16,4096]{1,0:T(8,128)(2,1)S(1)}, u32[]{:S(2)}, u32[]{:S(2)}) collective-permute-start(bf16[16,4096]{1,0:T(8,128)(2,1)S(1)} %get-tuple-element.31), channel_id=1, source_target_pairs={{0,4},{1,5},{2,6},{3,7},{4,8},{5,9},{6,10},{7,11},{8,12},{9,13},{1... | collective-permute-start | bytes 393224 | tf_op jit(solution)/shard_map/ppermute | solution.py:34
  217.7 17.2 %collective-permute-done.19 = bf16[16,4096]{1,0:T(8,128)(2,1)S(1)} collective-permute-done((bf16[16,4096]{1,0:T(8,128)(2,1)S(1)}, bf16[16,4096]{1,0:T(8,128)(2,1)S(1)}, u32[]{:S(2)}, u32[]{:S(2)}) %collective-permute-start.19) | collective-permute-done | bytes 131104 | tf_op jit(solution)/shard_map/ppermute | solution.py:34
  234.9 0.7 fusion.9
  (76 shorter events, 4.1 us)
Async XLA Ops:
  0.0 58.5 %copy-start = (bf16[4096,256]{1,0:T(8,128)(2,1)S(1)}, bf16[4096,256]{1,0:T(8,128)(2,1)}, u32[]{:S(2)}) copy-start(bf16[4096,256]{1,0:T(8,128)(2,1)} %param.16) | copy-start | bytes 6291460
  2.2 31.6 %collective-permute-start.2 = (bf16[16,4096]{1,0:T(8,128)(2,1)S(1)}, bf16[16,4096]{1,0:T(8,128)(2,1)S(1)}, u32[]{:S(2)}, u32[]{:S(2)}) collective-permute-start(bf16[16,4096]{1,0:T(8,128)(2,1)S(1)} %fusion.8), channel_id=1, source_target_pairs={{0,4},{1,5},{2,6},{3,7},{4,8},{5,9},{6,10},{7,11},{8,12},{9,13},{1... | collective-permute-start | bytes 393224 | tf_op jit(solution)/shard_map/ppermute | solution.py:34
  12.9 33.5 %collective-permute-start.1 = (bf16[16,4096]{1,0:T(8,128)(2,1)S(1)}, bf16[16,4096]{1,0:T(8,128)(2,1)S(1)}, u32[]{:S(2)}, u32[]{:S(2)}) collective-permute-start(bf16[16,4096]{1,0:T(8,128)(2,1)S(1)} %fusion.8), channel_id=1, source_target_pairs={{0,8},{1,9},{2,10},{3,11},{4,12},{5,13},{6,14},{7,15},{8,0},{9,1},... | collective-permute-start | bytes 393224 | tf_op jit(solution)/shard_map/ppermute | solution.py:34
  27.2 24.2 %collective-permute-start = (bf16[16,4096]{1,0:T(8,128)(2,1)S(1)}, bf16[16,4096]{1,0:T(8,128)(2,1)S(1)}, u32[]{:S(2)}, u32[]{:S(2)}) collective-permute-start(bf16[16,4096]{1,0:T(8,128)(2,1)S(1)} %fusion.8), channel_id=1, source_target_pairs={{0,12},{1,13},{2,14},{3,15},{4,0},{5,1},{6,2},{7,3},{8,4},{9,5},{1... | collective-permute-start | bytes 393224 | tf_op jit(solution)/shard_map/ppermute | solution.py:34
  32.2 25.7 %copy-start.2 = (bf16[4096,256]{1,0:T(8,128)(2,1)S(1)}, bf16[4096,256]{1,0:T(8,128)(2,1)}, u32[]{:S(2)}) copy-start(bf16[4096,256]{1,0:T(8,128)(2,1)} %param.17) | copy-start | bytes 6291460
  51.5 14.9 %copy-start.6 = (bf16[4096,4]{0,1:T(4,128)(2,1)S(1)}, bf16[4096,4]{0,1:T(4,128)(2,1)}, u32[]{:S(2)}) copy-start(bf16[4096,4]{0,1:T(4,128)(2,1)} %param.19) | copy-start | bytes 98308
  51.5 29.8 %collective-permute-start.6 = (bf16[64,4096]{1,0:T(8,128)(2,1)S(1)}, bf16[64,4096]{1,0:T(8,128)(2,1)S(1)}, u32[]{:S(2)}, u32[]{:S(2)}) collective-permute-start(bf16[64,4096]{1,0:T(8,128)(2,1)S(1)} %pad_maximum_fusion), channel_id=1, source_target_pairs={{0,1},{1,2},{2,3},{3,4},{4,5},{5,6},{6,7},{7,8},{8,9},{9,10},{10,1... | collective-permute-start | bytes 1572872 | tf_op jit(solution)/shard_map/ppermute | solution.py:34
  53.4 28.2 %collective-permute-start.3 = (bf16[64,4096]{1,0:T(8,128)(2,1)S(1)}, bf16[64,4096]{1,0:T(8,128)(2,1)S(1)}, u32[]{:S(2)}, u32[]{:S(2)}) collective-permute-start(bf16[64,4096]{1,0:T(8,128)(2,1)S(1)} %pad_maximum_fusion), channel_id=1, source_target_pairs={{0,15},{1,0},{2,1},{3,2},{4,3},{5,4},{6,5},{7,6},{8,7},{9,8},{10,9... | collective-permute-start | bytes 1572872 | tf_op jit(solution)/shard_map/ppermute | solution.py:34
  58.5 8.1 %copy-start.4 = (bf16[4096,64]{0,1:T(8,128)(2,1)S(1)}, bf16[4096,64]{0,1:T(8,128)(2,1)}, u32[]{:S(2)}) copy-start(bf16[4096,64]{0,1:T(8,128)(2,1)} %param.18) | copy-start | bytes 1572868
  59.0 16.2 %collective-permute-start.4 = (bf16[64,2048]{1,0:T(8,128)(2,1)S(1)}, bf16[64,2048]{1,0:T(8,128)(2,1)S(1)}, u32[]{:S(2)}, u32[]{:S(2)}) collective-permute-start(bf16[64,2048]{1,0:T(8,128)(2,1)S(1)} %get-tuple-element.32), channel_id=1, source_target_pairs={{0,2},{1,3},{2,4},{3,5},{4,6},{5,7},{6,8},{7,9},{8,10},{9,11},{10,... | collective-permute-start | bytes 786440 | tf_op jit(solution)/shard_map/ppermute | solution.py:34
  60.9 18.9 %collective-permute-start.5 = (bf16[64,2048]{1,0:T(8,128)(2,1)S(1)}, bf16[64,2048]{1,0:T(8,128)(2,1)S(1)}, u32[]{:S(2)}, u32[]{:S(2)}) collective-permute-start(bf16[64,2048]{1,0:T(8,128)(2,1)S(1)} %get-tuple-element.33), channel_id=1, source_target_pairs={{0,14},{1,15},{2,0},{3,1},{4,2},{5,3},{6,4},{7,5},{8,6},{9,7},{10,... | collective-permute-start | bytes 786440 | tf_op jit(solution)/shard_map/ppermute | solution.py:34
  82.2 5.3 %collective-permute-start.8 = (bf16[64,3]{1,0:T(8,128)(2,1)S(1)}, bf16[64,3]{1,0:T(8,128)(2,1)S(1)}, u32[]{:S(2)}, u32[]{:S(2)}) collective-permute-start(bf16[64,3]{1,0:T(8,128)(2,1)S(1)} %slice.133), channel_id=1, source_target_pairs={{0,16},{16,32},{32,48},{48,64},{64,80},{80,96},{96,112},{1,17},{17... | collective-permute-start | bytes 1160 | tf_op jit(solution)/shard_map/ppermute | solution.py:24
  88.6 33.3 %all-to-all-start = ((bf16[16,64,256]{2,1,0:T(8,128)(2,1)}), bf16[16,64,256]{2,1,0:T(8,128)(2,1)}, u32[]{:S(2)}, u32[]{:S(2)}) async-start(bf16[16,64,256]{2,1,0:T(8,128)(2,1)} %broadcast_in_dim.9), calls=%async_computation | async-start | bytes 1048576 | tf_op jit(solution)/shard_map/all_to_all | solution.py:29
  99.1 5.3 %copy-start.3 = (bf16[4096,256]{1,0:T(8,128)(2,1)S(1)}, bf16[4096,256]{1,0:T(8,128)(2,1)}, u32[]{:S(2)}) copy-start(bf16[4096,256]{1,0:T(8,128)(2,1)} %param.17) | copy-start | bytes 6291460
  99.9 5.5 %copy-start.11 = (bf16[256,256]{1,0:T(8,128)(2,1)}, bf16[256,256]{1,0:T(8,128)(2,1)S(1)}, u32[]{:S(2)}) copy-start(bf16[256,256]{1,0:T(8,128)(2,1)S(1)} %convolution_convert_fusion.6.inner_ref) | copy-start | bytes 393220
  99.9 7.8 %collective-permute-start.7 = (bf16[3,256]{1,0:T(4,128)(2,1)S(1)}, bf16[3,256]{1,0:T(4,128)(2,1)S(1)}, u32[]{:S(2)}, u32[]{:S(2)}) collective-permute-start(bf16[3,256]{1,0:T(4,128)(2,1)S(1)} %slice.132), channel_id=1, source_target_pairs={{0,16},{16,32},{32,48},{48,64},{64,80},{80,96},{96,112},{1,17},{17... | collective-permute-start | bytes 4616 | tf_op jit(solution)/shard_map/ppermute | solution.py:24
  104.9 2.0 copy-start.14
  107.7 0.6 copy-start.12
  125.2 46.3 %copy-start.13 = (f32[256]{0:T(256)S(1)}, f32[256]{0:T(256)}, u32[]{:S(2)}) copy-start(f32[256]{0:T(256)} %param.25) | copy-start | bytes 3076
  125.2 10.1 %collective-permute-start.9 = (bf16[144,256]{1,0:T(8,128)(2,1)}, bf16[144,256]{1,0:T(8,128)(2,1)S(1)}, u32[]{:S(2)}, u32[]{:S(2)}) collective-permute-start(bf16[144,256]{1,0:T(8,128)(2,1)} %get-tuple-element.20), channel_id=1, source_target_pairs={{0,16},{16,0},{32,48},{48,32},{64,80},{80,64},{96,112},{112,96},{1... | collective-permute-start | bytes 221192 | tf_op jit(solution)/shard_map/ppermute | solution.py:336
  135.4 13.9 %copy-start.7 = (bf16[144,256]{1,0:T(8,128)(2,1)}, bf16[144,256]{1,0:T(8,128)(2,1)S(1)}, u32[]{:S(2)}) copy-start(bf16[144,256]{1,0:T(8,128)(2,1)S(1)} %collective-permute-done.9.partner_ref) | copy-start | bytes 221188
  136.3 3.9 %collective-permute-start.12 = (bf16[2,144,256]{2,1,0:T(8,128)(2,1)S(1)}, bf16[2,144,256]{2,1,0:T(8,128)(2,1)S(1)}, u32[]{:S(2)}, u32[]{:S(2)}) collective-permute-start(bf16[2,144,256]{2,1,0:T(8,128)(2,1)S(1)} %pad_maximum_fusion.2), channel_id=1, source_target_pairs={{0,96},{16,112},{1,97},{17,113},{2,98},{18,114},{3,99},{19,115},{4... | collective-permute-start | bytes 442376 | tf_op jit(solution)/shard_map/ppermute | solution.py:24
  137.0 8.5 %collective-permute-start.11 = (bf16[2,144,256]{2,1,0:T(8,128)(2,1)S(1)}, bf16[2,144,256]{2,1,0:T(8,128)(2,1)S(1)}, u32[]{:S(2)}, u32[]{:S(2)}) collective-permute-start(bf16[2,144,256]{2,1,0:T(8,128)(2,1)S(1)} %pad_maximum_fusion.2), channel_id=1, source_target_pairs={{0,64},{16,80},{32,96},{48,112},{1,65},{17,81},{33,97},{49,113},{2... | collective-permute-start | bytes 442376 | tf_op jit(solution)/shard_map/ppermute | solution.py:24
  138.3 11.0 %collective-permute-start.10 = (bf16[2,144,256]{2,1,0:T(8,128)(2,1)S(1)}, bf16[2,144,256]{2,1,0:T(8,128)(2,1)S(1)}, u32[]{:S(2)}, u32[]{:S(2)}) collective-permute-start(bf16[2,144,256]{2,1,0:T(8,128)(2,1)S(1)} %pad_maximum_fusion.2), channel_id=1, source_target_pairs={{0,32},{16,48},{32,64},{48,80},{64,96},{80,112},{1,33},{17,49},{33... | collective-permute-start | bytes 442376 | tf_op jit(solution)/shard_map/ppermute | solution.py:24
  140.2 9.1 %copy-start.8 = (bf16[2,144,256]{2,1,0:T(8,128)(2,1)}, bf16[2,144,256]{2,1,0:T(8,128)(2,1)S(1)}, u32[]{:S(2)}) copy-start(bf16[2,144,256]{2,1,0:T(8,128)(2,1)S(1)} %collective-permute-done.12.far_ref) | copy-start | bytes 442372
  145.5 3.8 %copy-start.9 = (bf16[2,144,256]{2,1,0:T(8,128)(2,1)}, bf16[2,144,256]{2,1,0:T(8,128)(2,1)S(1)}, u32[]{:S(2)}) copy-start(bf16[2,144,256]{2,1,0:T(8,128)(2,1)S(1)} %collective-permute-done.11.mid_ref) | copy-start | bytes 442372
  149.3 0.7 copy-start.10
  171.4 3.4 %copy-start.1 = (bf16[256,4096]{1,0:T(8,128)(2,1)S(1)}, bf16[256,4096]{1,0:T(8,128)(2,1)}, u32[]{:S(2)}) copy-start(bf16[256,4096]{1,0:T(8,128)(2,1)} %param.26) | copy-start | bytes 6291460
  175.4 26.8 %collective-permute-start.13 = (bf16[64,4096]{1,0:T(8,128)(2,1)S(1)}, bf16[64,4096]{1,0:T(8,128)(2,1)S(1)}, u32[]{:S(2)}, u32[]{:S(2)}) collective-permute-start(bf16[64,4096]{1,0:T(8,128)(2,1)S(1)} %convolution_convert_fusion.1), channel_id=1, source_target_pairs={{0,1},{1,2},{2,3},{3,4},{4,5},{5,6},{6,7},{7,8},{8,9},{9,10},{10,1... | collective-permute-start | bytes 1572872 | tf_op jit(solution)/shard_map/ppermute | solution.py:34
  178.2 24.1 %collective-permute-start.14 = (bf16[64,4096]{1,0:T(8,128)(2,1)S(1)}, bf16[64,4096]{1,0:T(8,128)(2,1)S(1)}, u32[]{:S(2)}, u32[]{:S(2)}) collective-permute-start(bf16[64,4096]{1,0:T(8,128)(2,1)S(1)} %convolution_convert_fusion), channel_id=1, source_target_pairs={{0,15},{1,0},{2,1},{3,2},{4,3},{5,4},{6,5},{7,6},{8,7},{9,8},{10,9... | collective-permute-start | bytes 1572872 | tf_op jit(solution)/shard_map/ppermute | solution.py:34
  182.2 15.1 %collective-permute-start.16 = (bf16[64,2048]{1,0:T(8,128)(2,1)S(1)}, bf16[64,2048]{1,0:T(8,128)(2,1)S(1)}, u32[]{:S(2)}, u32[]{:S(2)}) collective-permute-start(bf16[64,2048]{1,0:T(8,128)(2,1)S(1)} %convolution_convert_fusion.3), channel_id=1, source_target_pairs={{0,2},{1,3},{2,4},{3,5},{4,6},{5,7},{6,8},{7,9},{8,10},{9,11},{10,... | collective-permute-start | bytes 786440 | tf_op jit(solution)/shard_map/ppermute | solution.py:34
  184.5 17.8 %collective-permute-start.15 = (bf16[64,2048]{1,0:T(8,128)(2,1)S(1)}, bf16[64,2048]{1,0:T(8,128)(2,1)S(1)}, u32[]{:S(2)}, u32[]{:S(2)}) collective-permute-start(bf16[64,2048]{1,0:T(8,128)(2,1)S(1)} %convolution_convert_fusion.2), channel_id=1, source_target_pairs={{0,14},{1,15},{2,0},{3,1},{4,2},{5,3},{6,4},{7,5},{8,6},{9,7},{10,... | collective-permute-start | bytes 786440 | tf_op jit(solution)/shard_map/ppermute | solution.py:34
  189.9 45.0 %copy-start.5 = (bf16[16,4096]{1,0:T(8,128)(2,1)S(1)}, bf16[16,4096]{1,0:T(8,128)(2,1)}, u32[]{:S(2)}) copy-start(bf16[16,4096]{1,0:T(8,128)(2,1)} %param.14) | copy-start | bytes 393220
  202.9 14.8 %collective-permute-start.17 = (bf16[16,4096]{1,0:T(8,128)(2,1)S(1)}, bf16[16,4096]{1,0:T(8,128)(2,1)S(1)}, u32[]{:S(2)}, u32[]{:S(2)}) collective-permute-start(bf16[16,4096]{1,0:T(8,128)(2,1)S(1)} %get-tuple-element.29), channel_id=1, source_target_pairs={{0,8},{1,9},{2,10},{3,11},{4,12},{5,13},{6,14},{7,15},{8,0},{9,1},... | collective-permute-start | bytes 393224 | tf_op jit(solution)/shard_map/ppermute | solution.py:34
  208.5 26.5 %collective-permute-start.19 = (bf16[16,4096]{1,0:T(8,128)(2,1)S(1)}, bf16[16,4096]{1,0:T(8,128)(2,1)S(1)}, u32[]{:S(2)}, u32[]{:S(2)}) collective-permute-start(bf16[16,4096]{1,0:T(8,128)(2,1)S(1)} %get-tuple-element.30), channel_id=1, source_target_pairs={{0,12},{1,13},{2,14},{3,15},{4,0},{5,1},{6,2},{7,3},{8,4},{9,5},{1... | collective-permute-start | bytes 393224 | tf_op jit(solution)/shard_map/ppermute | solution.py:34
  214.2 20.7 %collective-permute-start.18 = (bf16[16,4096]{1,0:T(8,128)(2,1)S(1)}, bf16[16,4096]{1,0:T(8,128)(2,1)S(1)}, u32[]{:S(2)}, u32[]{:S(2)}) collective-permute-start(bf16[16,4096]{1,0:T(8,128)(2,1)S(1)} %get-tuple-element.31), channel_id=1, source_target_pairs={{0,4},{1,5},{2,6},{3,7},{4,8},{5,9},{6,10},{7,11},{8,12},{9,13},{1... | collective-permute-start | bytes 393224 | tf_op jit(solution)/shard_map/ppermute | solution.py:34

commit v7 on v5

--- a/solution.py
+++ b/solution.py
@@ -9,6 +9,7 @@
 STATE = 128
 GROUP_HEADS = 16
 TAPS = 4
+VMEM_GRANT = 16 * 2**20
 ORDER = (0, 4, 8, 12, 1, 5, 9, 13, 2, 6, 10, 14, 15, 3, 7, 11)
 TAIL_ROWS = 8
 GROUPS = 4
@@ -213,6 +214,7 @@
         in_specs=in_vmem(7),
         out_specs=tuple(in_vmem(3)),
         scratch_shapes=[pltpu.VMEM((length + TAIL_ROWS, width), jnp.float32)],
+        compiler_params=pltpu.CompilerParams(vmem_limit_bytes=VMEM_GRANT),
         interpret=interpret,
         name="local_scan",
     )(inner, halo, taps, states, step, decay, skip)
@@ -228,6 +230,7 @@
         ),
         in_specs=[pl.BlockSpec(memory_space=pltpu.SMEM)] + in_vmem(5),
         out_specs=tuple(in_vmem(2)),
+        compiler_params=pltpu.CompilerParams(vmem_limit_bytes=VMEM_GRANT),
         interpret=interpret,
         name="carry_in",
     )(position, messages, states, reach, local, gate)
@@ -278,17 +281,19 @@
     state_proj = product(project_across(proj_states).astype(jnp.bfloat16), place, flat)
     state_proj = state_proj.astype(jnp.bfloat16)
     before_states = from_behind(state_proj[:, row_count - margin :], "seq", 1)
-    inner_proj = project(proj_inner)
-    gate_proj = project(proj_gate)
     steps = product(project_across(proj_step), place.astype(jnp.float32), flat, highest)
     step_size = jax.nn.softplus(steps + step_bias[:, None])
     log_decay = -jnp.exp(log_rate)[:, None] * step_size
-    before_inner = from_behind(inner_proj[row_count - margin :], "seq", 1)
     padded = jnp.concatenate((before_states, state_proj), axis=1).astype(jnp.float32)
     mixed_local = jnp.zeros(state_proj.shape, jnp.float32)
     for tap in range(TAPS):
         mixed_local = mixed_local + conv_states[tap][:, None] * padded[:, tap : tap + row_count]
     mixed_local = jax.nn.silu(mixed_local).astype(jnp.bfloat16)
+    held = lax.optimization_barrier((pieces[1:], mixed_local))[0]
+    pieces = (pieces[0], *held)
+    inner_proj = project(proj_inner)
+    gate_proj = project(proj_gate)
+    before_inner = from_behind(inner_proj[row_count - margin :], "seq", 1)
     mixed_all = from_everyone(mixed_local, "tp").reshape(-1, row_count)
     skip_row = jnp.repeat(skip_gain, HEAD_DIM)[None]
     local, message, reach = local_scan(

time: 235 us -> 228 us (0.970)
  Pallas kernels: 6.43 us -> 2.6 us
  transfers between devices with their start and end apart: 17 -> 17, of which waited for: 10 -> 9; matrix products, arithmetic and copies ran while one was open for 5% -> 5% of each run, Pallas kernels for 0% -> 0%
where the time goes in v7:
time: 228 us; the launch traced here: 226 us
  starting transfers between devices  89.8 us (39%)
  waiting for transfers between devices  74.3 us (33%)
  blocking collectives  39.2 us (17%)
  matrix products  12.2 us (5%)
  other arithmetic  4.31 us (2%)
  local copies, waits for them, and re-layouts  3 us (1%)
  Pallas kernels  2.6 us (1%)
    ppermute x14, starting transfers between devices, shifted(): lax.ppermute(x, axis, [(k, (k + steps) % count) for k in range(count)])  74 us
    ppermute x14, waiting for transfers between devices, shifted(): lax.ppermute(x, axis, [(k, (k + steps) % count) for k in range(count)])  57.8 us
    all_to_all x1, blocking collectives, from_everyone(): return lax.all_to_all(copies, axis, split_axis=0, concat_axis=0, tiled=True)  19.7 us
    all_gather x1, blocking collectives, body(): messages = lax.all_gather(message, 'seq', axis=0, tiled=True)  19.5 us
    all_to_all x1, waiting for transfers between devices, from_everyone(): return lax.all_to_all(copies, axis, split_axis=0, concat_axis=0, tiled=True)  16.4 us
    all_to_all x1, starting transfers between devices, from_everyone(): return lax.all_to_all(copies, axis, split_axis=0, concat_axis=0, tiled=True)  10.7 us
    dot_general x21, matrix products, product(): lax.dot_general(left, right, dims, precision=precision, preferred_element...  8.31 us
    ppermute x2, starting transfers between devices, from_behind(): lax.ppermute(value, axis, [(source, source + steps) for source in range(i...  5.17 us
  transfers between devices with their start and end apart: 17, of which 9 were waited for; matrix products, arithmetic and copies ran while one was open for 5% of the time, Pallas kernels for 0%

profile of v7, /device:TPU:56, one launch (start us, length us, event | category | flops | bytes accessed | tf_op | source)
XLA Modules:
  0.0 226.0 jit_solution(18159354203672701269)
XLA Ops:
  0.0 1.2 fusion.6
  1.2 1.0 fusion.8
  2.2 10.9 %collective-permute-start.2 = (bf16[16,4096]{1,0:T(8,128)(2,1)S(1)}, bf16[16,4096]{1,0:T(8,128)(2,1)S(1)}, u32[]{:S(2)}, u32[]{:S(2)}) collective-permute-start(bf16[16,4096]{1,0:T(8,128)(2,1)S(1)} %fusion.8), channel_id=1, source_target_pairs={{0,4},{1,5},{2,6},{3,7},{4,8},{5,9},{6,10},{7,11},{8,12},{9,13},{1... | collective-permute-start | bytes 393224 | tf_op jit(solution)/shard_map/ppermute | solution.py:35
  13.2 14.6 %collective-permute-start.1 = (bf16[16,4096]{1,0:T(8,128)(2,1)S(1)}, bf16[16,4096]{1,0:T(8,128)(2,1)S(1)}, u32[]{:S(2)}, u32[]{:S(2)}) collective-permute-start(bf16[16,4096]{1,0:T(8,128)(2,1)S(1)} %fusion.8), channel_id=1, source_target_pairs={{0,8},{1,9},{2,10},{3,11},{4,12},{5,13},{6,14},{7,15},{8,0},{9,1},... | collective-permute-start | bytes 393224 | tf_op jit(solution)/shard_map/ppermute | solution.py:35
  27.7 3.6 %collective-permute-start = (bf16[16,4096]{1,0:T(8,128)(2,1)S(1)}, bf16[16,4096]{1,0:T(8,128)(2,1)S(1)}, u32[]{:S(2)}, u32[]{:S(2)}) collective-permute-start(bf16[16,4096]{1,0:T(8,128)(2,1)S(1)} %fusion.8), channel_id=1, source_target_pairs={{0,12},{1,13},{2,14},{3,15},{4,0},{5,1},{6,2},{7,3},{8,4},{9,5},{1... | collective-permute-start | bytes 393224 | tf_op jit(solution)/shard_map/ppermute | solution.py:35
  31.7 0.7 broadcast_in_dim.9
  32.5 0.9 slice_bitcast_fusion.3
  33.4 0.7 exponential_negate_fusion
  34.1 13.2 %collective-permute-done.1 = bf16[16,4096]{1,0:T(8,128)(2,1)S(1)} collective-permute-done((bf16[16,4096]{1,0:T(8,128)(2,1)S(1)}, bf16[16,4096]{1,0:T(8,128)(2,1)S(1)}, u32[]{:S(2)}, u32[]{:S(2)}) %collective-permute-start.1) | collective-permute-done | bytes 131104 | tf_op jit(solution)/shard_map/ppermute | solution.py:35
  47.3 4.4 %collective-permute-done = bf16[16,4096]{1,0:T(8,128)(2,1)S(1)} collective-permute-done((bf16[16,4096]{1,0:T(8,128)(2,1)S(1)}, bf16[16,4096]{1,0:T(8,128)(2,1)S(1)}, u32[]{:S(2)}, u32[]{:S(2)}) %collective-permute-start) | collective-permute-done | bytes 131104 | tf_op jit(solution)/shard_map/ppermute | solution.py:35
  51.8 2.4 %collective-permute-start.6 = (bf16[64,4096]{1,0:T(8,128)(2,1)S(1)}, bf16[64,4096]{1,0:T(8,128)(2,1)S(1)}, u32[]{:S(2)}, u32[]{:S(2)}) collective-permute-start(bf16[64,4096]{1,0:T(8,128)(2,1)S(1)} %pad_maximum_fusion), channel_id=1, source_target_pairs={{0,1},{1,2},{2,3},{3,4},{4,5},{5,6},{6,7},{7,8},{8,9},{9,10},{10,1... | collective-permute-start | bytes 1572872 | tf_op jit(solution)/shard_map/ppermute | solution.py:35
  54.3 4.6 %collective-permute-start.3 = (bf16[64,4096]{1,0:T(8,128)(2,1)S(1)}, bf16[64,4096]{1,0:T(8,128)(2,1)S(1)}, u32[]{:S(2)}, u32[]{:S(2)}) collective-permute-start(bf16[64,4096]{1,0:T(8,128)(2,1)S(1)} %pad_maximum_fusion), channel_id=1, source_target_pairs={{0,15},{1,0},{2,1},{3,2},{4,3},{5,4},{6,5},{7,6},{8,7},{9,8},{10,9... | collective-permute-start | bytes 1572872 | tf_op jit(solution)/shard_map/ppermute | solution.py:35
  58.9 0.5 convolution_convert_fusion.11
  59.4 0.5 convolution_convert_fusion.15
  59.9 1.9 collective-permute-start.4
  61.8 6.0 %collective-permute-start.5 = (bf16[64,2048]{1,0:T(8,128)(2,1)S(1)}, bf16[64,2048]{1,0:T(8,128)(2,1)S(1)}, u32[]{:S(2)}, u32[]{:S(2)}) collective-permute-start(bf16[64,2048]{1,0:T(8,128)(2,1)S(1)} %get-tuple-element.29), channel_id=1, source_target_pairs={{0,14},{1,15},{2,0},{3,1},{4,2},{5,3},{6,4},{7,5},{8,6},{9,7},{10,... | collective-permute-start | bytes 786440 | tf_op jit(solution)/shard_map/ppermute | solution.py:35
  67.9 0.2 convolution_bitcast_fusion.3
  68.1 0.3 fusion
  68.4 7.2 %collective-permute-done.4 = bf16[64,2048]{1,0:T(8,128)(2,1)S(1)} collective-permute-done((bf16[64,2048]{1,0:T(8,128)(2,1)S(1)}, bf16[64,2048]{1,0:T(8,128)(2,1)S(1)}, u32[]{:S(2)}, u32[]{:S(2)}) %collective-permute-start.4) | collective-permute-done | bytes 262176 | tf_op jit(solution)/shard_map/ppermute | solution.py:35
  75.6 5.2 %collective-permute-done.5 = bf16[64,2048]{1,0:T(8,128)(2,1)S(1)} collective-permute-done((bf16[64,2048]{1,0:T(8,128)(2,1)S(1)}, bf16[64,2048]{1,0:T(8,128)(2,1)S(1)}, u32[]{:S(2)}, u32[]{:S(2)}) %collective-permute-start.5) | collective-permute-done | bytes 262176 | tf_op jit(solution)/shard_map/ppermute | solution.py:35
  80.9 0.2 convolution_bitcast_fusion.1
  81.1 0.3 fusion.2
  81.5 0.3 fusion.3
  81.8 0.3 fusion.1
  82.1 0.2 convolution_convert_fusion.7
  82.4 1.3 collective-permute-start.7
  83.7 0.2 convolution_bitcast_fusion
  83.9 0.3 convolution_bitcast_fusion.2
  84.2 0.3 broadcast_multiply_fusion
  84.6 0.2 multiply_convert_fusion.2
  84.7 0.9 broadcast_in_dim.8
  85.6 10.7 %all-to-all-start = ((bf16[16,64,256]{2,1,0:T(8,128)(2,1)}), bf16[16,64,256]{2,1,0:T(8,128)(2,1)S(1)}, u32[]{:S(2)}, u32[]{:S(2)}) async-start(bf16[16,64,256]{2,1,0:T(8,128)(2,1)} %broadcast_in_dim.8), calls=%async_computation | async-start | bytes 1048576 | tf_op jit(solution)/shard_map/all_to_all | solution.py:30
  96.3 1.6 convolution_convert_fusion.14
  97.9 0.5 convolution_convert_fusion.13
  98.4 0.5 convolution_convert_fusion.12
  98.8 0.3 convolution_convert_fusion.6.inner_ref
  99.2 3.9 %collective-permute-start.8 = (bf16[3,256]{1,0:T(4,128)(2,1)S(1)}, bf16[3,256]{1,0:T(4,128)(2,1)S(1)}, u32[]{:S(2)}, u32[]{:S(2)}) collective-permute-start(bf16[3,256]{1,0:T(4,128)(2,1)S(1)} %slice.137), channel_id=1, source_target_pairs={{0,16},{16,32},{32,48},{48,64},{64,80},{80,96},{96,112},{1,17},{17... | collective-permute-start | bytes 4616 | tf_op jit(solution)/shard_map/ppermute | solution.py:25
  103.1 0.5 convolution_convert_fusion.10
  103.6 0.5 convolution_convert_fusion.9
  104.1 0.5 convolution_convert_fusion.8
  104.5 0.3 convolution_convert_fusion.5.gate_ref
  104.9 16.4 %all-to-all-done = bf16[16,64,256]{2,1,0:T(8,128)(2,1)S(1)} async-done(((bf16[16,64,256]{2,1,0:T(8,128)(2,1)}), bf16[16,64,256]{2,1,0:T(8,128)(2,1)S(1)}, u32[]{:S(2)}, u32[]{:S(2)}) %all-to-all-start) | async-done | bytes 524320 | tf_op jit(solution)/shard_map/all_to_all | solution.py:30
  121.3 1.7 local_scan.1
  123.0 19.5 %all_gather.3.messages_ref = bf16[8,144,256]{2,1,0:T(8,128)(2,1)S(1)} all-gather(bf16[1,144,256]{2,1,0:T(8,128)(2,1)S(1)} %get-tuple-element.17), channel_id=1, replica_groups=mesh['dp'=8,'seq'=8,'tp'=16] {'seq'}, dimensions={0}, use_global_device_ids=true | all-gather | bytes 663552 | tf_op jit(solution)/shard_map/all_gather | solution.py:302
  142.5 0.9 carry_in.1
  143.4 19.7 %all_to_all.10 = f32[16,4,256]{2,1,0:T(4,128)S(1)} all-to-all(f32[16,4,256]{2,1,0:T(4,128)S(1)} %broadcast_in_dim.10), channel_id=1, replica_groups=mesh['dp'=8,'seq'=8,'tp'=16] {'tp'}, dimensions={0} | all-to-all | bytes 131072 | tf_op jit(solution)/shard_map/all_to_all | solution.py:30
  163.3 0.2 convolution_convert_fusion.4
  163.6 2.2 convolution_convert_fusion
  165.8 0.5 convolution_convert_fusion.1
  166.3 2.9 %collective-permute-start.9 = (bf16[64,4096]{1,0:T(8,128)(2,1)S(1)}, bf16[64,4096]{1,0:T(8,128)(2,1)S(1)}, u32[]{:S(2)}, u32[]{:S(2)}) collective-permute-start(bf16[64,4096]{1,0:T(8,128)(2,1)S(1)} %convolution_convert_fusion.1), channel_id=1, source_target_pairs={{0,1},{1,2},{2,3},{3,4},{4,5},{5,6},{6,7},{7,8},{8,9},{9,10},{10,1... | collective-permute-start | bytes 1572872 | tf_op jit(solution)/shard_map/ppermute | solution.py:35
  169.1 4.2 %collective-permute-start.10 = (bf16[64,4096]{1,0:T(8,128)(2,1)S(1)}, bf16[64,4096]{1,0:T(8,128)(2,1)S(1)}, u32[]{:S(2)}, u32[]{:S(2)}) collective-permute-start(bf16[64,4096]{1,0:T(8,128)(2,1)S(1)} %convolution_convert_fusion), channel_id=1, source_target_pairs={{0,15},{1,0},{2,1},{3,2},{4,3},{5,4},{6,5},{7,6},{8,7},{9,8},{10,9... | collective-permute-start | bytes 1572872 | tf_op jit(solution)/shard_map/ppermute | solution.py:35
  173.3 0.3 convolution_convert_fusion.3
  173.7 1.9 collective-permute-start.12
  175.6 0.3 convolution_convert_fusion.2
  175.9 6.0 %collective-permute-start.11 = (bf16[64,2048]{1,0:T(8,128)(2,1)S(1)}, bf16[64,2048]{1,0:T(8,128)(2,1)S(1)}, u32[]{:S(2)}, u32[]{:S(2)}) collective-permute-start(bf16[64,2048]{1,0:T(8,128)(2,1)S(1)} %convolution_convert_fusion.2), channel_id=1, source_target_pairs={{0,14},{1,15},{2,0},{3,1},{4,2},{5,3},{6,4},{7,5},{8,6},{9,7},{10,... | collective-permute-start | bytes 786440 | tf_op jit(solution)/shard_map/ppermute | solution.py:35
  182.0 10.6 %collective-permute-done.12 = bf16[64,2048]{1,0:T(8,128)(2,1)S(1)} collective-permute-done((bf16[64,2048]{1,0:T(8,128)(2,1)S(1)}, bf16[64,2048]{1,0:T(8,128)(2,1)S(1)}, u32[]{:S(2)}, u32[]{:S(2)}) %collective-permute-start.12) | collective-permute-done | bytes 262176 | tf_op jit(solution)/shard_map/ppermute | solution.py:35
  192.6 2.0 collective-permute-done.11
  194.6 0.6 fusion.65
  195.3 5.1 %collective-permute-start.13 = (bf16[16,4096]{1,0:T(8,128)(2,1)S(1)}, bf16[16,4096]{1,0:T(8,128)(2,1)S(1)}, u32[]{:S(2)}, u32[]{:S(2)}) collective-permute-start(bf16[16,4096]{1,0:T(8,128)(2,1)S(1)} %get-tuple-element.25), channel_id=1, source_target_pairs={{0,8},{1,9},{2,10},{3,11},{4,12},{5,13},{6,14},{7,15},{8,0},{9,1},... | collective-permute-start | bytes 393224 | tf_op jit(solution)/shard_map/ppermute | solution.py:35
  200.4 5.7 %collective-permute-start.15 = (bf16[16,4096]{1,0:T(8,128)(2,1)S(1)}, bf16[16,4096]{1,0:T(8,128)(2,1)S(1)}, u32[]{:S(2)}, u32[]{:S(2)}) collective-permute-start(bf16[16,4096]{1,0:T(8,128)(2,1)S(1)} %get-tuple-element.26), channel_id=1, source_target_pairs={{0,12},{1,13},{2,14},{3,15},{4,0},{5,1},{6,2},{7,3},{8,4},{9,5},{1... | collective-permute-start | bytes 393224 | tf_op jit(solution)/shard_map/ppermute | solution.py:35
  206.2 4.0 %collective-permute-start.14 = (bf16[16,4096]{1,0:T(8,128)(2,1)S(1)}, bf16[16,4096]{1,0:T(8,128)(2,1)S(1)}, u32[]{:S(2)}, u32[]{:S(2)}) collective-permute-start(bf16[16,4096]{1,0:T(8,128)(2,1)S(1)} %get-tuple-element.27), channel_id=1, source_target_pairs={{0,4},{1,5},{2,6},{3,7},{4,8},{5,9},{6,10},{7,11},{8,12},{9,13},{1... | collective-permute-start | bytes 393224 | tf_op jit(solution)/shard_map/ppermute | solution.py:35
  210.2 6.1 %collective-permute-done.13 = bf16[16,4096]{1,0:T(8,128)(2,1)S(1)} collective-permute-done((bf16[16,4096]{1,0:T(8,128)(2,1)S(1)}, bf16[16,4096]{1,0:T(8,128)(2,1)S(1)}, u32[]{:S(2)}, u32[]{:S(2)}) %collective-permute-start.13) | collective-permute-done | bytes 131104 | tf_op jit(solution)/shard_map/ppermute | solution.py:35
  216.3 9.0 %collective-permute-done.15 = bf16[16,4096]{1,0:T(8,128)(2,1)S(1)} collective-permute-done((bf16[16,4096]{1,0:T(8,128)(2,1)S(1)}, bf16[16,4096]{1,0:T(8,128)(2,1)S(1)}, u32[]{:S(2)}, u32[]{:S(2)}) %collective-permute-start.15) | collective-permute-done | bytes 131104 | tf_op jit(solution)/shard_map/ppermute | solution.py:35
  225.3 0.7 fusion.9
  (66 shorter events, 1.1 us)
Async XLA Ops:
  0.0 59.4 %copy-start = (bf16[4096,256]{1,0:T(8,128)(2,1)S(1)}, bf16[4096,256]{1,0:T(8,128)(2,1)}, u32[]{:S(2)}) copy-start(bf16[4096,256]{1,0:T(8,128)(2,1)} %param.16) | copy-start | bytes 6291460
  2.2 31.9 %collective-permute-start.2 = (bf16[16,4096]{1,0:T(8,128)(2,1)S(1)}, bf16[16,4096]{1,0:T(8,128)(2,1)S(1)}, u32[]{:S(2)}, u32[]{:S(2)}) collective-permute-start(bf16[16,4096]{1,0:T(8,128)(2,1)S(1)} %fusion.8), channel_id=1, source_target_pairs={{0,4},{1,5},{2,6},{3,7},{4,8},{5,9},{6,10},{7,11},{8,12},{9,13},{1... | collective-permute-start | bytes 393224 | tf_op jit(solution)/shard_map/ppermute | solution.py:35
  13.2 34.2 %collective-permute-start.1 = (bf16[16,4096]{1,0:T(8,128)(2,1)S(1)}, bf16[16,4096]{1,0:T(8,128)(2,1)S(1)}, u32[]{:S(2)}, u32[]{:S(2)}) collective-permute-start(bf16[16,4096]{1,0:T(8,128)(2,1)S(1)} %fusion.8), channel_id=1, source_target_pairs={{0,8},{1,9},{2,10},{3,11},{4,12},{5,13},{6,14},{7,15},{8,0},{9,1},... | collective-permute-start | bytes 393224 | tf_op jit(solution)/shard_map/ppermute | solution.py:35
  27.7 24.0 %collective-permute-start = (bf16[16,4096]{1,0:T(8,128)(2,1)S(1)}, bf16[16,4096]{1,0:T(8,128)(2,1)S(1)}, u32[]{:S(2)}, u32[]{:S(2)}) collective-permute-start(bf16[16,4096]{1,0:T(8,128)(2,1)S(1)} %fusion.8), channel_id=1, source_target_pairs={{0,12},{1,13},{2,14},{3,15},{4,0},{5,1},{6,2},{7,3},{8,4},{9,5},{1... | collective-permute-start | bytes 393224 | tf_op jit(solution)/shard_map/ppermute | solution.py:35
  32.5 26.4 %copy-start.2 = (bf16[4096,256]{1,0:T(8,128)(2,1)S(1)}, bf16[4096,256]{1,0:T(8,128)(2,1)}, u32[]{:S(2)}) copy-start(bf16[4096,256]{1,0:T(8,128)(2,1)} %param.17) | copy-start | bytes 6291460
  51.8 16.0 %copy-start.11 = (bf16[4096,4]{0,1:T(4,128)(2,1)S(1)}, bf16[4096,4]{0,1:T(4,128)(2,1)}, u32[]{:S(2)}) copy-start(bf16[4096,4]{0,1:T(4,128)(2,1)} %param.19) | copy-start | bytes 98308
  51.8 29.6 %collective-permute-start.6 = (bf16[64,4096]{1,0:T(8,128)(2,1)S(1)}, bf16[64,4096]{1,0:T(8,128)(2,1)S(1)}, u32[]{:S(2)}, u32[]{:S(2)}) collective-permute-start(bf16[64,4096]{1,0:T(8,128)(2,1)S(1)} %pad_maximum_fusion), channel_id=1, source_target_pairs={{0,1},{1,2},{2,3},{3,4},{4,5},{5,6},{6,7},{7,8},{8,9},{9,10},{10,1... | collective-permute-start | bytes 1572872 | tf_op jit(solution)/shard_map/ppermute | solution.py:35
  54.3 27.4 %collective-permute-start.3 = (bf16[64,4096]{1,0:T(8,128)(2,1)S(1)}, bf16[64,4096]{1,0:T(8,128)(2,1)S(1)}, u32[]{:S(2)}, u32[]{:S(2)}) collective-permute-start(bf16[64,4096]{1,0:T(8,128)(2,1)S(1)} %pad_maximum_fusion), channel_id=1, source_target_pairs={{0,15},{1,0},{2,1},{3,2},{4,3},{5,4},{6,5},{7,6},{8,7},{9,8},{10,9... | collective-permute-start | bytes 1572872 | tf_op jit(solution)/shard_map/ppermute | solution.py:35
  59.4 8.7 %copy-start.5 = (bf16[4096,64]{0,1:T(8,128)(2,1)S(1)}, bf16[4096,64]{0,1:T(8,128)(2,1)}, u32[]{:S(2)}) copy-start(bf16[4096,64]{0,1:T(8,128)(2,1)} %param.18) | copy-start | bytes 1572868
  59.9 15.7 %collective-permute-start.4 = (bf16[64,2048]{1,0:T(8,128)(2,1)S(1)}, bf16[64,2048]{1,0:T(8,128)(2,1)S(1)}, u32[]{:S(2)}, u32[]{:S(2)}) collective-permute-start(bf16[64,2048]{1,0:T(8,128)(2,1)S(1)} %get-tuple-element.28), channel_id=1, source_target_pairs={{0,2},{1,3},{2,4},{3,5},{4,6},{5,7},{6,8},{7,9},{8,10},{9,11},{10,... | collective-permute-start | bytes 786440 | tf_op jit(solution)/shard_map/ppermute | solution.py:35
  61.8 19.0 %collective-permute-start.5 = (bf16[64,2048]{1,0:T(8,128)(2,1)S(1)}, bf16[64,2048]{1,0:T(8,128)(2,1)S(1)}, u32[]{:S(2)}, u32[]{:S(2)}) collective-permute-start(bf16[64,2048]{1,0:T(8,128)(2,1)S(1)} %get-tuple-element.29), channel_id=1, source_target_pairs={{0,14},{1,15},{2,0},{3,1},{4,2},{5,3},{6,4},{7,5},{8,6},{9,7},{10,... | collective-permute-start | bytes 786440 | tf_op jit(solution)/shard_map/ppermute | solution.py:35
  81.1 3.0 %copy-start.13 = (f32[4]{0:T(128)S(1)}, f32[4]{0:T(128)}, u32[]{:S(2)}) copy-start(f32[4]{0:T(128)} %param.20) | copy-start | bytes 52
  81.4 2.5 %copy-start.6 = (bf16[64,4096]{1,0:T(8,128)(2,1)}, bf16[64,4096]{1,0:T(8,128)(2,1)S(1)}, u32[]{:S(2)}) copy-start(bf16[64,4096]{1,0:T(8,128)(2,1)S(1)} %collective-permute-done.6) | copy-start | bytes 1572868
  81.8 2.4 %copy-start.8 = (bf16[64,4096]{1,0:T(8,128)(2,1)}, bf16[64,4096]{1,0:T(8,128)(2,1)S(1)}, u32[]{:S(2)}) copy-start(bf16[64,4096]{1,0:T(8,128)(2,1)S(1)} %collective-permute-done.3) | copy-start | bytes 1572868
  82.4 2.1 collective-permute-start.7
  85.6 35.7 %all-to-all-start = ((bf16[16,64,256]{2,1,0:T(8,128)(2,1)}), bf16[16,64,256]{2,1,0:T(8,128)(2,1)S(1)}, u32[]{:S(2)}, u32[]{:S(2)}) async-start(bf16[16,64,256]{2,1,0:T(8,128)(2,1)} %broadcast_in_dim.8), calls=%async_computation | async-start | bytes 1048576 | tf_op jit(solution)/shard_map/all_to_all | solution.py:30
  96.3 2.0 copy-start.7
  98.4 4.7 %copy-start.3 = (bf16[4096,256]{1,0:T(8,128)(2,1)S(1)}, bf16[4096,256]{1,0:T(8,128)(2,1)}, u32[]{:S(2)}) copy-start(bf16[4096,256]{1,0:T(8,128)(2,1)} %param.17) | copy-start | bytes 6291460
  98.4 4.7 %copy-start.9 = (bf16[64,4096]{1,0:T(8,128)(2,1)S(1)}, bf16[64,4096]{1,0:T(8,128)(2,1)}, u32[]{:S(2)}) copy-start(bf16[64,4096]{1,0:T(8,128)(2,1)} %copy-done.8) | copy-start | bytes 1572868
  99.2 5.7 %collective-permute-start.8 = (bf16[3,256]{1,0:T(4,128)(2,1)S(1)}, bf16[3,256]{1,0:T(4,128)(2,1)S(1)}, u32[]{:S(2)}, u32[]{:S(2)}) collective-permute-start(bf16[3,256]{1,0:T(4,128)(2,1)S(1)} %slice.137), channel_id=1, source_target_pairs={{0,16},{16,32},{32,48},{48,64},{64,80},{80,96},{96,112},{1,17},{17... | collective-permute-start | bytes 4616 | tf_op jit(solution)/shard_map/ppermute | solution.py:25
  104.0 17.2 %copy-start.1 = (f32[4,256]{1,0:T(4,128)S(1)}, f32[4,256]{1,0:T(4,128)}, u32[]{:S(2)}) copy-start(f32[4,256]{1,0:T(4,128)} %taps_ref.1) | copy-start | bytes 12292
  104.9 58.5 %copy-start.12 = (f32[256]{0:T(256)S(1)}, f32[256]{0:T(256)}, u32[]{:S(2)}) copy-start(f32[256]{0:T(256)} %param.25) | copy-start | bytes 3076
  163.3 2.5 %copy-start.4 = (bf16[256,4096]{1,0:T(8,128)(2,1)S(1)}, bf16[256,4096]{1,0:T(8,128)(2,1)}, u32[]{:S(2)}) copy-start(bf16[256,4096]{1,0:T(8,128)(2,1)} %param.26) | copy-start | bytes 6291460
  166.3 28.4 %collective-permute-start.9 = (bf16[64,4096]{1,0:T(8,128)(2,1)S(1)}, bf16[64,4096]{1,0:T(8,128)(2,1)S(1)}, u32[]{:S(2)}, u32[]{:S(2)}) collective-permute-start(bf16[64,4096]{1,0:T(8,128)(2,1)S(1)} %convolution_convert_fusion.1), channel_id=1, source_target_pairs={{0,1},{1,2},{2,3},{3,4},{4,5},{5,6},{6,7},{7,8},{8,9},{9,10},{10,1... | collective-permute-start | bytes 1572872 | tf_op jit(solution)/shard_map/ppermute | solution.py:35
  169.1 25.5 %collective-permute-start.10 = (bf16[64,4096]{1,0:T(8,128)(2,1)S(1)}, bf16[64,4096]{1,0:T(8,128)(2,1)S(1)}, u32[]{:S(2)}, u32[]{:S(2)}) collective-permute-start(bf16[64,4096]{1,0:T(8,128)(2,1)S(1)} %convolution_convert_fusion), channel_id=1, source_target_pairs={{0,15},{1,0},{2,1},{3,2},{4,3},{5,4},{6,5},{7,6},{8,7},{9,8},{10,9... | collective-permute-start | bytes 1572872 | tf_op jit(solution)/shard_map/ppermute | solution.py:35
  173.7 18.9 %collective-permute-start.12 = (bf16[64,2048]{1,0:T(8,128)(2,1)S(1)}, bf16[64,2048]{1,0:T(8,128)(2,1)S(1)}, u32[]{:S(2)}, u32[]{:S(2)}) collective-permute-start(bf16[64,2048]{1,0:T(8,128)(2,1)S(1)} %convolution_convert_fusion.3), channel_id=1, source_target_pairs={{0,2},{1,3},{2,4},{3,5},{4,6},{5,7},{6,8},{7,9},{8,10},{9,11},{10,... | collective-permute-start | bytes 786440 | tf_op jit(solution)/shard_map/ppermute | solution.py:35
  175.9 18.7 %collective-permute-start.11 = (bf16[64,2048]{1,0:T(8,128)(2,1)S(1)}, bf16[64,2048]{1,0:T(8,128)(2,1)S(1)}, u32[]{:S(2)}, u32[]{:S(2)}) collective-permute-start(bf16[64,2048]{1,0:T(8,128)(2,1)S(1)} %convolution_convert_fusion.2), channel_id=1, source_target_pairs={{0,14},{1,15},{2,0},{3,1},{4,2},{5,3},{6,4},{7,5},{8,6},{9,7},{10,... | collective-permute-start | bytes 786440 | tf_op jit(solution)/shard_map/ppermute | solution.py:35
  181.9 43.3 %copy-start.10 = (bf16[16,4096]{1,0:T(8,128)(2,1)S(1)}, bf16[16,4096]{1,0:T(8,128)(2,1)}, u32[]{:S(2)}) copy-start(bf16[16,4096]{1,0:T(8,128)(2,1)} %param.14) | copy-start | bytes 393220
  195.3 21.0 %collective-permute-start.13 = (bf16[16,4096]{1,0:T(8,128)(2,1)S(1)}, bf16[16,4096]{1,0:T(8,128)(2,1)S(1)}, u32[]{:S(2)}, u32[]{:S(2)}) collective-permute-start(bf16[16,4096]{1,0:T(8,128)(2,1)S(1)} %get-tuple-element.25), channel_id=1, source_target_pairs={{0,8},{1,9},{2,10},{3,11},{4,12},{5,13},{6,14},{7,15},{8,0},{9,1},... | collective-permute-start | bytes 393224 | tf_op jit(solution)/shard_map/ppermute | solution.py:35
  200.4 24.8 %collective-permute-start.15 = (bf16[16,4096]{1,0:T(8,128)(2,1)S(1)}, bf16[16,4096]{1,0:T(8,128)(2,1)S(1)}, u32[]{:S(2)}, u32[]{:S(2)}) collective-permute-start(bf16[16,4096]{1,0:T(8,128)(2,1)S(1)} %get-tuple-element.26), channel_id=1, source_target_pairs={{0,12},{1,13},{2,14},{3,15},{4,0},{5,1},{6,2},{7,3},{8,4},{9,5},{1... | collective-permute-start | bytes 393224 | tf_op jit(solution)/shard_map/ppermute | solution.py:35
  206.2 19.1 %collective-permute-start.14 = (bf16[16,4096]{1,0:T(8,128)(2,1)S(1)}, bf16[16,4096]{1,0:T(8,128)(2,1)S(1)}, u32[]{:S(2)}, u32[]{:S(2)}) collective-permute-start(bf16[16,4096]{1,0:T(8,128)(2,1)S(1)} %get-tuple-element.27), channel_id=1, source_target_pairs={{0,4},{1,5},{2,6},{3,7},{4,8},{5,9},{6,10},{7,11},{8,12},{9,13},{1... | collective-permute-start | bytes 393224 | tf_op jit(solution)/shard_map/ppermute | solution.py:35
